TPU v7x, 8 devices: a whole 2x2x1 slice. The times are simulated.
8 devices in a mesh: data: 1 (over z), graph: 8 (over y, x, core).
Axes of the slice: x: 2, y: 2, z: 1, core: 2. Of those that a mesh axis runs over, the one named last changes fastest.
Arguments:
- x_feat: bfloat16 [16384, 50], P(('data', 'graph'))
- dst_local: int32 [65536], P(('data', 'graph'))
- src_slot: int32 [65536], P(('data', 'graph'))
- edge_w: float32 [65536], P(('data', 'graph'))
- send_idx: int32 [4096], P(('data', 'graph'))
- hub_ids: int32 [64], P('data')
- w_first: bfloat16 [50, 512], replicated
- b_first: float32 [512], replicated
- w_second: bfloat16 [512, 121], replicated
- grad_out: float32 [16384, 121], P(('data', 'graph'))
Outputs:
- output 1: float32 [16384, 50], P(('data', 'graph'))
- output 2: float32 [50, 512], P('data')
- output 3: float32 [512, 121], P('data')
- output 4: float32 [512], P('data')
- output 5: float32 [121], P('data')
All inputs are finite; a program needn't handle non-finite values.
Results may differ from a plain program's by a relative error of at most 0.0015773.
Values are sent between devices in bfloat16 or wider.
A program may use at most 1 GiB of HBM per device.

v0:
```python
import jax
import jax.numpy as jnp
from jax import lax
from jax.sharding import PartitionSpec as P

CONTRACT_ROWS = (((0,), (0,)), ((), ()))
CONTRACT_COLS = (((1,), (1,)), ((), ()))


def hub_collect(dev_rows, hub_owned, hub_row):
    picked = jnp.where(hub_owned[:, None], dev_rows[hub_row], jnp.zeros((), dev_rows.dtype))
    return lax.psum(picked, "graph")


def hub_return(dev_rows, hub_sum, hub_owned, hub_row):
    return dev_rows.at[hub_row].add(jnp.where(hub_owned[:, None], hub_sum, 0.0))


def propagate(features, graph_data, groups):
    send_loc, hub_owned, hub_row, dst_loc, src_loc, w_loc = graph_data
    num_nodes = features.shape[0]
    send_rows = send_loc.shape[0] // groups
    outgoing = features[send_loc].reshape(groups, send_rows, -1)
    halo_feat = lax.all_to_all(outgoing, "graph", 0, 0).reshape(groups * send_rows, -1)
    hub_feat = hub_collect(features, hub_owned, hub_row)
    feat_table = jnp.concatenate([features, halo_feat, hub_feat], axis=0)
    weighted = feat_table[src_loc].astype(jnp.float32) * w_loc[:, None]
    dev_sums = jax.ops.segment_sum(weighted, dst_loc, num_segments=num_nodes + hub_row.shape[0])
    hub_sum = lax.psum(dev_sums[num_nodes:], "graph")
    return hub_return(dev_sums[:num_nodes], hub_sum, hub_owned, hub_row)


def propagate_adjoint(grad_y, graph_data, groups):
    send_loc, hub_owned, hub_row, dst_loc, src_loc, w_loc = graph_data
    num_nodes = grad_y.shape[0]
    halo_rows = send_loc.shape[0]
    hub_grad = hub_collect(grad_y, hub_owned, hub_row)
    extended = jnp.concatenate([grad_y, hub_grad], axis=0)
    weighted = extended[dst_loc] * w_loc[:, None]
    table_grad = jax.ops.segment_sum(weighted, src_loc, num_segments=num_nodes + halo_rows + hub_row.shape[0])
    outgoing = table_grad[num_nodes:num_nodes + halo_rows].reshape(groups, halo_rows // groups, -1)
    returned = lax.all_to_all(outgoing, "graph", 0, 0).reshape(halo_rows, -1)
    grad_z = table_grad[:num_nodes].at[send_loc].add(returned)
    hub_back = lax.psum(table_grad[num_nodes + halo_rows:], "graph")
    return hub_return(grad_z, hub_back, hub_owned, hub_row)


def solution(mesh):
    groups = mesh.shape["graph"]
    vertex_spec = P(("data", "graph"))
    vertex_rows = P(("data", "graph"), None)
    part_spec = P("data")
    part_rows = P("data", None)
    replicated = P()

    def device_step(x_loc, dst_loc, src_loc, w_loc, send_loc, hub_ids, w_first, b_first, w_second, dy_out):
        num_nodes = x_loc.shape[0]
        my_index = lax.axis_index("graph")
        hub_owned = (hub_ids // num_nodes) == my_index
        hub_row = hub_ids % num_nodes
        graph_data = (send_loc, hub_owned, hub_row, dst_loc, src_loc, w_loc)
        z_first = jnp.dot(x_loc, w_first, preferred_element_type=jnp.float32).astype(jnp.bfloat16)
        pre_act = propagate(z_first, graph_data, groups) + b_first
        hidden = jax.nn.relu(pre_act).astype(jnp.bfloat16)
        grad_z2 = propagate_adjoint(dy_out, graph_data, groups).astype(jnp.bfloat16)
        grad_w2 = lax.psum(lax.dot_general(hidden, grad_z2, CONTRACT_ROWS, preferred_element_type=jnp.float32), "graph")
        grad_h = lax.dot_general(grad_z2, w_second, CONTRACT_COLS, preferred_element_type=jnp.float32)
        grad_pre = jnp.where(pre_act > 0, grad_h, 0.0)
        grad_b1 = lax.psum(grad_pre.sum(axis=0), "graph")
        grad_z1 = propagate_adjoint(grad_pre, graph_data, groups).astype(jnp.bfloat16)
        grad_w1 = lax.psum(lax.dot_general(x_loc, grad_z1, CONTRACT_ROWS, preferred_element_type=jnp.float32), "graph")
        grad_x = lax.dot_general(grad_z1, w_first, CONTRACT_COLS, preferred_element_type=jnp.float32)
        grad_b2 = lax.psum(dy_out.sum(axis=0), "graph")
        return grad_x, grad_w1, grad_w2, grad_b1, grad_b2

    return jax.shard_map(
        device_step,
        mesh=mesh,
        in_specs=(vertex_rows, vertex_spec, vertex_spec, vertex_spec, vertex_spec, part_spec, replicated, replicated, replicated, vertex_rows),
        out_specs=(vertex_rows, part_rows, part_rows, part_spec, part_spec),
        check_vma=False,
    )
```

profile of v0, /device:TPU:0, one launch (start us, length us, event | category | flops | bytes accessed | tf_op | source)
XLA Modules:
  0.0 1030.9 jit_solution(3845854937976009451)
XLA Ops:
  7.2 0.0 copy-start
  7.2 0.0 copy-start.4
  7.2 0.7 compare_select_fusion.4
  7.9 0.7 fusion.34
  8.6 0.8 fusion.29
  9.4 0.0 copy-start.9
  9.4 1.8 gather_fusion.2
  11.2 0.1 broadcast_select_fusion.2
  11.3 25.2 %psum.72 = f32[64,121]{1,0:T(8,128)S(1)} all-reduce(f32[64,121]{1,0:T(8,128)S(1)} %broadcast_select_fusion.2), channel_id=1, replica_groups=mesh['data'=1,'graph'=8] {'graph'}, use_global_device_ids=true, to_apply=%region_4.5 | all-reduce | flops 7744 | bytes 61952 | tf_op jit(solution)/shard_map/psum | solution.py:12
  36.5 1.3 pad_maximum_fusion.2
  37.8 79.2 %scatter_custom_fusion.2 = f32[2624,121]{1,0:T(8,128)S(1)} fusion(s32[8192]{0:T(1024)} %param.12, f32[8192]{0:T(1024)} %param.13, f32[]{:T(128)} %constant.20.clone.1, f32[2112,121]{1,0:T(8,128)S(1)} %pad_maximum_fusion.2, s32[8192]{0:T(1024)S(1)} %fusion.29), kind=kCustom, calls=%fused_computation.25 | custom fusion | flops 1982464 | bytes 2358272 | tf_op jit(solution)/shard_map/scatter-add | solution.py:40
  117.0 0.8 slice.49
  117.7 0.4 copy-done.1
  118.2 2.8 all-to-all-start.1
  121.0 0.0 copy-start.7
  121.0 0.7 convolution_convert_fusion
  121.7 0.7 gather_fusion.1
  122.5 2.6 gather_fusion
  125.1 2.5 all-to-all-done.1
  127.6 2.9 all-to-all-start
  130.4 0.0 all-reduce.8.cloned.1.call-start
  130.5 0.7 broadcast_select_fusion.1
  131.2 0.0 all-reduce.8.cloned.1.call-update
  131.2 0.0 all-reduce.10.cloned.1.call-start
  131.3 25.3 %psum.73 = f32[64,121]{1,0:T(8,128)S(1)} all-reduce(f32[64,121]{1,0:T(8,128)S(1)} %slice-done), channel_id=1, replica_groups=mesh['data'=1,'graph'=8] {'graph'}, use_global_device_ids=true, to_apply=%region_7.8 | all-reduce | flops 7744 | bytes 61952 | tf_op jit(solution)/shard_map/psum | solution.py:44
  156.7 4.1 scatter_fusion
  160.8 0.0 copy-start.3
  160.8 1.7 scatter_custom_fusion.4
  162.5 15.7 %all-reduce.8.cloned.1.call-done = bf16[64,512]{1,0:T(8,128)(2,1)} async-done(((bf16[64,512]{1,0:T(8,128)(2,1)}), bf16[64,512]{1,0:T(8,128)(2,1)}) %all-reduce.8.cloned.1.call-update) | async-done | bytes 65552 | tf_op jit(solution)/shard_map/psum | solution.py:12
  178.1 0.0 all-to-all-done
  178.2 2.8 pad_maximum_fusion.1
  180.9 316.5 %scatter_custom_fusion = f32[2112,512]{1,0:T(8,128)} fusion(s32[8192]{0:T(1024)} %param.11, f32[8192]{0:T(1024)S(1)} %copy-done.3, f32[]{:T(128)} %constant.20.clone.1, bf16[2624,512]{1,0:T(8,128)(2,1)} %pad_maximum_fusion.1, s32[8192]{0:T(1024)S(1)} %fusion.28), kind=kCustom, calls=%fused_computation.17 | custom fusion | flops 12582912 | bytes 7078400 | tf_op jit(solution)/shard_map/scatter-add | solution.py:28
  497.4 1.6 slice.47
  499.0 0.0 all-reduce.10.cloned.1.call-update
  499.0 0.0 all-reduce.12.cloned.1.call-start
  499.1 4.6 slice_add_fusion
  503.7 37.0 %all-reduce.10.cloned.1.call-done = f32[64,512]{1,0:T(8,128)} async-done(((f32[64,512]{1,0:T(8,128)}), f32[64,512]{1,0:T(8,128)}) %all-reduce.10.cloned.1.call-update) | async-done | bytes 131088 | tf_op jit(solution)/shard_map/psum | solution.py:29
  540.7 5.5 scatter_custom_fusion.1
  546.2 4.9 fusion.39
  551.0 2.9 gather_fusion.3
  553.9 0.7 broadcast_select_fusion
  554.7 0.0 all-reduce.12.cloned.1.call-update
  554.7 41.7 %all-reduce.12.cloned.1.call-done = f32[64,512]{1,0:T(8,128)} async-done(((f32[64,512]{1,0:T(8,128)}), f32[64,512]{1,0:T(8,128)}) %all-reduce.12.cloned.1.call-update) | async-done | bytes 131088 | tf_op jit(solution)/shard_map/psum | solution.py:12
  596.4 4.9 pad_maximum_fusion
  601.3 315.3 %scatter_custom_fusion.5 = f32[2624,512]{1,0:T(8,128)} fusion(s32[8192]{0:T(1024)S(1)} %copy-done.7, f32[8192]{0:T(1024)S(1)} %copy-done.3, f32[]{:T(128)} %constant.20.clone.1, f32[2112,512]{1,0:T(8,128)} %pad_maximum_fusion, s32[8192]{0:T(1024)S(1)} %fusion.29), kind=kCustom, calls=%fused_computation.15 | custom fusion | flops 8388608 | bytes 9764868 | tf_op jit(solution)/shard_map/scatter-add | solution.py:40
  916.6 2.4 slice.52
  918.9 2.3 all-to-all-start.2
  921.2 0.0 all-reduce.14.cloned.1.call-start
  921.3 0.3 reduce_sum.19
  921.6 1.6 slice.53
  923.1 0.0 all-reduce.14.cloned.1.call-update
  923.2 0.0 all-reduce.16.cloned.1.call-start
  923.2 3.6 fusion.11
  926.8 26.6 %all-reduce = (f32[512]{0:T(512)}, f32[121]{0:T(128)}) all-reduce(f32[512]{0:T(512)S(1)} %get-tuple-element.9, f32[121]{0:T(128)S(1)} %reduce_sum.19), channel_id=1, replica_groups=mesh['data'=1,'graph'=8] {'graph'}, use_global_device_ids=true, to_apply=%region_17.18 | all-reduce | flops 633 | bytes 5064 | tf_op jit(solution)/shard_map/psum | solution.py:69
  953.4 4.6 slice.51
  958.0 7.7 scatter_fusion.1
  965.6 4.1 all-reduce.14.cloned.1.call-done
  969.8 5.5 scatter_custom_fusion.7
  975.2 3.3 convolution_bitcast_fusion
  978.5 0.0 all-reduce.16.cloned.1.call-update
  978.6 3.7 fusion.15
  982.3 38.9 %all-reduce.16.cloned.1.call-done = (f32[50,512]{1,0:T(8,128)}, f32[512,121]{1,0:T(8,128)}) async-done(((f32[50,512]{1,0:T(8,128)}, f32[512,121]{1,0:T(8,128)}), (f32[50,512]{1,0:T(8,128)}, f32[512,121]{1,0:T(8,128)})) %all-reduce.16.cloned.1.call-update) | async-done | bytes 350224 | tf_op jit(solution)/shard_map/psum | solution.py:71
  1021.2 1.6 copy.26
  1022.7 1.7 copy.27
  (25 shorter events, 0.1 us)
Async XLA Ops:
  7.2 113.8 %copy-start = (bf16[2048,50]{0,1:T(8,128)(2,1)S(1)}, bf16[2048,50]{0,1:T(8,128)(2,1)}, u32[]{:S(2)}) copy-start(bf16[2048,50]{0,1:T(8,128)(2,1)} %param.10) | copy-start | bytes 614404
  7.2 113.8 %copy-start.4 = (bf16[50,512]{1,0:T(8,128)(2,1)S(1)}, bf16[50,512]{1,0:T(8,128)(2,1)}, u32[]{:S(2)}) copy-start(bf16[50,512]{1,0:T(8,128)(2,1)} %param.16) | copy-start | bytes 153604
  7.9 0.7 copy-start.10
  9.4 112.4 %copy-start.9 = (s32[512]{0:T(512)S(1)}, s32[512]{0:T(512)}, u32[]{:S(2)}) copy-start(s32[512]{0:T(512)} %param.14) | copy-start | bytes 6148
  117.0 1.2 copy-start.1
  118.2 9.4 all-to-all-start.1
  121.0 10.3 copy-start.7
  122.4 8.9 slice-start
  122.5 34.2 %slice-start.1 = ((f32[2624,121]{1,0:T(8,128)}), f32[2048,121]{1,0:T(8,128)S(1)}, s32[]{:S(2)}) async-start(f32[2624,121]{1,0:T(8,128)} %copy-done.1), calls=%async_computation.9 | async-start | bytes 2097152 | tf_op jit(solution)/shard_map/slice | solution.py:43
  127.6 50.6 %all-to-all-start = ((bf16[8,64,512]{2,1,0:T(8,128)(2,1)}), bf16[8,64,512]{2,1,0:T(8,128)(2,1)}, u32[]{:S(2)}, u32[]{:S(2)}) async-start(bf16[8,64,512]{2,1,0:T(8,128)(2,1)} %bitcast.15), calls=%async_computation | async-start | bytes 1048576 | tf_op jit(solution)/shard_map/all_to_all | solution.py:24
  130.4 47.7 %all-reduce.8.cloned.1.call-start = ((), (), s32[]{:S(2)}) async-start(), calls=%async_computation.3 | async-start | bytes 131072 | tf_op jit(solution)/shard_map/psum | solution.py:12
  131.2 409.5 %all-reduce.10.cloned.1.call-start = ((), (), s32[]{:S(2)}) async-start(), calls=%async_computation.4 | async-start | bytes 262144 | tf_op jit(solution)/shard_map/psum | solution.py:29
  160.8 20.1 %copy-start.3 = (f32[8192]{0:T(1024)S(1)}, f32[8192]{0:T(1024)}, u32[]{:S(2)}) copy-start(f32[8192]{0:T(1024)} %param.13) | copy-start | bytes 98308
  180.9 318.1 %copy-start.8 = (f32[512]{0:T(512)S(1)}, f32[512]{0:T(512)}, u32[]{:S(2)}) copy-start(f32[512]{0:T(512)} %param.17) | copy-start | bytes 6148
  499.0 97.4 %all-reduce.12.cloned.1.call-start = ((), (), s32[]{:S(2)}) async-start(), calls=%async_computation.5 | async-start | bytes 262144 | tf_op jit(solution)/shard_map/psum | solution.py:12
  503.7 42.5 %copy-start.6 = (bf16[512,121]{1,0:T(8,128)(2,1)S(1)}, bf16[512,121]{1,0:T(8,128)(2,1)}, u32[]{:S(2)}) copy-start(bf16[512,121]{1,0:T(8,128)(2,1)} %param.18) | copy-start | bytes 371716
  916.6 4.7 copy-start.2
  918.9 39.1 %all-to-all-start.2 = ((f32[8,64,512]{2,1,0:T(8,128)}), f32[8,64,512]{2,1,0:T(8,128)S(1)}, u32[]{:S(2)}, u32[]{:S(2)}) async-start(f32[8,64,512]{2,1,0:T(8,128)} %bitcast.14), calls=%async_computation.2 | async-start | bytes 2097152 | tf_op jit(solution)/shard_map/all_to_all | solution.py:42
  921.2 48.5 %all-reduce.14.cloned.1.call-start = ((), (), s32[]{:S(2)}) async-start(), calls=%async_computation.6 | async-start | bytes 262144 | tf_op jit(solution)/shard_map/psum | solution.py:44
  923.2 98.0 %all-reduce.16.cloned.1.call-start = ((), (), s32[]{:S(2)}) async-start(), calls=%async_computation.7 | async-start | bytes 753664 | tf_op jit(solution)/shard_map/psum | solution.py:71
  965.6 12.9 %copy-start.5 = (bf16[50,512]{1,0:T(8,128)(2,1)S(1)}, bf16[50,512]{1,0:T(8,128)(2,1)}, u32[]{:S(2)}) copy-start(bf16[50,512]{1,0:T(8,128)(2,1)} %param.16) | copy-start | bytes 153604
Sparse Core Ops, SparseCore 0:
  134.8 43.2 all-reduce.7
  499.1 41.5 all-reduce.9
  554.8 41.5 all-reduce.11
  925.3 44.4 all-reduce.13
  978.7 42.4 all-reduce.15
where the time goes:
time: 1030 us
  other arithmetic  753 us (73%)
  waiting for transfers between devices  140 us (14%)
  blocking collectives  77.1 us (7%)
  local copies, waits for them, and re-layouts  22.6 us (2%)
  matrix products  16.2 us (2%)
  between operations  14 us (1%)
    scatter-add x2, other arithmetic, propagate_adjoint(): jax.ops.segment_sum(weighted, src_loc, num_segments=num_nodes + halo_rows...  394 us
    scatter-add x1, other arithmetic, propagate(): jax.ops.segment_sum(weighted, dst_loc, num_segments=num_nodes + hub_row.s...  317 us
    psum x2, waiting for transfers between devices, hub_collect(): return lax.psum(picked, 'graph')  57.3 us
    psum x1, waiting for transfers between devices, device_step(): lax.psum(lax.dot_general(x_loc, grad_z1, CONTRACT_ROWS, preferred_element...  38.9 us
    psum x1, waiting for transfers between devices, propagate(): hub_sum = lax.psum(dev_sums[num_nodes:], 'graph')  37 us
    psum x1, blocking collectives, device_step(): grad_b1 = lax.psum(grad_pre.sum(axis=0), 'graph')  26.6 us
    psum x1, blocking collectives, propagate_adjoint(): hub_back = lax.psum(table_grad[num_nodes + halo_rows:], 'graph')  25.3 us
    psum x1, blocking collectives, hub_collect(): return lax.psum(picked, 'graph')  25.2 us
  transfers between devices with their start and end apart: 8, of which 6 were waited for; matrix products, arithmetic and copies ran while one was open for 4% of the time, Pallas kernels for 0%

commit v1 on v0

v1 whole, which is shorter than its diff:
```python
import functools

import jax
import jax.numpy as jnp
from jax import lax
from jax.experimental import pallas as pl
from jax.experimental.pallas import tpu as pltpu
from jax.sharding import PartitionSpec as P

F32, BF16, I32 = jnp.float32, jnp.bfloat16, jnp.int32
CONTRACT_ROWS = (((0,), (0,)), ((), ()))
CONTRACT_COLS = (((1,), (1,)), ((), ()))
LANES = 128
HID = 512
TILES = HID // LANES
CHUNK = 256
VMEM_LIMIT = 63 * 2**20
VMEM = pl.BlockSpec(memory_space=pltpu.VMEM)
SMEM = pl.BlockSpec(memory_space=pltpu.SMEM)


def dot(a, b, dims=(((1,), (0,)), ((), ()))):
    return lax.dot_general(a, b, dims, preferred_element_type=F32)


def iota(shape, dim):
    return lax.broadcasted_iota(I32, shape, dim)


def split3(value):
    high = value.astype(BF16)
    rest = value - high.astype(F32)
    mid = rest.astype(BF16)
    low = (rest - mid.astype(F32)).astype(BF16)
    return high, mid, low


def select_rows(onehot, value, dims=(((1,), (0,)), ((), ()))):
    high, mid, low = split3(value)
    return dot(onehot, low, dims) + dot(onehot, mid, dims) + dot(onehot, high, dims)


def pad_lanes(value):
    rows, cols = value.shape
    if cols == LANES:
        return value
    return jnp.concatenate([value, jnp.zeros((rows, LANES - cols), value.dtype)], axis=1)


def greet(groups, me):
    barrier = pltpu.get_barrier_semaphore()
    for step in range(1, groups):
        pl.semaphore_signal(barrier, inc=1, device_id={"graph": lax.rem(me + step, groups)}, device_id_type=pl.DeviceIdType.MESH)
    return barrier


def send(src, dst, send_sem, recv_sem, peer):
    copy = pltpu.make_async_remote_copy(
        src_ref=src, dst_ref=dst, send_sem=send_sem, recv_sem=recv_sem,
        device_id={"graph": peer}, device_id_type=pl.DeviceIdType.MESH)
    copy.start()
    return copy


def gather_kernel(groups, x_ref, dh_ref, send_ref, hub_ref, hubrow_ref, dst_ref, src_ref,
                  xh_ref, hx_ref, dhh_ref, d4_ref, s4_ref, db2_ref,
                  x32, xg, hxg, dhg, xs, xr, dhr, ssem, rsem):
    me = lax.axis_index("graph")
    barrier = greet(groups, me)
    nodes, feat = x_ref.shape
    hubs = hub_ref.shape[0]
    halo = send_ref.shape[0]
    block = halo // groups
    base = me * nodes
    eye = (iota((feat, LANES), 0) == iota((feat, LANES), 1)).astype(BF16)
    tags = jnp.where(iota((hubs, LANES), 1) == feat, iota((hubs, LANES), 0) + 1, 0).astype(F32).astype(BF16)
    hubrow = hubrow_ref[...]
    for row in range(0, nodes, CHUNK):
        owned = (iota((CHUNK, hubs), 0) + (base + row) == hubrow).astype(BF16)
        x32[pl.ds(row, CHUNK), :] = dot(x_ref[pl.ds(row, CHUNK), :], eye) + dot(owned, tags)

    def pick(i, carry):
        for u in range(16):
            j = i * 16 + u
            xg[pl.ds(j, 1), :] = x32[pl.ds(send_ref[j], 1), :]
        return carry

    lax.fori_loop(0, halo // 16, pick, 0)
    dhg[...] = jnp.zeros_like(dhg)

    def pick_hub(i, carry):
        for u in range(8):
            k = i * 8 + u
            row = hub_ref[k] - base
            own = jnp.logical_and(row >= 0, row < nodes)
            row = jnp.clip(row, 0, nodes - 1)
            hxg[pl.ds(k, 1), :] = jnp.where(own, x32[pl.ds(row, 1), :], 0.0)
            value = dh_ref[pl.ds(row, 1), :]
            dhg[pl.ds(k, 1), pl.ds(0, value.shape[1])] = jnp.where(own, value, 0.0)
        return carry

    lax.fori_loop(0, hubs // 8, pick_hub, 0)
    for q in range(groups):
        xs[q, pl.ds(0, block), :] = xg[pl.ds(q * block, block), :].astype(BF16)
        xs[q, pl.ds(block, hubs), :] = hxg[...].astype(BF16)
    pl.semaphore_wait(barrier, groups - 1)
    copies = []
    for step in range(1, groups):
        peer = lax.rem(me + step, groups)
        copies.append(send(xs.at[peer], xr.at[me], ssem.at[0, step], rsem.at[0, step], peer))
        copies.append(send(dhg, dhr.at[me], ssem.at[1, step], rsem.at[1, step], peer))
    d4_ref[...] = dst_ref[...] * TILES
    s4_ref[...] = src_ref[...] * TILES
    total = jnp.zeros((8, dh_ref.shape[1]), F32)
    for row in range(0, nodes, CHUNK):
        total = total + dh_ref[pl.ds(row, CHUNK), :].reshape(CHUNK // 8, 8, dh_ref.shape[1]).sum(axis=0)
    db2_ref[...] = jnp.broadcast_to(pad_lanes(total.sum(axis=0, keepdims=True)), db2_ref.shape)
    xr[me] = xs[me]
    dhr[me] = dhg[...]
    for copy in copies:
        copy.wait()
    hx = jnp.zeros((hubs, LANES), F32)
    dhh = jnp.zeros((hubs, LANES), F32)
    for q in range(groups):
        xh_ref[pl.ds(q * block, block), :] = xr[q, pl.ds(0, block), :]
        hx = hx + xr[q, pl.ds(block, hubs), :].astype(F32)
        dhh = dhh + dhr[q]
    hx_ref[...] = hx
    dhh_ref[...] = dhh


def hub_position(hub_ref, k, base, nodes):
    row = hub_ref[k] - base
    own = jnp.logical_and(row >= 0, row < nodes)
    return own, pl.multiple_of(jnp.clip(row, 0, nodes - 1) * TILES, TILES)


def strided(first, rows):
    return pl.ds(first, rows, stride=TILES)


def total_of(refs, where):
    value = refs[0][where, :]
    for ref in refs[1:]:
        value = value + ref[where, :]
    return value


def edges_forward_kernel(copies, unroll, d4_ref, s4_ref, w_ref, hub_ref, x_ref, xh_ref, hx_ref, dh_ref, dhh_ref, w1_ref, b1_ref,
                         h1_ref, dz_ref, hz_ref, hub_out, zt, dt, *accs):
    ya, da = accs[:copies], accs[copies:]
    me = lax.axis_index("graph")
    nodes, feat = x_ref.shape
    halo, hubs = xh_ref.shape[0], hx_ref.shape[0]
    edges = w_ref.shape[0]
    base = me * nodes
    for acc in ya:
        acc[...] = jnp.zeros_like(acc)
    for acc in da:
        acc[strided(0, nodes + halo + hubs), :] = jnp.zeros((nodes + halo + hubs, LANES), F32)
    w1 = w1_ref[...]

    def put_rows(first, x_rows):
        z = dot(x_rows, w1).astype(BF16).astype(F32)
        for c in range(TILES):
            zt[strided(first * TILES + c, x_rows.shape[0]), :] = z[:, c * LANES:(c + 1) * LANES]

    for row in range(0, nodes, CHUNK):
        put_rows(row, x_ref[pl.ds(row, CHUNK), :])
        dt[strided(row * TILES, CHUNK), :] = pad_lanes(dh_ref[pl.ds(row, CHUNK), :])
    for row in range(0, halo, CHUNK):
        put_rows(nodes + row, xh_ref[pl.ds(row, CHUNK), pl.ds(0, feat)])
    put_rows(nodes + halo, hx_ref[:, pl.ds(0, feat)].astype(BF16))
    dt[strided(nodes * TILES, hubs), :] = dhh_ref[...]

    def step(i, carry):
        for u0 in range(0, unroll, copies):
            new = []
            for u in range(copies):
                j = i * unroll + u0 + u
                s4 = pl.multiple_of(s4_ref[j], TILES)
                d4 = pl.multiple_of(d4_ref[j], TILES)
                w = w_ref[j]
                new.append((s4, d4, ya[u][pl.ds(d4, TILES), :] + w * zt[pl.ds(s4, TILES), :],
                            da[u][pl.ds(s4, 1), :] + w * dt[pl.ds(d4, 1), :]))
            for u, (s4, d4, y_new, z_new) in enumerate(new):
                ya[u][pl.ds(d4, TILES), :] = y_new
                da[u][pl.ds(s4, 1), :] = z_new
        return carry

    lax.fori_loop(0, edges // unroll, step, 0)

    def fold(k, carry):
        own, row = hub_position(hub_ref, k, base, nodes)
        here = pl.multiple_of((nodes + k) * TILES, TILES)
        ya[0][pl.ds(here, TILES), :] += jnp.where(own, total_of(ya, pl.ds(row, TILES)), 0.0)
        here = (nodes + halo + k) * TILES
        value = total_of(da, pl.ds(row, 1))
        da[0][pl.ds(here, 1), :] += jnp.where(own, value, 0.0)
        da[0][pl.ds(row, 1), :] = jnp.where(own, 0.0, value)
        for acc in da[1:]:
            acc[pl.ds(row, 1), :] = jnp.zeros((1, LANES), F32)
        return carry

    lax.fori_loop(0, hubs, fold, 0)
    for row in range(0, nodes, CHUNK):
        for c in range(TILES):
            cols = pl.ds(c * LANES, LANES)
            y = total_of(ya, strided(row * TILES + c, CHUNK)) + b1_ref[:, cols]
            h1_ref[pl.ds(row, CHUNK), cols] = jnp.maximum(y, 0.0).astype(BF16)
        dz_ref[pl.ds(row, CHUNK), :] = total_of(da, strided(row * TILES, CHUNK))
    hz = total_of(da, strided(nodes * TILES, halo))
    tag = xh_ref[...].astype(F32)[:, feat:feat + 1]
    onehot = (tag == (iota((halo, hubs), 1) + 1).astype(F32)).astype(BF16)
    hub_z = total_of(da, strided((nodes + halo) * TILES, hubs)) + select_rows(onehot, hz, CONTRACT_ROWS)
    hz_ref[...] = jnp.where(tag > 0.0, 0.0, hz)
    for c in range(TILES):
        hub_out[:, pl.ds(c * LANES, LANES)] = total_of(ya, strided(nodes * TILES + c, hubs))
    hub_out[:, pl.ds(HID, LANES)] = hub_z


def middle_kernel(groups, hz_ref, hub_ref, dz_ref, sendrow_ref, w2_ref, b1_ref,
                  dz2_ref, dyh_ref, h1h_ref, dz2h_ref,
                  hzr, hubr, dyr, dys, ssem, rsem):
    me = lax.axis_index("graph")
    barrier = greet(groups, me)
    nodes = dz_ref.shape[0]
    out = w2_ref.shape[1]
    home = hub_ref.shape[1]
    block = hz_ref.shape[1]
    halo = groups * block
    hubr[me] = hub_ref[me]
    hzr[me] = jnp.zeros(hzr.shape[1:], F32)
    pl.semaphore_wait(barrier, groups - 1)
    hub_copies, halo_copies, back = [], [], []
    for step in range(1, groups):
        peer = lax.rem(me + step, groups)
        hub_copies.append(send(hub_ref.at[peer], hubr.at[me], ssem.at[0, step], rsem.at[0, step], peer))
    for step in range(1, groups):
        peer = lax.rem(me + step, groups)
        halo_copies.append(send(hz_ref.at[peer], hzr.at[me], ssem.at[1, step], rsem.at[1, step], peer))
    for copy in hub_copies:
        copy.wait()
    total = hubr[0]
    for q in range(1, groups):
        total = total + hubr[q]
    pre = total[:, :HID] + b1_ref[...]
    dz2h = total[:, HID:].astype(BF16)
    h1h_ref[...] = jnp.maximum(pre, 0.0).astype(BF16)
    dz2h_ref[...] = dz2h
    dys[...] = jnp.where(pre > 0, dot(dz2h[:, :out], w2_ref[...], CONTRACT_COLS), 0.0)
    for step in range(1, groups):
        peer = lax.rem(me + step, groups)
        back.append(send(dys, dyr.at[me], ssem.at[2, step], rsem.at[2, step], peer))
    dyr[me] = dys[...]
    for copy in halo_copies:
        copy.wait()
    pieces = split3(hzr[...].reshape(halo, LANES))
    sendrow = sendrow_ref[...]
    for row in range(0, nodes, CHUNK):
        onehot = (iota((CHUNK, halo), 0) + row == sendrow).astype(BF16)
        value = dz_ref[pl.ds(row, CHUNK), :]
        for piece in reversed(pieces):
            value = value + dot(onehot, piece)
        dz2_ref[pl.ds(row, CHUNK), :] = value.astype(BF16)
    for copy in back:
        copy.wait()
    for q in range(groups):
        dyh_ref[pl.ds(q * home, home), :] = dyr[q]


def edges_backward_kernel(copies, unroll, d4_ref, s4_ref, w_ref, hub_ref, h1_ref, dz2_ref, dyh_ref, w2_ref, h1h_ref, dz2h_ref, xh_ref, db2_ref,
                          dz1_ref, hz_ref, hub_out, dw2_ref, bias_ref, yt, *za):
    me = lax.axis_index("graph")
    nodes = h1_ref.shape[0]
    out = w2_ref.shape[1]
    halo, hubs = xh_ref.shape[0], dyh_ref.shape[0]
    home = h1h_ref.shape[0]
    feat = 50
    edges = w_ref.shape[0]
    base = me * nodes
    for acc in za:
        acc[...] = jnp.zeros_like(acc)
    w2 = w2_ref[...]
    mine = dyh_ref[pl.ds(pl.multiple_of(me * home, 8), home), :]
    db1 = mine
    for row in range(0, nodes, CHUNK):
        rows = pl.ds(row, CHUNK)
        grad = dot(dz2_ref[rows, pl.ds(0, out)], w2, CONTRACT_COLS)
        grad = jnp.where(h1_ref[rows, :] > 0, grad, 0.0)
        db1 = db1 + grad.reshape(CHUNK // 8, 8, HID).sum(axis=0)
        for c in range(TILES):
            yt[strided(row * TILES + c, CHUNK), :] = grad[:, c * LANES:(c + 1) * LANES]
    db1 = db1.sum(axis=0, keepdims=True)
    bias_ref[...] = db2_ref[...]
    for c in range(TILES):
        bias_ref[pl.ds(c, 1), :] = db1[:, c * LANES:(c + 1) * LANES]
        yt[strided(nodes * TILES + c, hubs), :] = dyh_ref[:, pl.ds(c * LANES, LANES)]
    dw2_ref[...] = dot(h1_ref[...], dz2_ref[...], CONTRACT_ROWS) + dot(h1h_ref[...], dz2h_ref[...], CONTRACT_ROWS)

    def place(k, carry):
        own, row = hub_position(hub_ref, k, base, nodes)
        here = pl.multiple_of((nodes + k) * TILES, TILES)
        yt[pl.ds(row, TILES), :] = jnp.where(own, yt[pl.ds(here, TILES), :], yt[pl.ds(row, TILES), :])
        return carry

    lax.fori_loop(0, hubs, place, 0)

    def step(i, carry):
        for u0 in range(0, unroll, copies):
            new = []
            for u in range(copies):
                j = i * unroll + u0 + u
                s4 = pl.multiple_of(s4_ref[j], TILES)
                d4 = pl.multiple_of(d4_ref[j], TILES)
                w = w_ref[j]
                new.append((s4, za[u][pl.ds(s4, TILES), :] + w * yt[pl.ds(d4, TILES), :]))
            for u, (s4, z_new) in enumerate(new):
                za[u][pl.ds(s4, TILES), :] = z_new
        return carry

    lax.fori_loop(0, edges // unroll, step, 0)

    def fold(k, carry):
        own, row = hub_position(hub_ref, k, base, nodes)
        here = pl.multiple_of((nodes + halo + k) * TILES, TILES)
        value = total_of(za, pl.ds(row, TILES))
        za[0][pl.ds(here, TILES), :] += jnp.where(own, value, 0.0)
        za[0][pl.ds(row, TILES), :] = jnp.where(own, 0.0, value)
        for acc in za[1:]:
            acc[pl.ds(row, TILES), :] = jnp.zeros((TILES, LANES), F32)
        return carry

    lax.fori_loop(0, hubs, fold, 0)
    for row in range(0, nodes, CHUNK):
        for c in range(TILES):
            dz1_ref[pl.ds(row, CHUNK), pl.ds(c * LANES, LANES)] = total_of(za, strided(row * TILES + c, CHUNK))
    tag = xh_ref[...].astype(F32)[:, feat:feat + 1]
    onehot = (tag == (iota((halo, hubs), 1) + 1).astype(F32)).astype(BF16)
    for c in range(TILES):
        cols = pl.ds(c * LANES, LANES)
        hz = total_of(za, strided(nodes * TILES + c, halo))
        hub_out[:, cols] = total_of(za, strided((nodes + halo) * TILES + c, hubs)) + select_rows(onehot, hz, CONTRACT_ROWS)
        hz_ref[:, cols] = jnp.where(tag > 0.0, 0.0, hz)


def final_kernel(groups, hz_ref, hub_ref, dw2_ref, bias_ref, dz1_ref, x_ref, hx_ref, w1_ref, sendrow_ref, hubrow_ref,
                 gx_ref, gw1_ref, gw2_ref, gb1_ref, gb2_ref,
                 hzr, hubr, dw2r, biasr, pieces, dw2s, dw2a, dxs, dxa, dw1s, dw1r, dw1t, dw1a, ssem, rsem):
    me = lax.axis_index("graph")
    barrier = greet(groups, me)
    nodes, feat = x_ref.shape
    home = hub_ref.shape[1]
    hubs = groups * home
    block = hz_ref.shape[1]
    halo = groups * block
    out = gw2_ref.shape[1]
    part = dw2_ref.shape[1]
    base = me * nodes
    hubr[me] = hub_ref[me]
    dw2r[me] = dw2_ref[me]
    biasr[me] = bias_ref[...]
    hzr[me] = jnp.zeros(hzr.shape[1:], F32)
    pl.semaphore_wait(barrier, groups - 1)
    peers = [lax.rem(me + step, groups) for step in range(1, groups)]

    def to_all(slot, src, dst):
        return [send(src(peer), dst.at[me], ssem.at[slot, i], rsem.at[slot, i], peer) for i, peer in enumerate(peers)]

    hub_copies = to_all(0, lambda p: hub_ref.at[p], hubr)
    dw2_copies = to_all(1, lambda p: dw2_ref.at[p], dw2r)
    bias_copies = to_all(2, lambda p: bias_ref, biasr)
    halo_copies = to_all(3, lambda p: hz_ref.at[p], hzr)
    w1 = w1_ref[...]
    for copy in hub_copies:
        copy.wait()
    total = hubr[0]
    for q in range(1, groups):
        total = total + hubr[q]
    dz1h = total.astype(BF16)
    dxs[...] = pad_lanes(dot(dz1h, w1, CONTRACT_COLS))
    dx_copies = to_all(4, lambda p: dxs, dxa)
    dxa[me] = dxs[...]
    hx_mine = hx_ref[pl.ds(pl.multiple_of(me * home, 8), home), :].astype(BF16)
    dw1h = dot(hx_mine[:, :feat], dz1h, CONTRACT_ROWS)
    for copy in dw2_copies:
        copy.wait()
    total = dw2r[0]
    for q in range(1, groups):
        total = total + dw2r[q]
    dw2s[...] = total
    dw2_back = to_all(5, lambda p: dw2s, dw2a)
    dw2a[me] = dw2s[...]
    for copy in bias_copies:
        copy.wait()
    total = biasr[0]
    for q in range(1, groups):
        total = total + biasr[q]
    for c in range(TILES):
        gb1_ref[:, pl.ds(c * LANES, LANES)] = total[c:c + 1, :]
    gb2_ref[...] = total[TILES:TILES + 1, :out]
    for copy in halo_copies:
        copy.wait()
    for q in range(groups):
        high, mid, low = split3(hzr[q])
        pieces[0, pl.ds(q * block, block), :] = low
        pieces[1, pl.ds(q * block, block), :] = mid
        pieces[2, pl.ds(q * block, block), :] = high
    for copy in dx_copies:
        copy.wait()
    dx_pieces = split3(dxa[...].reshape(hubs, LANES))
    sendrow = sendrow_ref[...]
    hubrow = hubrow_ref[...]
    dw1s[...] = jnp.zeros_like(dw1s)
    dw1s[pl.ds(0, feat), :] = dw1h

    def rows_step(i, carry):
        row = pl.multiple_of(i * CHUNK, CHUNK)
        rows = pl.ds(row, CHUNK)
        onehot = (iota((CHUNK, halo), 0) + row == sendrow).astype(BF16)
        value = dz1_ref[rows, :]
        for k in range(3):
            value = value + dot(onehot, pieces[k])
        dz1 = value.astype(BF16)
        owned = (iota((CHUNK, hubs), 0) + (base + row) == hubrow).astype(BF16)
        dx = jnp.zeros((CHUNK, LANES), F32)
        for piece in reversed(dx_pieces):
            dx = dx + dot(owned, piece)
        gx_ref[rows, :] = dot(dz1, w1, CONTRACT_COLS) + dx[:, :feat]
        dw1s[pl.ds(0, feat), :] += dot(x_ref[rows, :], dz1, CONTRACT_ROWS)
        return carry

    lax.fori_loop(0, nodes // CHUNK, rows_step, 0)
    dw1_copies = to_all(6, lambda p: dw1s.at[pl.ds(pl.multiple_of(p * 8, 8), 8)], dw1r)
    dw1r[me] = dw1s[pl.ds(pl.multiple_of(me * 8, 8), 8), :]
    for copy in dw2_back:
        copy.wait()
    for q in range(groups):
        gw2_ref[pl.ds(q * part, part), :] = dw2a[q][:, :out]
    for copy in dw1_copies:
        copy.wait()
    total = dw1r[0]
    for q in range(1, groups):
        total = total + dw1r[q]
    dw1t[...] = total
    dw1_back = to_all(7, lambda p: dw1t, dw1a)
    dw1a[me] = dw1t[...]
    for copy in dw1_back:
        copy.wait()
    for q in range(groups):
        rows = min(8, feat - q * 8)
        if rows > 0:
            gw1_ref[pl.ds(q * 8, rows), :] = dw1a[q][:rows, :]


def shape(dims, dtype):
    return jax.ShapeDtypeStruct(dims, dtype)


def solution(mesh):
    groups = mesh.shape["graph"]
    vertex_spec = P(("data", "graph"))
    vertex_rows = P(("data", "graph"), None)
    part_spec = P("data")
    part_rows = P("data", None)
    replicated = P()
    copies1, unroll1 = 3, 48
    copies2, unroll2 = 4, 64

    def params(collective_id=None):
        if collective_id is None:
            return pltpu.CompilerParams(vmem_limit_bytes=VMEM_LIMIT)
        return pltpu.CompilerParams(vmem_limit_bytes=VMEM_LIMIT, collective_id=collective_id, has_side_effects=True)

    def device_step(x_loc, dst_loc, src_loc, w_loc, send_loc, hub_ids, w_first, b_first, w_second, dy_out):
        nodes, feat = x_loc.shape
        edges = dst_loc.shape[0]
        halo = send_loc.shape[0]
        hubs = hub_ids.shape[0]
        out = dy_out.shape[1]
        block, home = halo // groups, hubs // groups
        src_rows, dst_rows = nodes + halo + hubs, nodes + hubs
        hub_lanes = hub_ids.reshape(1, hubs)
        send_lanes = send_loc.reshape(1, halo)
        bias = b_first.reshape(1, HID)
        sems = lambda n: [pltpu.SemaphoreType.DMA((n, groups)), pltpu.SemaphoreType.DMA((n, groups))]

        xh, hx, dhh, d4, s4, db2 = pl.pallas_call(
            functools.partial(gather_kernel, groups),
            name="gather_rows",
            out_shape=(shape((halo, LANES), BF16), shape((hubs, LANES), F32), shape((hubs, LANES), F32),
                       shape((edges // LANES, LANES), I32), shape((edges // LANES, LANES), I32), shape((8, LANES), F32)),
            in_specs=[VMEM, VMEM, SMEM, SMEM, VMEM, VMEM, VMEM],
            out_specs=(VMEM,) * 6,
            scratch_shapes=[pltpu.VMEM((nodes, LANES), F32), pltpu.VMEM((halo, LANES), F32), pltpu.VMEM((hubs, LANES), F32),
                            pltpu.VMEM((hubs, LANES), F32), pltpu.VMEM((groups, block + hubs, LANES), BF16),
                            pltpu.VMEM((groups, block + hubs, LANES), BF16), pltpu.VMEM((groups, hubs, LANES), F32)] + sems(2),
            compiler_params=params(0),
        )(x_loc, dy_out, send_loc, hub_ids, hub_lanes, dst_loc.reshape(edges // LANES, LANES), src_loc.reshape(edges // LANES, LANES))
        d4, s4 = d4.reshape(edges), s4.reshape(edges)
        pad1, pad2 = -edges % unroll1, -edges % unroll2
        grow = lambda a, n: jnp.pad(a, (0, n)) if n else a

        h1, dz, hz, hub = pl.pallas_call(
            functools.partial(edges_forward_kernel, copies1, unroll1),
            name="edges_forward",
            out_shape=(shape((nodes, HID), BF16), shape((nodes, LANES), F32), shape((halo, LANES), F32), shape((hubs, HID + LANES), F32)),
            in_specs=[SMEM] * 4 + [VMEM] * 7,
            out_specs=(VMEM,) * 4,
            scratch_shapes=[pltpu.VMEM((src_rows * TILES, LANES), F32), pltpu.VMEM((dst_rows * TILES, LANES), F32)]
            + [pltpu.VMEM((dst_rows * TILES, LANES), F32)] * copies1 + [pltpu.VMEM((src_rows * TILES, LANES), F32)] * copies1,
            compiler_params=params(),
        )(grow(d4, pad1), grow(s4, pad1), grow(w_loc, pad1), hub_ids, x_loc, xh, hx, dy_out, dhh, w_first, bias)

        dz2, dyh, h1h, dz2h = pl.pallas_call(
            functools.partial(middle_kernel, groups),
            name="middle",
            out_shape=(shape((nodes, LANES), BF16), shape((hubs, HID), F32), shape((home, HID), BF16), shape((home, LANES), BF16)),
            in_specs=[VMEM] * 6,
            out_specs=(VMEM,) * 4,
            scratch_shapes=[pltpu.VMEM((groups, block, LANES), F32), pltpu.VMEM((groups, home, HID + LANES), F32),
                            pltpu.VMEM((groups, home, HID), F32), pltpu.VMEM((home, HID), F32)] + sems(3),
            compiler_params=params(1),
        )(hz.reshape(groups, block, LANES), hub.reshape(groups, home, HID + LANES), dz, send_lanes, w_second, bias)

        dz1, hz1, hub1, dw2, biases = pl.pallas_call(
            functools.partial(edges_backward_kernel, copies2, unroll2),
            name="edges_backward",
            out_shape=(shape((nodes, HID), F32), shape((halo, HID), F32), shape((hubs, HID), F32), shape((HID, LANES), F32), shape((8, LANES), F32)),
            in_specs=[SMEM] * 4 + [VMEM] * 8,
            out_specs=(VMEM,) * 5,
            scratch_shapes=[pltpu.VMEM((dst_rows * TILES, LANES), F32)] + [pltpu.VMEM((src_rows * TILES, LANES), F32)] * copies2,
            compiler_params=params(),
        )(grow(d4, pad2), grow(s4, pad2), grow(w_loc, pad2), hub_ids, h1, dz2, dyh, w_second, h1h, dz2h, xh, db2)

        grad_x, grad_w1, grad_w2, grad_b1, grad_b2 = pl.pallas_call(
            functools.partial(final_kernel, groups),
            name="final",
            out_shape=(shape((nodes, feat), F32), shape((feat, HID), F32), shape((HID, out), F32), shape((1, HID), F32), shape((1, out), F32)),
            in_specs=[VMEM] * 10,
            out_specs=(VMEM,) * 5,
            scratch_shapes=[pltpu.VMEM((groups, block, HID), F32), pltpu.VMEM((groups, home, HID), F32),
                            pltpu.VMEM((groups, HID // groups, LANES), F32), pltpu.VMEM((groups, 8, LANES), F32),
                            pltpu.VMEM((3, halo, HID), BF16), pltpu.VMEM((HID // groups, LANES), F32),
                            pltpu.VMEM((groups, HID // groups, LANES), F32), pltpu.VMEM((home, LANES), F32),
                            pltpu.VMEM((groups, home, LANES), F32), pltpu.VMEM((groups * 8, HID), F32),
                            pltpu.VMEM((groups, 8, HID), F32), pltpu.VMEM((8, HID), F32), pltpu.VMEM((groups, 8, HID), F32)] + sems(8),
            compiler_params=params(2),
        )(hz1.reshape(groups, block, HID), hub1.reshape(groups, home, HID), dw2.reshape(groups, HID // groups, LANES), biases, dz1,
          x_loc, hx, w_first, send_lanes, hub_lanes)
        return grad_x, grad_w1, grad_w2, grad_b1.reshape(HID), grad_b2.reshape(out)

    return jax.shard_map(
        device_step,
        mesh=mesh,
        in_specs=(vertex_rows, vertex_spec, vertex_spec, vertex_spec, vertex_spec, part_spec, replicated, replicated, replicated, vertex_rows),
        out_specs=(vertex_rows, part_rows, part_rows, part_spec, part_spec),
        check_vma=False,
    )
```

time: 1030 us -> 147 us (0.14)
  other arithmetic: 753 us -> 0 us
  waiting for transfers between devices: 140 us -> 0 us
  Pallas kernels: 0 us -> 131 us
  blocking collectives: 77.1 us -> 0 us
  matrix products: 16.2 us -> 0 us
  between operations: 14 us -> 0.66 us
    scatter-add x8 -> x0, other arithmetic: 735 us -> none  [the longest x2 394 us: propagate_adjoint(): jax.ops.segment_sum(weighted, src_loc, num_segments=num_nodes + halo_rows...]
    psum x5 -> x0, waiting for transfers between devices: 137 us -> none  [the longest x2 57.3 us: hub_collect(): return lax.psum(picked, 'graph')]
    pallas_call x0 -> x5, Pallas kernels: none -> 131 us  [the longest x1 42.9 us: device_step(): pl.pallas_call(functools.partial(final_kernel, groups), name='final', out...]
    psum x3 -> x0, blocking collectives: 77.1 us -> none  [the longest x1 26.6 us: device_step(): grad_b1 = lax.psum(grad_pre.sum(axis=0), 'graph')]
    dot_general x5 -> x0, matrix products: 16.2 us -> none  [the longest x1 4.86 us: device_step(): lax.dot_general(grad_z2, w_second, CONTRACT_COLS, preferred_element_type=...]
    slice x9 -> x0, local copies, waits for them, and re-layouts: 10.8 us -> none  [the longest x3 4.57 us: propagate_adjoint(): grad_z = table_grad[:num_nodes].at[send_loc].add(returned)]
  transfers between devices with their start and end apart: 8 -> 0, of which waited for: 6 -> 0; matrix products, arithmetic and copies ran while one was open for 4% -> 0% of each run, Pallas kernels for 0% -> 0%
where the time goes in v1:
time: 147 us; the launch traced here: 146 us
  Pallas kernels  131 us (89%)
  local copies, waits for them, and re-layouts  14.1 us (10%)
    pallas_call x1, Pallas kernels, device_step(): pl.pallas_call(functools.partial(final_kernel, groups), name='final', out...  42.9 us
    pallas_call x1, Pallas kernels, device_step(): pl.pallas_call(functools.partial(edges_forward_kernel, copies1, unroll1),...  28.2 us
    pallas_call x1, Pallas kernels, device_step(): pl.pallas_call(functools.partial(edges_backward_kernel, copies2, unroll2)...  25.6 us
    pallas_call x1, Pallas kernels, device_step(): pl.pallas_call(functools.partial(middle_kernel, groups), name='middle', o...  21.7 us
    pallas_call x1, Pallas kernels, device_step(): pl.pallas_call(functools.partial(gather_kernel, groups), name='gather_row...  13.1 us
    unnamed x6, local copies, waits for them, and re-layouts  9.95 us
    pad x3, local copies, waits for them, and re-layouts, device_step(): grow = lambda a, n: jnp.pad(a, (0, n)) if n else a  4.12 us

profile of v1, /device:TPU:0, one launch (start us, length us, event | category | flops | bytes accessed | tf_op | source)
XLA Modules:
  0.0 146.2 jit_solution(9346715519419613761)
XLA Ops:
  0.6 1.4 pad.13.w_ref
  2.0 2.0 %copy.15.x_ref = bf16[2048,50]{1,0:T(8,128)(2,1)} copy(bf16[2048,50]{0,1:T(8,128)(2,1)} %param.10) | data formatting | bytes 409600 | tf_op args[0]
  4.0 13.1 %gather_rows.1 = (bf16[512,128]{1,0:T(8,128)(2,1)}, f32[64,128]{1,0:T(8,128)}, f32[64,128]{1,0:T(8,128)}, s32[64,128]{1,0:T(8,128)}, s32[64,128]{1,0:T(8,128)}, /*index=5*/f32[8,128]{1,0:T(8,128)}) custom-call(bf16[2048,50]{1,0:T(8,128)(2,1)} %copy.15.x_ref, f32[2048,121]{1,0:T(8,128)} %dh_ref.3, s32[512]{0:T(512)} %send_ref.1, s32[64]{0:T(128)} %hub_ref.5, ...), custom_call_target="tpu_custom_call" | custom-call | tf_op jit(solution)/shard_map/gather_rows/pallas_call | solution.py:488
  17.0 1.4 pad.12.s4_ref
  18.4 1.4 pad.11.d4_ref
  19.8 28.2 %edges_forward.1 = (bf16[2048,512]{1,0:T(8,128)(2,1)}, f32[2048,128]{1,0:T(8,128)}, f32[512,128]{1,0:T(8,128)}, f32[64,640]{1,0:T(8,128)}) custom-call(s32[8208]{0:T(1024)} %pad.11.d4_ref, s32[8208]{0:T(1024)} %pad.12.s4_ref, f32[8208]{0:T(1024)} %pad.13.w_ref, s32[64]{0:T(128)} %hub_ref.5, bf16[2048,50]{1,0:T(8,128)(2,1)} %copy.15.x_ref, ...), custom_call_target="tpu_custom_call" | custom-call | tf_op jit(solution)/shard_map/edges_forward/pallas_call | solution.py:504
  48.0 21.7 %middle.1 = (bf16[2048,128]{1,0:T(8,128)(2,1)}, f32[64,512]{1,0:T(8,128)}, bf16[8,512]{1,0:T(8,128)(2,1)}, bf16[8,128]{1,0:T(8,128)(2,1)}) custom-call(f32[8,64,128]{2,1,0:T(8,128)} %bitcast.15, f32[8,8,640]{2,1,0:T(8,128)} %bitcast.17, f32[2048,128]{1,0:T(8,128)} %get-tuple-element.37.dz_ref, s32[1,512]{1,0:T(1,128)} %bitcast.25, bf16[512,121]{1,0:T(8,128)(2,1)} %w2_ref.3, ...), custom_call_target="tpu_custom_call" | custom-call | tf_op jit(solution)/shard_map/middle/pallas_call | solution.py:515
  69.8 25.6 %edges_backward.1 = (f32[2048,512]{1,0:T(8,128)}, f32[512,512]{1,0:T(8,128)}, f32[64,512]{1,0:T(8,128)}, f32[512,128]{1,0:T(8,128)}, f32[8,128]{1,0:T(8,128)}) custom-call(s32[8192]{0:T(1024)} %bitcast.19, s32[8192]{0:T(1024)} %bitcast.21, f32[8192]{0:T(1024)} %w_ref.1, s32[64]{0:T(128)} %hub_ref.5, bf16[2048,512]{1,0:T(8,128)(2,1)} %get-tuple-element.34.h1_ref, ...), custom_call_target="tpu_custom_call" | custom-call | tf_op jit(solution)/shard_map/edges_backward/pallas_call | solution.py:526
  95.3 42.9 %final.1 = (f32[2048,50]{1,0:T(8,128)}, f32[50,512]{1,0:T(8,128)}, f32[512,121]{1,0:T(8,128)}, f32[1,512]{1,0:T(1,128)}, f32[1,121]{1,0:T(1,128)}) custom-call(f32[8,64,512]{2,1,0:T(8,128)} %bitcast.14, f32[8,8,512]{2,1,0:T(8,128)} %bitcast.22, f32[8,64,128]{2,1,0:T(8,128)} %bitcast.16, f32[8,128]{1,0:T(8,128)} %get-tuple-element.46.bias_ref, ...), custom_call_target="tpu_custom_call" | custom-call | tf_op jit(solution)/shard_map/final/pallas_call | solution.py:536
  138.2 2.3 %copy.18 = f32[2048,50]{0,1:T(8,128)} copy(f32[2048,50]{1,0:T(8,128)} %get-tuple-element.53) | data formatting | bytes 819200
  140.6 1.6 %copy.23 = f32[50,512]{1,0:T(8,128)} copy(f32[50,512]{1,0:T(8,128)} %get-tuple-element.64) | data formatting | bytes 204800
  142.1 1.7 %copy.24 = f32[512,121]{1,0:T(8,128)} copy(f32[512,121]{1,0:T(8,128)} %get-tuple-element.65) | data formatting | bytes 495616
  143.8 1.3 copy.25
  145.0 1.2 copy.26

commit v2 on v1

--- a/solution.py
+++ b/solution.py
@@ -14,7 +14,6 @@
 HID = 512
 TILES = HID // LANES
 CHUNK = 256
-VMEM_LIMIT = 63 * 2**20
 VMEM = pl.BlockSpec(memory_space=pltpu.VMEM)
 SMEM = pl.BlockSpec(memory_space=pltpu.SMEM)
 
@@ -62,12 +61,22 @@
     return copy
 
 
-def gather_kernel(groups, x_ref, dh_ref, send_ref, hub_ref, hubrow_ref, dst_ref, src_ref,
-                  xh_ref, hx_ref, dhh_ref, d4_ref, s4_ref, db2_ref,
+def pack_rows(value):
+    half = value.shape[0] // 2
+    low = iota((half, LANES), 1) < LANES // 2
+    return jnp.where(low, value[:half], pltpu.roll(value[half:], LANES // 2, 1)).astype(BF16)
+
+
+def unpack_rows(value):
+    return jnp.concatenate([value, pltpu.roll(value, LANES // 2, 1)], axis=0)
+
+
+def gather_kernel(groups, xt_ref, dh_ref, send_ref, hub_ref, hubrow_ref, dst_ref, src_ref, w_ref,
+                  xh_ref, hx_ref, dhh_ref, d4_ref, s4_ref, used_ref, db2_ref,
                   x32, xg, hxg, dhg, xs, xr, dhr, ssem, rsem):
     me = lax.axis_index("graph")
     barrier = greet(groups, me)
-    nodes, feat = x_ref.shape
+    feat, nodes = xt_ref.shape
     hubs = hub_ref.shape[0]
     halo = send_ref.shape[0]
     block = halo // groups
@@ -77,7 +86,7 @@
     hubrow = hubrow_ref[...]
     for row in range(0, nodes, CHUNK):
         owned = (iota((CHUNK, hubs), 0) + (base + row) == hubrow).astype(BF16)
-        x32[pl.ds(row, CHUNK), :] = dot(x_ref[pl.ds(row, CHUNK), :], eye) + dot(owned, tags)
+        x32[pl.ds(row, CHUNK), :] = dot(xt_ref[:, pl.ds(row, CHUNK)], eye, CONTRACT_ROWS) + dot(owned, tags)
 
     def pick(i, carry):
         for u in range(16):
@@ -100,9 +109,10 @@
         return carry
 
     lax.fori_loop(0, hubs // 8, pick_hub, 0)
+    hub_rows = pack_rows(hxg[...])
     for q in range(groups):
-        xs[q, pl.ds(0, block), :] = xg[pl.ds(q * block, block), :].astype(BF16)
-        xs[q, pl.ds(block, hubs), :] = hxg[...].astype(BF16)
+        xs[q, pl.ds(0, block // 2), :] = pack_rows(xg[pl.ds(q * block, block), :])
+        xs[q, pl.ds(block // 2, hubs // 2), :] = hub_rows
     pl.semaphore_wait(barrier, groups - 1)
     copies = []
     for step in range(1, groups):
@@ -111,6 +121,8 @@
         copies.append(send(dhg, dhr.at[me], ssem.at[1, step], rsem.at[1, step], peer))
     d4_ref[...] = dst_ref[...] * TILES
     s4_ref[...] = src_ref[...] * TILES
+    used = jnp.where(w_ref[...] > 0.0, 1.0, 0.0).sum(axis=0, keepdims=True).sum(axis=1, keepdims=True)
+    used_ref[...] = jnp.broadcast_to(used, used_ref.shape).astype(I32)
     total = jnp.zeros((8, dh_ref.shape[1]), F32)
     for row in range(0, nodes, CHUNK):
         total = total + dh_ref[pl.ds(row, CHUNK), :].reshape(CHUNK // 8, 8, dh_ref.shape[1]).sum(axis=0)
@@ -119,13 +131,13 @@
     dhr[me] = dhg[...]
     for copy in copies:
         copy.wait()
-    hx = jnp.zeros((hubs, LANES), F32)
+    hx = jnp.zeros((hubs // 2, LANES), F32)
     dhh = jnp.zeros((hubs, LANES), F32)
     for q in range(groups):
-        xh_ref[pl.ds(q * block, block), :] = xr[q, pl.ds(0, block), :]
-        hx = hx + xr[q, pl.ds(block, hubs), :].astype(F32)
+        xh_ref[pl.ds(q * block, block), :] = unpack_rows(xr[q, pl.ds(0, block // 2), :].astype(F32)).astype(BF16)
+        hx = hx + xr[q, pl.ds(block // 2, hubs // 2), :].astype(F32)
         dhh = dhh + dhr[q]
-    hx_ref[...] = hx
+    hx_ref[...] = unpack_rows(hx)
     dhh_ref[...] = dhh
 
 
@@ -146,13 +158,12 @@
     return value
 
 
-def edges_forward_kernel(copies, unroll, d4_ref, s4_ref, w_ref, hub_ref, x_ref, xh_ref, hx_ref, dh_ref, dhh_ref, w1_ref, b1_ref,
+def edges_forward_kernel(copies, unroll, d4_ref, s4_ref, w_ref, hub_ref, used_ref, xt_ref, xh_ref, hx_ref, dh_ref, dhh_ref, w1_ref, b1_ref,
                          h1_ref, dz_ref, hz_ref, hub_out, zt, dt, *accs):
     ya, da = accs[:copies], accs[copies:]
     me = lax.axis_index("graph")
-    nodes, feat = x_ref.shape
+    feat, nodes = xt_ref.shape
     halo, hubs = xh_ref.shape[0], hx_ref.shape[0]
-    edges = w_ref.shape[0]
     base = me * nodes
     for acc in ya:
         acc[...] = jnp.zeros_like(acc)
@@ -160,23 +171,23 @@
         acc[strided(0, nodes + halo + hubs), :] = jnp.zeros((nodes + halo + hubs, LANES), F32)
     w1 = w1_ref[...]
 
-    def put_rows(first, x_rows):
-        z = dot(x_rows, w1).astype(BF16).astype(F32)
+    def put_rows(first, z):
+        z = z.astype(BF16).astype(F32)
         for c in range(TILES):
-            zt[strided(first * TILES + c, x_rows.shape[0]), :] = z[:, c * LANES:(c + 1) * LANES]
-
-    for row in range(0, nodes, CHUNK):
-        put_rows(row, x_ref[pl.ds(row, CHUNK), :])
+            zt[strided(first * TILES + c, z.shape[0]), :] = z[:, c * LANES:(c + 1) * LANES]
+
+    for row in range(0, nodes, CHUNK):
+        put_rows(row, dot(xt_ref[:, pl.ds(row, CHUNK)], w1, CONTRACT_ROWS))
         dt[strided(row * TILES, CHUNK), :] = pad_lanes(dh_ref[pl.ds(row, CHUNK), :])
     for row in range(0, halo, CHUNK):
-        put_rows(nodes + row, xh_ref[pl.ds(row, CHUNK), pl.ds(0, feat)])
-    put_rows(nodes + halo, hx_ref[:, pl.ds(0, feat)].astype(BF16))
+        put_rows(nodes + row, dot(xh_ref[pl.ds(row, CHUNK), pl.ds(0, feat)], w1))
+    put_rows(nodes + halo, dot(hx_ref[:, pl.ds(0, feat)].astype(BF16), w1))
     dt[strided(nodes * TILES, hubs), :] = dhh_ref[...]
 
     def step(i, carry):
         for u0 in range(0, unroll, copies):
             new = []
-            for u in range(copies):
+            for u in range(min(copies, unroll - u0)):
                 j = i * unroll + u0 + u
                 s4 = pl.multiple_of(s4_ref[j], TILES)
                 d4 = pl.multiple_of(d4_ref[j], TILES)
@@ -188,7 +199,7 @@
                 da[u][pl.ds(s4, 1), :] = z_new
         return carry
 
-    lax.fori_loop(0, edges // unroll, step, 0)
+    lax.fori_loop(0, (used_ref[0, 0] + (unroll - 1)) // unroll, step, 0)
 
     def fold(k, carry):
         own, row = hub_position(hub_ref, k, base, nodes)
@@ -269,15 +280,13 @@
         dyh_ref[pl.ds(q * home, home), :] = dyr[q]
 
 
-def edges_backward_kernel(copies, unroll, d4_ref, s4_ref, w_ref, hub_ref, h1_ref, dz2_ref, dyh_ref, w2_ref, h1h_ref, dz2h_ref, xh_ref, db2_ref,
+def edges_backward_kernel(copies, unroll, feat, d4_ref, s4_ref, w_ref, hub_ref, used_ref, h1_ref, dz2_ref, dyh_ref, w2_ref, h1h_ref, dz2h_ref, xh_ref, db2_ref,
                           dz1_ref, hz_ref, hub_out, dw2_ref, bias_ref, yt, *za):
     me = lax.axis_index("graph")
     nodes = h1_ref.shape[0]
     out = w2_ref.shape[1]
     halo, hubs = xh_ref.shape[0], dyh_ref.shape[0]
     home = h1h_ref.shape[0]
-    feat = 50
-    edges = w_ref.shape[0]
     base = me * nodes
     for acc in za:
         acc[...] = jnp.zeros_like(acc)
@@ -319,7 +328,7 @@
                 za[u][pl.ds(s4, TILES), :] = z_new
         return carry
 
-    lax.fori_loop(0, edges // unroll, step, 0)
+    lax.fori_loop(0, (used_ref[0, 0] + (unroll - 1)) // unroll, step, 0)
 
     def fold(k, carry):
         own, row = hub_position(hub_ref, k, base, nodes)
@@ -341,116 +350,131 @@
         cols = pl.ds(c * LANES, LANES)
         hz = total_of(za, strided(nodes * TILES + c, halo))
         hub_out[:, cols] = total_of(za, strided((nodes + halo) * TILES + c, hubs)) + select_rows(onehot, hz, CONTRACT_ROWS)
-        hz_ref[:, cols] = jnp.where(tag > 0.0, 0.0, hz)
-
-
-def final_kernel(groups, hz_ref, hub_ref, dw2_ref, bias_ref, dz1_ref, x_ref, hx_ref, w1_ref, sendrow_ref, hubrow_ref,
-                 gx_ref, gw1_ref, gw2_ref, gb1_ref, gb2_ref,
-                 hzr, hubr, dw2r, biasr, pieces, dw2s, dw2a, dxs, dxa, dw1s, dw1r, dw1t, dw1a, ssem, rsem):
+        hz_ref[c] = jnp.where(tag > 0.0, 0.0, hz)
+
+
+def last_kernel(groups, hz_ref, hub_ref, dw2_ref, bias_ref, dz1_ref, xt_ref, sendrow_ref, hubrow_ref,
+                dz_out, dw1a, dw2a, bias_out,
+                hzr, hubr, biasr, dhs, dha, dw2p, dw2h, dw2r, dw2s, dw1s, dw1r, dw1t, ssem, rsem):
     me = lax.axis_index("graph")
     barrier = greet(groups, me)
-    nodes, feat = x_ref.shape
+    feat, nodes = xt_ref.shape
     home = hub_ref.shape[1]
     hubs = groups * home
-    block = hz_ref.shape[1]
+    block = hz_ref.shape[2]
     halo = groups * block
-    out = gw2_ref.shape[1]
-    part = dw2_ref.shape[1]
     base = me * nodes
+    core = lax.rem(me, 2)
+    partner = me + 1 - 2 * core
+    chip = me // 2
+    chips = groups // 2
+    part = dw2_ref.shape[2]
     hubr[me] = hub_ref[me]
-    dw2r[me] = dw2_ref[me]
     biasr[me] = bias_ref[...]
-    hzr[me] = jnp.zeros(hzr.shape[1:], F32)
+    for c in range(TILES):
+        hzr[c, me] = jnp.zeros((block, LANES), F32)
+        dw1s[c] = jnp.zeros(dw1s.shape[1:], F32)
     pl.semaphore_wait(barrier, groups - 1)
     peers = [lax.rem(me + step, groups) for step in range(1, groups)]
-
-    def to_all(slot, src, dst):
-        return [send(src(peer), dst.at[me], ssem.at[slot, i], rsem.at[slot, i], peer) for i, peer in enumerate(peers)]
-
-    hub_copies = to_all(0, lambda p: hub_ref.at[p], hubr)
-    dw2_copies = to_all(1, lambda p: dw2_ref.at[p], dw2r)
-    bias_copies = to_all(2, lambda p: bias_ref, biasr)
-    halo_copies = to_all(3, lambda p: hz_ref.at[p], hzr)
-    w1 = w1_ref[...]
-    for copy in hub_copies:
-        copy.wait()
+    others = [lax.rem(me + 2 * step, groups) for step in range(1, chips)]
+
+    def to(devices, slot, src, dst):
+        return [send(src(peer), dst, ssem.at[slot, i], rsem.at[slot, i], peer) for i, peer in enumerate(devices)]
+
+    def wait(pending):
+        for copy in pending:
+            copy.wait()
+
+    hub_copies = to(peers, 0, lambda p: hub_ref.at[p], hubr.at[me])
+    pair_copies = to([partner], 1, lambda p: dw2_ref.at[1 - core], dw2p)
+    halo_copies = [to(peers, 5 + c, lambda p: hz_ref.at[c, p], hzr.at[c, me]) for c in range(2)]
+    wait(hub_copies)
     total = hubr[0]
     for q in range(1, groups):
         total = total + hubr[q]
-    dz1h = total.astype(BF16)
-    dxs[...] = pad_lanes(dot(dz1h, w1, CONTRACT_COLS))
-    dx_copies = to_all(4, lambda p: dxs, dxa)
-    dxa[me] = dxs[...]
-    hx_mine = hx_ref[pl.ds(pl.multiple_of(me * home, 8), home), :].astype(BF16)
-    dw1h = dot(hx_mine[:, :feat], dz1h, CONTRACT_ROWS)
-    for copy in dw2_copies:
-        copy.wait()
-    total = dw2r[0]
-    for q in range(1, groups):
-        total = total + dw2r[q]
-    dw2s[...] = total
-    dw2_back = to_all(5, lambda p: dw2s, dw2a)
-    dw2a[me] = dw2s[...]
-    for copy in bias_copies:
-        copy.wait()
+    dhs[...] = total.astype(BF16).astype(F32)
+    back_copies = to(peers, 3, lambda p: dhs, dha.at[me])
+    dha[me] = dhs[...]
+    wait(pair_copies)
+    dw2h[...] = dw2_ref[core] + dw2p[...]
+    dw2r[chip] = dw2h[chip]
+    dw2_copies = to(others, 2, lambda p: dw2h.at[p // 2], dw2r.at[chip])
+    halo_copies += [to(peers, 5 + c, lambda p: hz_ref.at[c, p], hzr.at[c, me]) for c in range(2, TILES)]
+    bias_copies = to(peers, 4, lambda p: bias_ref, biasr.at[me])
+    sendrow = sendrow_ref[...]
+    hubrow = hubrow_ref[...]
+    wait(back_copies)
+    hub_rows = dha[...].reshape(hubs, HID).astype(BF16)
+    rs_copies, ag_copies = [None] * TILES, [None] * TILES
+
+    def spread(c):
+        wait(rs_copies[c])
+        total = dw1r[c, 0]
+        for q in range(1, groups):
+            total = total + dw1r[c, q]
+        dw1t[c] = total
+        ag_copies[c] = to(peers, 13 + c, lambda p: dw1t.at[c], dw1a.at[c, me])
+        dw1a[c, me] = total
+
+    for c in range(TILES):
+        wait(halo_copies[c])
+        cols = pl.ds(c * LANES, LANES)
+        pieces = split3(hzr[c].reshape(halo, LANES))
+        hub_cols = hub_rows[:, c * LANES:(c + 1) * LANES]
+
+        def rows_step(i, carry):
+            row = pl.multiple_of(i * CHUNK, CHUNK)
+            rows = pl.ds(row, CHUNK)
+            onehot = (iota((CHUNK, halo), 0) + row == sendrow).astype(BF16)
+            owned = (iota((CHUNK, hubs), 0) + (base + row) == hubrow).astype(BF16)
+            value = dz1_ref[rows, cols] + dot(owned, hub_cols)
+            for piece in reversed(pieces):
+                value = value + dot(onehot, piece)
+            dz_out[rows, cols] = value.astype(BF16)
+            return carry
+
+        lax.fori_loop(0, nodes // CHUNK, rows_step, 0)
+        dw1s[c, pl.ds(0, feat), :] = dot(xt_ref[...], dz_out[:, cols])
+        rs_copies[c] = to(peers, 9 + c, lambda p: dw1s.at[c, pl.ds(pl.multiple_of(p * 8, 8), 8)], dw1r.at[c, me])
+        dw1r[c, me] = dw1s[c, pl.ds(pl.multiple_of(me * 8, 8), 8), :]
+        if c == 0:
+            wait(dw2_copies)
+            total = dw2r[0]
+            for q in range(1, chips):
+                total = total + dw2r[q]
+            dw2s[...] = total
+            dw2_back = to(peers, 17, lambda p: dw2s, dw2a.at[core, chip])
+            dw2a[core, chip] = total
+        if c > 0:
+            spread(c - 1)
+    wait(bias_copies)
     total = biasr[0]
     for q in range(1, groups):
         total = total + biasr[q]
-    for c in range(TILES):
-        gb1_ref[:, pl.ds(c * LANES, LANES)] = total[c:c + 1, :]
-    gb2_ref[...] = total[TILES:TILES + 1, :out]
-    for copy in halo_copies:
-        copy.wait()
-    for q in range(groups):
-        high, mid, low = split3(hzr[q])
-        pieces[0, pl.ds(q * block, block), :] = low
-        pieces[1, pl.ds(q * block, block), :] = mid
-        pieces[2, pl.ds(q * block, block), :] = high
-    for copy in dx_copies:
-        copy.wait()
-    dx_pieces = split3(dxa[...].reshape(hubs, LANES))
-    sendrow = sendrow_ref[...]
-    hubrow = hubrow_ref[...]
-    dw1s[...] = jnp.zeros_like(dw1s)
-    dw1s[pl.ds(0, feat), :] = dw1h
-
-    def rows_step(i, carry):
-        row = pl.multiple_of(i * CHUNK, CHUNK)
-        rows = pl.ds(row, CHUNK)
-        onehot = (iota((CHUNK, halo), 0) + row == sendrow).astype(BF16)
-        value = dz1_ref[rows, :]
-        for k in range(3):
-            value = value + dot(onehot, pieces[k])
-        dz1 = value.astype(BF16)
-        owned = (iota((CHUNK, hubs), 0) + (base + row) == hubrow).astype(BF16)
-        dx = jnp.zeros((CHUNK, LANES), F32)
-        for piece in reversed(dx_pieces):
-            dx = dx + dot(owned, piece)
-        gx_ref[rows, :] = dot(dz1, w1, CONTRACT_COLS) + dx[:, :feat]
-        dw1s[pl.ds(0, feat), :] += dot(x_ref[rows, :], dz1, CONTRACT_ROWS)
-        return carry
-
-    lax.fori_loop(0, nodes // CHUNK, rows_step, 0)
-    dw1_copies = to_all(6, lambda p: dw1s.at[pl.ds(pl.multiple_of(p * 8, 8), 8)], dw1r)
-    dw1r[me] = dw1s[pl.ds(pl.multiple_of(me * 8, 8), 8), :]
-    for copy in dw2_back:
-        copy.wait()
-    for q in range(groups):
-        gw2_ref[pl.ds(q * part, part), :] = dw2a[q][:, :out]
-    for copy in dw1_copies:
-        copy.wait()
-    total = dw1r[0]
-    for q in range(1, groups):
-        total = total + dw1r[q]
-    dw1t[...] = total
-    dw1_back = to_all(7, lambda p: dw1t, dw1a)
-    dw1a[me] = dw1t[...]
-    for copy in dw1_back:
-        copy.wait()
-    for q in range(groups):
-        rows = min(8, feat - q * 8)
-        if rows > 0:
-            gw1_ref[pl.ds(q * 8, rows), :] = dw1a[q][:rows, :]
+    bias_out[...] = total
+    spread(TILES - 1)
+    wait(dw2_back)
+    for c in range(TILES):
+        wait(ag_copies[c])
+
+
+def outputs_kernel(dz_ref, w1_ref, dw1_ref, dw2_ref, bias_ref, gxt_ref, gw1_ref, gw2_ref, gb1_ref, gb2_ref):
+    nodes = dz_ref.shape[0]
+    feat = w1_ref.shape[0]
+    out = gw2_ref.shape[1]
+    w1 = w1_ref[...]
+    for row in range(0, nodes, 2 * CHUNK):
+        rows = pl.ds(row, 2 * CHUNK)
+        gxt_ref[:, rows] = dot(w1, dz_ref[rows, :], CONTRACT_COLS)
+    for c in range(TILES):
+        cols = pl.ds(c * LANES, LANES)
+        for q in range(dw1_ref.shape[1]):
+            rows = min(8, feat - q * 8)
+            if rows > 0:
+                gw1_ref[pl.ds(q * 8, rows), cols] = dw1_ref[c, q, pl.ds(0, rows), :]
+        gb1_ref[:, cols] = bias_ref[pl.ds(c, 1), :]
+    gw2_ref[...] = dw2_ref[:, pl.ds(0, out)]
+    gb2_ref[...] = bias_ref[pl.ds(TILES, 1), pl.ds(0, out)]
 
 
 def shape(dims, dtype):
@@ -464,13 +488,13 @@
     part_spec = P("data")
     part_rows = P("data", None)
     replicated = P()
-    copies1, unroll1 = 3, 48
+    copies1, unroll1 = 3, 64
     copies2, unroll2 = 4, 64
 
-    def params(collective_id=None):
+    def params(mib, collective_id=None):
         if collective_id is None:
-            return pltpu.CompilerParams(vmem_limit_bytes=VMEM_LIMIT)
-        return pltpu.CompilerParams(vmem_limit_bytes=VMEM_LIMIT, collective_id=collective_id, has_side_effects=True)
+            return pltpu.CompilerParams(vmem_limit_bytes=mib * 2**20)
+        return pltpu.CompilerParams(vmem_limit_bytes=mib * 2**20, collective_id=collective_id, has_side_effects=True)
 
     def device_step(x_loc, dst_loc, src_loc, w_loc, send_loc, hub_ids, w_first, b_first, w_second, dy_out):
         nodes, feat = x_loc.shape
@@ -480,37 +504,39 @@
         out = dy_out.shape[1]
         block, home = halo // groups, hubs // groups
         src_rows, dst_rows = nodes + halo + hubs, nodes + hubs
+        x_t = x_loc.T
         hub_lanes = hub_ids.reshape(1, hubs)
         send_lanes = send_loc.reshape(1, halo)
         bias = b_first.reshape(1, HID)
         sems = lambda n: [pltpu.SemaphoreType.DMA((n, groups)), pltpu.SemaphoreType.DMA((n, groups))]
-
-        xh, hx, dhh, d4, s4, db2 = pl.pallas_call(
+        table = lambda a: a.reshape(edges // LANES, LANES)
+        rows = (edges // LANES, LANES)
+        packed = (block + hubs) // 2
+
+        xh, hx, dhh, d4, s4, used, db2 = pl.pallas_call(
             functools.partial(gather_kernel, groups),
             name="gather_rows",
             out_shape=(shape((halo, LANES), BF16), shape((hubs, LANES), F32), shape((hubs, LANES), F32),
-                       shape((edges // LANES, LANES), I32), shape((edges // LANES, LANES), I32), shape((8, LANES), F32)),
-            in_specs=[VMEM, VMEM, SMEM, SMEM, VMEM, VMEM, VMEM],
-            out_specs=(VMEM,) * 6,
+                       shape(rows, I32), shape(rows, I32), shape((8, LANES), I32), shape((8, LANES), F32)),
+            in_specs=[VMEM, VMEM, SMEM, SMEM, VMEM, VMEM, VMEM, VMEM],
+            out_specs=(VMEM,) * 7,
             scratch_shapes=[pltpu.VMEM((nodes, LANES), F32), pltpu.VMEM((halo, LANES), F32), pltpu.VMEM((hubs, LANES), F32),
-                            pltpu.VMEM((hubs, LANES), F32), pltpu.VMEM((groups, block + hubs, LANES), BF16),
-                            pltpu.VMEM((groups, block + hubs, LANES), BF16), pltpu.VMEM((groups, hubs, LANES), F32)] + sems(2),
-            compiler_params=params(0),
-        )(x_loc, dy_out, send_loc, hub_ids, hub_lanes, dst_loc.reshape(edges // LANES, LANES), src_loc.reshape(edges // LANES, LANES))
+                            pltpu.VMEM((hubs, LANES), F32), pltpu.VMEM((groups, packed, LANES), BF16),
+                            pltpu.VMEM((groups, packed, LANES), BF16), pltpu.VMEM((groups, hubs, LANES), F32)] + sems(2),
+            compiler_params=params(16, 0),
+        )(x_t, dy_out, send_loc, hub_ids, hub_lanes, table(dst_loc), table(src_loc), table(w_loc))
         d4, s4 = d4.reshape(edges), s4.reshape(edges)
-        pad1, pad2 = -edges % unroll1, -edges % unroll2
-        grow = lambda a, n: jnp.pad(a, (0, n)) if n else a
 
         h1, dz, hz, hub = pl.pallas_call(
             functools.partial(edges_forward_kernel, copies1, unroll1),
             name="edges_forward",
             out_shape=(shape((nodes, HID), BF16), shape((nodes, LANES), F32), shape((halo, LANES), F32), shape((hubs, HID + LANES), F32)),
-            in_specs=[SMEM] * 4 + [VMEM] * 7,
+            in_specs=[SMEM] * 5 + [VMEM] * 7,
             out_specs=(VMEM,) * 4,
             scratch_shapes=[pltpu.VMEM((src_rows * TILES, LANES), F32), pltpu.VMEM((dst_rows * TILES, LANES), F32)]
             + [pltpu.VMEM((dst_rows * TILES, LANES), F32)] * copies1 + [pltpu.VMEM((src_rows * TILES, LANES), F32)] * copies1,
-            compiler_params=params(),
-        )(grow(d4, pad1), grow(s4, pad1), grow(w_loc, pad1), hub_ids, x_loc, xh, hx, dy_out, dhh, w_first, bias)
+            compiler_params=params(50),
+        )(d4, s4, w_loc, hub_ids, used, x_t, xh, hx, dy_out, dhh, w_first, bias)
 
         dz2, dyh, h1h, dz2h = pl.pallas_call(
             functools.partial(middle_kernel, groups),
@@ -520,35 +546,45 @@
             out_specs=(VMEM,) * 4,
             scratch_shapes=[pltpu.VMEM((groups, block, LANES), F32), pltpu.VMEM((groups, home, HID + LANES), F32),
                             pltpu.VMEM((groups, home, HID), F32), pltpu.VMEM((home, HID), F32)] + sems(3),
-            compiler_params=params(1),
+            compiler_params=params(12, 1),
         )(hz.reshape(groups, block, LANES), hub.reshape(groups, home, HID + LANES), dz, send_lanes, w_second, bias)
 
         dz1, hz1, hub1, dw2, biases = pl.pallas_call(
-            functools.partial(edges_backward_kernel, copies2, unroll2),
+            functools.partial(edges_backward_kernel, copies2, unroll2, feat),
             name="edges_backward",
-            out_shape=(shape((nodes, HID), F32), shape((halo, HID), F32), shape((hubs, HID), F32), shape((HID, LANES), F32), shape((8, LANES), F32)),
-            in_specs=[SMEM] * 4 + [VMEM] * 8,
+            out_shape=(shape((nodes, HID), F32), shape((TILES, halo, LANES), F32), shape((hubs, HID), F32), shape((HID, LANES), F32), shape((8, LANES), F32)),
+            in_specs=[SMEM] * 5 + [VMEM] * 8,
             out_specs=(VMEM,) * 5,
             scratch_shapes=[pltpu.VMEM((dst_rows * TILES, LANES), F32)] + [pltpu.VMEM((src_rows * TILES, LANES), F32)] * copies2,
-            compiler_params=params(),
-        )(grow(d4, pad2), grow(s4, pad2), grow(w_loc, pad2), hub_ids, h1, dz2, dyh, w_second, h1h, dz2h, xh, db2)
-
-        grad_x, grad_w1, grad_w2, grad_b1, grad_b2 = pl.pallas_call(
-            functools.partial(final_kernel, groups),
-            name="final",
-            out_shape=(shape((nodes, feat), F32), shape((feat, HID), F32), shape((HID, out), F32), shape((1, HID), F32), shape((1, out), F32)),
-            in_specs=[VMEM] * 10,
+            compiler_params=params(44),
+        )(d4, s4, w_loc, hub_ids, used, h1, dz2, dyh, w_second, h1h, dz2h, xh, db2)
+
+        chips = groups // 2
+        part = HID // groups
+        dz1, dw1, dw2, biases = pl.pallas_call(
+            functools.partial(last_kernel, groups),
+            name="last_exchange",
+            out_shape=(shape((nodes, HID), BF16), shape((TILES, groups, 8, LANES), F32), shape((2, chips, part, LANES), F32), shape((8, LANES), F32)),
+            in_specs=[VMEM] * 8,
+            out_specs=(VMEM,) * 4,
+            scratch_shapes=[pltpu.VMEM((TILES, groups, block, LANES), F32), pltpu.VMEM((groups, home, HID), F32),
+                            pltpu.VMEM((groups, 8, LANES), F32), pltpu.VMEM((home, HID), F32), pltpu.VMEM((groups, home, HID), F32),
+                            pltpu.VMEM((chips, part, LANES), F32), pltpu.VMEM((chips, part, LANES), F32), pltpu.VMEM((chips, part, LANES), F32),
+                            pltpu.VMEM((part, LANES), F32),
+                            pltpu.VMEM((TILES, groups * 8, LANES), F32), pltpu.VMEM((TILES, groups, 8, LANES), F32), pltpu.VMEM((TILES, 8, LANES), F32)] + sems(18),
+            compiler_params=params(20, 2),
+        )(hz1.reshape(TILES, groups, block, LANES), hub1.reshape(groups, home, HID), dw2.reshape(2, chips, part, LANES), biases, dz1,
+          x_t, send_lanes, hub_lanes)
+
+        grad_xt, grad_w1, grad_w2, grad_b1, grad_b2 = pl.pallas_call(
+            outputs_kernel,
+            name="outputs",
+            out_shape=(shape((feat, nodes), F32), shape((feat, HID), F32), shape((HID, out), F32), shape((1, HID), F32), shape((1, out), F32)),
+            in_specs=[VMEM] * 5,
             out_specs=(VMEM,) * 5,
-            scratch_shapes=[pltpu.VMEM((groups, block, HID), F32), pltpu.VMEM((groups, home, HID), F32),
-                            pltpu.VMEM((groups, HID // groups, LANES), F32), pltpu.VMEM((groups, 8, LANES), F32),
-                            pltpu.VMEM((3, halo, HID), BF16), pltpu.VMEM((HID // groups, LANES), F32),
-                            pltpu.VMEM((groups, HID // groups, LANES), F32), pltpu.VMEM((home, LANES), F32),
-                            pltpu.VMEM((groups, home, LANES), F32), pltpu.VMEM((groups * 8, HID), F32),
-                            pltpu.VMEM((groups, 8, HID), F32), pltpu.VMEM((8, HID), F32), pltpu.VMEM((groups, 8, HID), F32)] + sems(8),
-            compiler_params=params(2),
-        )(hz1.reshape(groups, block, HID), hub1.reshape(groups, home, HID), dw2.reshape(groups, HID // groups, LANES), biases, dz1,
-          x_loc, hx, w_first, send_lanes, hub_lanes)
-        return grad_x, grad_w1, grad_w2, grad_b1.reshape(HID), grad_b2.reshape(out)
+            compiler_params=params(12),
+        )(dz1, w_first, dw1, dw2.reshape(HID, LANES), biases)
+        return grad_xt.T, grad_w1, grad_w2, grad_b1.reshape(HID), grad_b2.reshape(out)
 
     return jax.shard_map(
         device_step,

time: 147 us -> 123 us (0.84)
  Pallas kernels: 131 us -> 110 us
  local copies, waits for them, and re-layouts: 14.1 us -> 11.2 us
    pallas_call x1, Pallas kernels: 21.7 us -> 10.4 us  [device_step(): pl.pallas_call(functools.partial(middle_kernel, groups), name='middle', o...]
    pallas_call x2 -> x3, Pallas kernels: 68.4 us -> 61.8 us  [the longest x1 36.8 us: device_step(): pl.pallas_call(functools.partial(last_kernel, groups), name='last_exchang...]
    pad x3 -> x0, local copies, waits for them, and re-layouts: 4.12 us -> none  [device_step(): grow = lambda a, n: jnp.pad(a, (0, n)) if n else a]
    pallas_call x1, Pallas kernels: 13.1 us -> 10.5 us  [device_step(): pl.pallas_call(functools.partial(gather_kernel, groups), name='gather_row...]
    unnamed x6 -> x40, local copies, waits for them, and re-layouts: 9.95 us -> 11.2 us
where the time goes in v2:
time: 123 us; the launch traced here: 122 us
  Pallas kernels  110 us (89%)
  local copies, waits for them, and re-layouts  11.2 us (9%)
    pallas_call x1, Pallas kernels, device_step(): pl.pallas_call(functools.partial(last_kernel, groups), name='last_exchang...  36.8 us
    pallas_call x1, Pallas kernels, device_step(): pl.pallas_call(functools.partial(edges_forward_kernel, copies1, unroll1),...  27.5 us
    pallas_call x1, Pallas kernels, device_step(): pl.pallas_call(functools.partial(edges_backward_kernel, copies2, unroll2,...  23.5 us
    unnamed x40, local copies, waits for them, and re-layouts  11.2 us
    pallas_call x1, Pallas kernels, device_step(): pl.pallas_call(functools.partial(gather_kernel, groups), name='gather_row...  10.5 us
    pallas_call x1, Pallas kernels, device_step(): pl.pallas_call(functools.partial(middle_kernel, groups), name='middle', o...  10.4 us

profile of v2, /device:TPU:0, one launch (start us, length us, event | category | flops | bytes accessed | tf_op | source)
XLA Modules:
  0.0 122.2 jit_solution(10534450938918970328)
XLA Ops:
  0.6 0.0 copy-start.15
  0.6 0.0 copy-start
  0.7 1.2 copy-done
  1.9 0.0 copy-start.3
  1.9 0.9 copy-done.3
  2.8 0.0 copy-start.7
  2.8 0.8 copy-done.7
  3.6 0.0 copy-start.12
  3.6 0.8 copy-done.12
  4.3 0.0 copy-start.13
  4.3 0.8 copy-done.13
  5.1 0.0 copy-start.14
  5.1 0.7 copy-done.14
  5.8 0.0 copy-start.16
  5.8 0.7 copy-done.16
  6.4 0.0 copy-start.1
  6.4 0.0 copy-start.6
  6.4 0.0 copy-start.9
  6.4 0.0 copy-start.18
  6.4 10.5 %gather_rows.1 = (bf16[512,128]{1,0:T(8,128)(2,1)S(1)}, f32[64,128]{1,0:T(8,128)S(1)}, f32[64,128]{1,0:T(8,128)S(1)}, s32[64,128]{1,0:T(8,128)S(1)}, s32[64,128]...) custom-call(bf16[50,2048]{1,0:T(8,128)(2,1)S(1)} %bitcast.18, f32[2048,121]{1,0:T(8,128)S(1)} %copy-done, ...), custom_call_target="tpu_custom_call" | custom-call | tf_op jit(solution)/shard_map/gather_rows/pallas_call | solution.py:516
  17.0 0.0 copy-done.1
  17.0 0.0 copy-start.4
  17.0 0.9 copy-done.4
  17.9 0.0 copy-start.8
  17.9 0.8 copy-done.8
  18.7 0.0 copy-start.10
  18.7 0.8 copy-done.10
  19.5 0.0 copy-start.17
  19.5 0.7 copy-done.17
  20.2 0.0 copy-start.19
  20.2 0.7 copy-done.19
  20.8 27.5 %edges_forward.1 = (bf16[2048,512]{1,0:T(8,128)(2,1)}, f32[2048,128]{1,0:T(8,128)S(1)}, f32[512,128]{1,0:T(8,128)S(1)}, f32[64,640]{1,0:T(8,128)S(1)}) custom-call(s32[8192]{0:T(1024)S(1)} %bitcast.27, s32[8192]{0:T(1024)S(1)} %bitcast.29, f32[8192]{0:T(1024)S(1)} %copy-done.8, s32[64]{0:T(128)S(1)} %copy-done.17, s32[8,128]{1,0:T(8,128)S(1)} %get-tuple-element.36.used_ref, ...), custom_call_target="tpu_custom_call" | custom-call | tf_op jit(solution)/shard_map/edges_forward/pallas_call | solution.py:530
  48.3 0.0 copy-done.15
  48.3 0.0 copy-done.6
  48.3 0.0 copy-start.5
  48.3 10.4 %middle.1 = (bf16[2048,128]{1,0:T(8,128)(2,1)S(1)}, f32[64,512]{1,0:T(8,128)S(1)}, bf16[8,512]{1,0:T(8,128)(2,1)S(1)}, bf16[8,128]{1,0:T(8,128)(2,1)S(1)}) custom-call(f32[8,64,128]{2,1,0:T(8,128)S(1)} %bitcast.25, f32[8,8,640]{2,1,0:T(8,128)S(1)} %bitcast.26, f32[2048,128]{1,0:T(8,128)S(1)} %get-tuple-element.43.dz_ref, s32[1,512]{1,0:T(1,128)S(1)} %bitcast.34, ...), custom_call_target="tpu_custom_call" | custom-call | tf_op jit(solution)/shard_map/middle/pallas_call | solution.py:541
  58.7 0.0 copy-done.9
  58.7 0.0 copy-done.18
  58.8 0.0 copy-start.2
  58.8 1.6 %copy-done.2 = bf16[2048,512]{1,0:T(8,128)(2,1)S(1)} copy-done((bf16[2048,512]{1,0:T(8,128)(2,1)S(1)}, bf16[2048,512]{1,0:T(8,128)(2,1)}, u32[]{:S(2)}) %copy-start.2) | copy-done | bytes 2097176
  60.3 23.5 %edges_backward.1 = (f32[2048,512]{1,0:T(8,128)S(1)}, f32[4,512,128]{2,1,0:T(8,128)S(1)}, f32[64,512]{1,0:T(8,128)S(1)}, f32[512,128]{1,0:T(8,128)S(1)}, f32[8,128]{1,0:T(8,128)S(1)}) custom-call(s32[8192]{0:T(1024)S(1)} %bitcast.28, s32[8192]{0:T(1024)S(1)} %bitcast.30, f32[8192]{0:T(1024)S(1)} %copy-done.9, s32[64]{0:T(128)S(1)} %copy-done.18, ...), custom_call_target="tpu_custom_call" | custom-call | tf_op jit(solution)/shard_map/edges_backward/pallas_call | solution.py:552
  83.8 0.0 copy-done.5
  83.9 0.0 copy-start.11
  83.9 36.8 %last_exchange.1 = (bf16[2048,512]{1,0:T(8,128)(2,1)S(1)}, f32[4,8,8,128]{3,2,1,0:T(8,128)S(1)}, f32[2,4,64,128]{3,2,1,0:T(8,128)S(1)}, f32[8,128]{1,0:T(8,128)S(1)}) custom-call(f32[4,8,64,128]{3,2,1,0:T(8,128)S(1)} %bitcast.21, f32[8,8,512]{2,1,0:T(8,128)S(1)} %bitcast.31, f32[2,4,64,128]{3,2,1,0:T(8,128)S(1)} %bitcast.23, ...), custom_call_target="tpu_custom_call" | custom-call | tf_op jit(solution)/shard_map/last_exchange/pallas_call | solution.py:564
  120.7 0.0 copy-done.11
  120.7 1.5 %outputs.1 = (f32[50,2048]{1,0:T(8,128)}, f32[50,512]{1,0:T(8,128)}, f32[512,121]{1,0:T(8,128)}, f32[1,512]{1,0:T(1,128)}, f32[1,121]{1,0:T(1,128)}) custom-call(bf16[2048,512]{1,0:T(8,128)(2,1)S(1)} %get-tuple-element.54.dz_ref, bf16[50,512]{1,0:T(8,128)(2,1)S(1)} %copy-done.11, f32[4,8,8,128]{3,2,1,0:T(8,128)S(1)} %get-tuple-element.55.dw1_ref, ...), custom_call_target="tpu_custom_call" | custom-call | tf_op jit(solution)/shard_map/outputs/pallas_call | solution.py:579
Async XLA Ops:
  0.6 47.7 %copy-start.15 = (s32[512]{0:T(512)S(1)}, s32[512]{0:T(512)}, u32[]{:S(2)}) copy-start(s32[512]{0:T(512)} %send_ref.1) | copy-start | bytes 6148
  0.6 1.2 %copy-start = (f32[2048,121]{1,0:T(8,128)S(1)}, f32[2048,121]{1,0:T(8,128)}, u32[]{:S(2)}) copy-start(f32[2048,121]{1,0:T(8,128)} %dh_ref.3) | copy-start | bytes 2973700
  1.9 0.9 copy-start.3
  2.8 0.8 copy-start.7
  3.6 0.8 copy-start.12
  4.3 0.8 copy-start.13
  5.1 0.7 copy-start.14
  5.8 0.7 copy-start.16
  6.4 10.5 %copy-start.1 = (f32[2048,121]{1,0:T(8,128)S(1)}, f32[2048,121]{1,0:T(8,128)}, u32[]{:S(2)}) copy-start(f32[2048,121]{1,0:T(8,128)} %dh_ref.3) | copy-start | bytes 2973700
  6.4 41.9 %copy-start.6 = (bf16[512,121]{1,0:T(8,128)(2,1)S(1)}, bf16[512,121]{1,0:T(8,128)(2,1)}, u32[]{:S(2)}) copy-start(bf16[512,121]{1,0:T(8,128)(2,1)} %w2_ref.3) | copy-start | bytes 371716
  6.4 52.3 %copy-start.9 = (f32[8192]{0:T(1024)S(1)}, f32[8192]{0:T(1024)}, u32[]{:S(2)}) copy-start(f32[8192]{0:T(1024)} %w_ref.3) | copy-start | bytes 98308
  6.4 52.3 %copy-start.18 = (s32[64]{0:T(128)S(1)}, s32[64]{0:T(128)}, u32[]{:S(2)}) copy-start(s32[64]{0:T(128)} %hub_ref.5) | copy-start | bytes 772
  17.0 0.9 copy-start.4
  17.9 0.8 copy-start.8
  18.7 0.8 copy-start.10
  19.5 0.7 copy-start.17
  20.2 0.7 copy-start.19
  48.3 35.5 %copy-start.5 = (bf16[2048,50]{0,1:T(8,128)(2,1)S(1)}, bf16[2048,50]{0,1:T(8,128)(2,1)}, u32[]{:S(2)}) copy-start(bf16[2048,50]{0,1:T(8,128)(2,1)} %param.10) | copy-start | bytes 614404
  58.8 1.6 %copy-start.2 = (bf16[2048,512]{1,0:T(8,128)(2,1)S(1)}, bf16[2048,512]{1,0:T(8,128)(2,1)}, u32[]{:S(2)}) copy-start(bf16[2048,512]{1,0:T(8,128)(2,1)} %get-tuple-element.40.h1_ref) | copy-start | bytes 6291460
  83.9 36.8 %copy-start.11 = (bf16[50,512]{1,0:T(8,128)(2,1)S(1)}, bf16[50,512]{1,0:T(8,128)(2,1)}, u32[]{:S(2)}) copy-start(bf16[50,512]{1,0:T(8,128)(2,1)} %w1_ref.3) | copy-start | bytes 153604

commit v3 on v2

--- a/solution.py
+++ b/solution.py
@@ -14,8 +14,58 @@
 HID = 512
 TILES = HID // LANES
 CHUNK = 256
-VMEM = pl.BlockSpec(memory_space=pltpu.VMEM)
-SMEM = pl.BlockSpec(memory_space=pltpu.SMEM)
+VMEM_LIMIT = 67043328
+HBM = pl.BlockSpec(memory_space=pltpu.HBM)
+
+
+class Fetched:
+    def __init__(self, src, dst, sem):
+        self.copy, self.ref, self.pending = pltpu.make_async_copy(src, dst, sem), dst, True
+        self.copy.start()
+
+    def get(self):
+        if self.pending:
+            self.copy.wait()
+            self.pending = False
+        return self.ref
+
+
+def call(kernel, args, out_shape, scratch_shapes, name, compiler_params):
+    spaces = {"vmem": pltpu.VMEM, "smem": pltpu.SMEM}
+    in_buffers = [spaces[space](array.shape, array.dtype) for array, space in args]
+    out_buffers = [pltpu.VMEM(out.shape, out.dtype) for out in out_shape]
+    n_in, n_out = len(args), len(out_shape)
+
+    def body(*refs):
+        inputs, outputs = refs[:n_in], refs[n_in:n_in + n_out]
+        bufs = refs[n_in + n_out:2 * n_in + 2 * n_out]
+        scratch, sems, out_sems = refs[2 * n_in + 2 * n_out:-2], refs[-2], refs[-1]
+        fetched = [Fetched(ref, bufs[n], sems.at[n]) for n, ref in enumerate(inputs)]
+        results = bufs[n_in:]
+        stores = {}
+
+        def flush(*buffers):
+            for buffer in buffers:
+                n = [k for k in range(n_out) if results[k] is buffer][0]
+                stores[n] = pltpu.make_async_copy(results[n], outputs[n], out_sems.at[n])
+                stores[n].start()
+
+        kernel(*fetched, *results, *scratch, flush=flush)
+        for item in fetched:
+            item.get()
+        flush(*[results[n] for n in range(n_out) if n not in stores])
+        for n in range(n_out):
+            stores[n].wait()
+
+    return pl.pallas_call(
+        body,
+        name=name,
+        out_shape=out_shape,
+        in_specs=[HBM] * n_in,
+        out_specs=(HBM,) * n_out,
+        scratch_shapes=in_buffers + out_buffers + list(scratch_shapes) + [pltpu.SemaphoreType.DMA((n_in,)), pltpu.SemaphoreType.DMA((n_out,))],
+        compiler_params=compiler_params,
+    )(*[array for array, _ in args])
 
 
 def dot(a, b, dims=(((1,), (0,)), ((), ()))):
@@ -71,22 +121,25 @@
     return jnp.concatenate([value, pltpu.roll(value, LANES // 2, 1)], axis=0)
 
 
-def gather_kernel(groups, xt_ref, dh_ref, send_ref, hub_ref, hubrow_ref, dst_ref, src_ref, w_ref,
+def gather_kernel(groups, hubrow, xt, send_idx, hub_ids, dh, dst, src, w,
                   xh_ref, hx_ref, dhh_ref, d4_ref, s4_ref, used_ref, db2_ref,
-                  x32, xg, hxg, dhg, xs, xr, dhr, ssem, rsem):
+                  x32, xg, hxg, dhg, xs, xr, dhr, ssem, rsem, flush):
     me = lax.axis_index("graph")
     barrier = greet(groups, me)
-    feat, nodes = xt_ref.shape
-    hubs = hub_ref.shape[0]
-    halo = send_ref.shape[0]
+    feat, nodes = xt.ref.shape
+    hubs = hub_ids.ref.shape[0]
+    halo = send_idx.ref.shape[0]
     block = halo // groups
     base = me * nodes
     eye = (iota((feat, LANES), 0) == iota((feat, LANES), 1)).astype(BF16)
     tags = jnp.where(iota((hubs, LANES), 1) == feat, iota((hubs, LANES), 0) + 1, 0).astype(F32).astype(BF16)
-    hubrow = hubrow_ref[...]
+    hubrow = hubrow.get()[...]
+    xt_ref = xt.get()
     for row in range(0, nodes, CHUNK):
         owned = (iota((CHUNK, hubs), 0) + (base + row) == hubrow).astype(BF16)
         x32[pl.ds(row, CHUNK), :] = dot(xt_ref[:, pl.ds(row, CHUNK)], eye, CONTRACT_ROWS) + dot(owned, tags)
+
+    send_ref = send_idx.get()
 
     def pick(i, carry):
         for u in range(16):
@@ -96,6 +149,7 @@
 
     lax.fori_loop(0, halo // 16, pick, 0)
     dhg[...] = jnp.zeros_like(dhg)
+    hub_ref, dh_ref = hub_ids.get(), dh.get()
 
     def pick_hub(i, carry):
         for u in range(8):
@@ -119,14 +173,15 @@
         peer = lax.rem(me + step, groups)
         copies.append(send(xs.at[peer], xr.at[me], ssem.at[0, step], rsem.at[0, step], peer))
         copies.append(send(dhg, dhr.at[me], ssem.at[1, step], rsem.at[1, step], peer))
-    d4_ref[...] = dst_ref[...] * TILES
-    s4_ref[...] = src_ref[...] * TILES
-    used = jnp.where(w_ref[...] > 0.0, 1.0, 0.0).sum(axis=0, keepdims=True).sum(axis=1, keepdims=True)
+    d4_ref[...] = dst.get()[...] * TILES
+    s4_ref[...] = src.get()[...] * TILES
+    used = jnp.where(w.get()[...] > 0.0, 1.0, 0.0).sum(axis=0, keepdims=True).sum(axis=1, keepdims=True)
     used_ref[...] = jnp.broadcast_to(used, used_ref.shape).astype(I32)
     total = jnp.zeros((8, dh_ref.shape[1]), F32)
     for row in range(0, nodes, CHUNK):
         total = total + dh_ref[pl.ds(row, CHUNK), :].reshape(CHUNK // 8, 8, dh_ref.shape[1]).sum(axis=0)
     db2_ref[...] = jnp.broadcast_to(pad_lanes(total.sum(axis=0, keepdims=True)), db2_ref.shape)
+    flush(d4_ref, s4_ref, used_ref, db2_ref)
     xr[me] = xs[me]
     dhr[me] = dhg[...]
     for copy in copies:
@@ -158,18 +213,19 @@
     return value
 
 
-def edges_forward_kernel(copies, unroll, d4_ref, s4_ref, w_ref, hub_ref, used_ref, xt_ref, xh_ref, hx_ref, dh_ref, dhh_ref, w1_ref, b1_ref,
-                         h1_ref, dz_ref, hz_ref, hub_out, zt, dt, *accs):
+def edges_forward_kernel(copies, unroll, w1, xt, dh, xh, hx, dhh, d4, s4, w, used, hub_ids, b1,
+                         h1_ref, dz_ref, hz_ref, hub_out, zt, dt, *accs, flush):
     ya, da = accs[:copies], accs[copies:]
     me = lax.axis_index("graph")
-    feat, nodes = xt_ref.shape
-    halo, hubs = xh_ref.shape[0], hx_ref.shape[0]
+    feat, nodes = xt.ref.shape
+    halo, hubs = xh.ref.shape[0], hx.ref.shape[0]
     base = me * nodes
     for acc in ya:
         acc[...] = jnp.zeros_like(acc)
     for acc in da:
         acc[strided(0, nodes + halo + hubs), :] = jnp.zeros((nodes + halo + hubs, LANES), F32)
-    w1 = w1_ref[...]
+    w1 = w1.get()[...]
+    xt_ref, dh_ref, xh_ref, hx_ref = xt.get(), dh.get(), xh.get(), hx.get()
 
     def put_rows(first, z):
         z = z.astype(BF16).astype(F32)
@@ -182,7 +238,8 @@
     for row in range(0, halo, CHUNK):
         put_rows(nodes + row, dot(xh_ref[pl.ds(row, CHUNK), pl.ds(0, feat)], w1))
     put_rows(nodes + halo, dot(hx_ref[:, pl.ds(0, feat)].astype(BF16), w1))
-    dt[strided(nodes * TILES, hubs), :] = dhh_ref[...]
+    dt[strided(nodes * TILES, hubs), :] = dhh.get()[...]
+    d4_ref, s4_ref, used_ref, w_ref, hub_ref, b1_ref = d4.get(), s4.get(), used.get(), w.get(), hub_ids.get(), b1.get()
 
     def step(i, carry):
         for u0 in range(0, unroll, copies):
@@ -219,7 +276,10 @@
             cols = pl.ds(c * LANES, LANES)
             y = total_of(ya, strided(row * TILES + c, CHUNK)) + b1_ref[:, cols]
             h1_ref[pl.ds(row, CHUNK), cols] = jnp.maximum(y, 0.0).astype(BF16)
+    flush(h1_ref)
+    for row in range(0, nodes, CHUNK):
         dz_ref[pl.ds(row, CHUNK), :] = total_of(da, strided(row * TILES, CHUNK))
+    flush(dz_ref)
     hz = total_of(da, strided(nodes * TILES, halo))
     tag = xh_ref[...].astype(F32)[:, feat:feat + 1]
     onehot = (tag == (iota((halo, hubs), 1) + 1).astype(F32)).astype(BF16)
@@ -230,16 +290,17 @@
     hub_out[:, pl.ds(HID, LANES)] = hub_z
 
 
-def middle_kernel(groups, hz_ref, hub_ref, dz_ref, sendrow_ref, w2_ref, b1_ref,
+def middle_kernel(groups, hub, hz, dz, b1, w2, sendrow,
                   dz2_ref, dyh_ref, h1h_ref, dz2h_ref,
-                  hzr, hubr, dyr, dys, ssem, rsem):
+                  hzr, hubr, dyr, dys, ssem, rsem, flush):
     me = lax.axis_index("graph")
     barrier = greet(groups, me)
-    nodes = dz_ref.shape[0]
-    out = w2_ref.shape[1]
-    home = hub_ref.shape[1]
-    block = hz_ref.shape[1]
+    nodes = dz.ref.shape[0]
+    out = w2.ref.shape[1]
+    home = hub.ref.shape[1]
+    block = hz.ref.shape[1]
     halo = groups * block
+    hub_ref, hz_ref = hub.get(), hz.get()
     hubr[me] = hub_ref[me]
     hzr[me] = jnp.zeros(hzr.shape[1:], F32)
     pl.semaphore_wait(barrier, groups - 1)
@@ -255,6 +316,7 @@
     total = hubr[0]
     for q in range(1, groups):
         total = total + hubr[q]
+    b1_ref, w2_ref, sendrow = b1.get(), w2.get(), sendrow.get()[...]
     pre = total[:, :HID] + b1_ref[...]
     dz2h = total[:, HID:].astype(BF16)
     h1h_ref[...] = jnp.maximum(pre, 0.0).astype(BF16)
@@ -267,7 +329,7 @@
     for copy in halo_copies:
         copy.wait()
     pieces = split3(hzr[...].reshape(halo, LANES))
-    sendrow = sendrow_ref[...]
+    dz_ref = dz.get()
     for row in range(0, nodes, CHUNK):
         onehot = (iota((CHUNK, halo), 0) + row == sendrow).astype(BF16)
         value = dz_ref[pl.ds(row, CHUNK), :]
@@ -280,17 +342,17 @@
         dyh_ref[pl.ds(q * home, home), :] = dyr[q]
 
 
-def edges_backward_kernel(copies, unroll, feat, d4_ref, s4_ref, w_ref, hub_ref, used_ref, h1_ref, dz2_ref, dyh_ref, w2_ref, h1h_ref, dz2h_ref, xh_ref, db2_ref,
-                          dz1_ref, hz_ref, hub_out, dw2_ref, bias_ref, yt, *za):
+def edges_backward_kernel(copies, unroll, feat, w2, h1, dz2, dyh, h1h, dz2h, d4, s4, w, used, hub_ids, xh, db2,
+                          dz1_ref, hz_ref, hub_out, dw2_ref, bias_ref, yt, *za, flush):
     me = lax.axis_index("graph")
-    nodes = h1_ref.shape[0]
-    out = w2_ref.shape[1]
-    halo, hubs = xh_ref.shape[0], dyh_ref.shape[0]
-    home = h1h_ref.shape[0]
+    nodes = h1.ref.shape[0]
+    out = w2.ref.shape[1]
+    halo, hubs = xh.ref.shape[0], dyh.ref.shape[0]
+    home = h1h.ref.shape[0]
     base = me * nodes
     for acc in za:
         acc[...] = jnp.zeros_like(acc)
-    w2 = w2_ref[...]
+    w2, h1_ref, dz2_ref, dyh_ref, h1h_ref, dz2h_ref = w2.get()[...], h1.get(), dz2.get(), dyh.get(), h1h.get(), dz2h.get()
     mine = dyh_ref[pl.ds(pl.multiple_of(me * home, 8), home), :]
     db1 = mine
     for row in range(0, nodes, CHUNK):
@@ -301,11 +363,13 @@
         for c in range(TILES):
             yt[strided(row * TILES + c, CHUNK), :] = grad[:, c * LANES:(c + 1) * LANES]
     db1 = db1.sum(axis=0, keepdims=True)
-    bias_ref[...] = db2_ref[...]
+    bias_ref[...] = db2.get()[...]
     for c in range(TILES):
         bias_ref[pl.ds(c, 1), :] = db1[:, c * LANES:(c + 1) * LANES]
         yt[strided(nodes * TILES + c, hubs), :] = dyh_ref[:, pl.ds(c * LANES, LANES)]
     dw2_ref[...] = dot(h1_ref[...], dz2_ref[...], CONTRACT_ROWS) + dot(h1h_ref[...], dz2h_ref[...], CONTRACT_ROWS)
+    flush(dw2_ref, bias_ref)
+    d4_ref, s4_ref, used_ref, w_ref, hub_ref, xh_ref = d4.get(), s4.get(), used.get(), w.get(), hub_ids.get(), xh.get()
 
     def place(k, carry):
         own, row = hub_position(hub_ref, k, base, nodes)
@@ -344,6 +408,7 @@
     for row in range(0, nodes, CHUNK):
         for c in range(TILES):
             dz1_ref[pl.ds(row, CHUNK), pl.ds(c * LANES, LANES)] = total_of(za, strided(row * TILES + c, CHUNK))
+    flush(dz1_ref)
     tag = xh_ref[...].astype(F32)[:, feat:feat + 1]
     onehot = (tag == (iota((halo, hubs), 1) + 1).astype(F32)).astype(BF16)
     for c in range(TILES):
@@ -353,17 +418,16 @@
         hz_ref[c] = jnp.where(tag > 0.0, 0.0, hz)
 
 
-def last_kernel(groups, hz_ref, hub_ref, dw2_ref, bias_ref, dz1_ref, xt_ref, sendrow_ref, hubrow_ref,
-                dz_out, dw1a, dw2a, bias_out,
-                hzr, hubr, biasr, dhs, dha, dw2p, dw2h, dw2r, dw2s, dw1s, dw1r, dw1t, ssem, rsem):
+def last_kernel(groups, hub, hz, dw2, bias, sendrow, xt, hx, dz1,
+                dz_out, dha, dw1a, dw2a, bias_out,
+                onehot, hzr, hubr, biasr, dhs, dw2p, dw2h, dw2r, dw2s, dw1s, dw1r, dw1t, ssem, rsem, flush):
     me = lax.axis_index("graph")
     barrier = greet(groups, me)
-    feat, nodes = xt_ref.shape
-    home = hub_ref.shape[1]
-    hubs = groups * home
-    block = hz_ref.shape[2]
+    feat, nodes = xt.ref.shape
+    home = hub.ref.shape[1]
+    block = hz.ref.shape[2]
     halo = groups * block
-    base = me * nodes
+    hub_ref, hz_ref, dw2_ref, bias_ref = hub.get(), hz.get(), dw2.get(), bias.get()
     core = lax.rem(me, 2)
     partner = me + 1 - 2 * core
     chip = me // 2
@@ -392,7 +456,8 @@
     total = hubr[0]
     for q in range(1, groups):
         total = total + hubr[q]
-    dhs[...] = total.astype(BF16).astype(F32)
+    dz1h = total.astype(BF16)
+    dhs[...] = dz1h
     back_copies = to(peers, 3, lambda p: dhs, dha.at[me])
     dha[me] = dhs[...]
     wait(pair_copies)
@@ -401,10 +466,11 @@
     dw2_copies = to(others, 2, lambda p: dw2h.at[p // 2], dw2r.at[chip])
     halo_copies += [to(peers, 5 + c, lambda p: hz_ref.at[c, p], hzr.at[c, me]) for c in range(2, TILES)]
     bias_copies = to(peers, 4, lambda p: bias_ref, biasr.at[me])
-    sendrow = sendrow_ref[...]
-    hubrow = hubrow_ref[...]
-    wait(back_copies)
-    hub_rows = dha[...].reshape(hubs, HID).astype(BF16)
+    hx_mine = hx.get()[pl.ds(pl.multiple_of(me * home, 8), home), :].astype(BF16)
+    dw1h = dot(hx_mine[:, :feat], dz1h, CONTRACT_ROWS)
+    sendrow, xt_ref, dz1_ref = sendrow.get()[...], xt.get(), dz1.get()
+    for row in range(0, nodes, CHUNK):
+        onehot[pl.ds(row, CHUNK), :] = (iota((CHUNK, halo), 0) + row == sendrow).astype(BF16)
     rs_copies, ag_copies = [None] * TILES, [None] * TILES
 
     def spread(c):
@@ -419,22 +485,17 @@
     for c in range(TILES):
         wait(halo_copies[c])
         cols = pl.ds(c * LANES, LANES)
-        pieces = split3(hzr[c].reshape(halo, LANES))
-        hub_cols = hub_rows[:, c * LANES:(c + 1) * LANES]
+        pieces = jnp.concatenate(split3(hzr[c].reshape(halo, LANES)), axis=1)
 
         def rows_step(i, carry):
-            row = pl.multiple_of(i * CHUNK, CHUNK)
-            rows = pl.ds(row, CHUNK)
-            onehot = (iota((CHUNK, halo), 0) + row == sendrow).astype(BF16)
-            owned = (iota((CHUNK, hubs), 0) + (base + row) == hubrow).astype(BF16)
-            value = dz1_ref[rows, cols] + dot(owned, hub_cols)
-            for piece in reversed(pieces):
-                value = value + dot(onehot, piece)
-            dz_out[rows, cols] = value.astype(BF16)
+            rows = pl.ds(pl.multiple_of(i * CHUNK, CHUNK), CHUNK)
+            value = dot(onehot[rows, :], pieces)
+            value = value[:, 2 * LANES:] + value[:, LANES:2 * LANES] + value[:, :LANES]
+            dz_out[rows, cols] = (dz1_ref[rows, cols] + value).astype(BF16)
             return carry
 
         lax.fori_loop(0, nodes // CHUNK, rows_step, 0)
-        dw1s[c, pl.ds(0, feat), :] = dot(xt_ref[...], dz_out[:, cols])
+        dw1s[c, pl.ds(0, feat), :] = dot(xt_ref[...], dz_out[:, cols]) + dw1h[:, c * LANES:(c + 1) * LANES]
         rs_copies[c] = to(peers, 9 + c, lambda p: dw1s.at[c, pl.ds(pl.multiple_of(p * 8, 8), 8)], dw1r.at[c, me])
         dw1r[c, me] = dw1s[c, pl.ds(pl.multiple_of(me * 8, 8), 8), :]
         if c == 0:
@@ -447,6 +508,7 @@
             dw2a[core, chip] = total
         if c > 0:
             spread(c - 1)
+    flush(dz_out)
     wait(bias_copies)
     total = biasr[0]
     for q in range(1, groups):
@@ -454,18 +516,25 @@
     bias_out[...] = total
     spread(TILES - 1)
     wait(dw2_back)
+    wait(back_copies)
     for c in range(TILES):
         wait(ag_copies[c])
 
 
-def outputs_kernel(dz_ref, w1_ref, dw1_ref, dw2_ref, bias_ref, gxt_ref, gw1_ref, gw2_ref, gb1_ref, gb2_ref):
-    nodes = dz_ref.shape[0]
-    feat = w1_ref.shape[0]
+def outputs_kernel(w1, hubrow, dzh, dw1, dw2, bias, dz, gxt_ref, gw1_ref, gw2_ref, gb1_ref, gb2_ref, flush):
+    nodes = dz.ref.shape[0]
+    hubs = dzh.ref.shape[0]
+    feat = w1.ref.shape[0]
     out = gw2_ref.shape[1]
-    w1 = w1_ref[...]
+    base = lax.axis_index("graph") * nodes
+    w1, hubrow, dzh_ref, dz_ref = w1.get()[...], hubrow.get()[...], dzh.get(), dz.get()
     for row in range(0, nodes, 2 * CHUNK):
         rows = pl.ds(row, 2 * CHUNK)
-        gxt_ref[:, rows] = dot(w1, dz_ref[rows, :], CONTRACT_COLS)
+        owned = (iota((2 * CHUNK, hubs), 0) + (base + row) == hubrow).astype(BF16)
+        dz = (dz_ref[rows, :].astype(F32) + dot(owned, dzh_ref[...])).astype(BF16)
+        gxt_ref[:, rows] = dot(w1, dz, CONTRACT_COLS)
+    flush(gxt_ref)
+    dw1_ref, dw2_ref, bias_ref = dw1.get(), dw2.get(), bias.get()
     for c in range(TILES):
         cols = pl.ds(c * LANES, LANES)
         for q in range(dw1_ref.shape[1]):
@@ -491,10 +560,10 @@
     copies1, unroll1 = 3, 64
     copies2, unroll2 = 4, 64
 
-    def params(mib, collective_id=None):
+    def params(collective_id=None):
         if collective_id is None:
-            return pltpu.CompilerParams(vmem_limit_bytes=mib * 2**20)
-        return pltpu.CompilerParams(vmem_limit_bytes=mib * 2**20, collective_id=collective_id, has_side_effects=True)
+            return pltpu.CompilerParams(vmem_limit_bytes=VMEM_LIMIT)
+        return pltpu.CompilerParams(vmem_limit_bytes=VMEM_LIMIT, collective_id=collective_id, has_side_effects=True)
 
     def device_step(x_loc, dst_loc, src_loc, w_loc, send_loc, hub_ids, w_first, b_first, w_second, dy_out):
         nodes, feat = x_loc.shape
@@ -513,77 +582,64 @@
         rows = (edges // LANES, LANES)
         packed = (block + hubs) // 2
 
-        xh, hx, dhh, d4, s4, used, db2 = pl.pallas_call(
+        xh, hx, dhh, d4, s4, used, db2 = call(
             functools.partial(gather_kernel, groups),
-            name="gather_rows",
-            out_shape=(shape((halo, LANES), BF16), shape((hubs, LANES), F32), shape((hubs, LANES), F32),
-                       shape(rows, I32), shape(rows, I32), shape((8, LANES), I32), shape((8, LANES), F32)),
-            in_specs=[VMEM, VMEM, SMEM, SMEM, VMEM, VMEM, VMEM, VMEM],
-            out_specs=(VMEM,) * 7,
-            scratch_shapes=[pltpu.VMEM((nodes, LANES), F32), pltpu.VMEM((halo, LANES), F32), pltpu.VMEM((hubs, LANES), F32),
-                            pltpu.VMEM((hubs, LANES), F32), pltpu.VMEM((groups, packed, LANES), BF16),
-                            pltpu.VMEM((groups, packed, LANES), BF16), pltpu.VMEM((groups, hubs, LANES), F32)] + sems(2),
-            compiler_params=params(16, 0),
-        )(x_t, dy_out, send_loc, hub_ids, hub_lanes, table(dst_loc), table(src_loc), table(w_loc))
+            [(hub_lanes, "vmem"), (x_t, "vmem"), (send_loc, "smem"), (hub_ids, "smem"), (dy_out, "vmem"),
+             (table(dst_loc), "vmem"), (table(src_loc), "vmem"), (table(w_loc), "vmem")],
+            (shape((halo, LANES), BF16), shape((hubs, LANES), F32), shape((hubs, LANES), F32),
+             shape(rows, I32), shape(rows, I32), shape((8, LANES), I32), shape((8, LANES), F32)),
+            [pltpu.VMEM((nodes, LANES), F32), pltpu.VMEM((halo, LANES), F32), pltpu.VMEM((hubs, LANES), F32),
+             pltpu.VMEM((hubs, LANES), F32), pltpu.VMEM((groups, packed, LANES), BF16),
+             pltpu.VMEM((groups, packed, LANES), BF16), pltpu.VMEM((groups, hubs, LANES), F32)] + sems(2),
+            "gather_rows", params(0))
         d4, s4 = d4.reshape(edges), s4.reshape(edges)
 
-        h1, dz, hz, hub = pl.pallas_call(
+        h1, dz, hz, hub = call(
             functools.partial(edges_forward_kernel, copies1, unroll1),
-            name="edges_forward",
-            out_shape=(shape((nodes, HID), BF16), shape((nodes, LANES), F32), shape((halo, LANES), F32), shape((hubs, HID + LANES), F32)),
-            in_specs=[SMEM] * 5 + [VMEM] * 7,
-            out_specs=(VMEM,) * 4,
-            scratch_shapes=[pltpu.VMEM((src_rows * TILES, LANES), F32), pltpu.VMEM((dst_rows * TILES, LANES), F32)]
+            [(w_first, "vmem"), (x_t, "vmem"), (dy_out, "vmem"), (xh, "vmem"), (hx, "vmem"), (dhh, "vmem"),
+             (d4, "smem"), (s4, "smem"), (w_loc, "smem"), (used, "smem"), (hub_ids, "smem"), (bias, "vmem")],
+            (shape((nodes, HID), BF16), shape((nodes, LANES), F32), shape((halo, LANES), F32), shape((hubs, HID + LANES), F32)),
+            [pltpu.VMEM((src_rows * TILES, LANES), F32), pltpu.VMEM((dst_rows * TILES, LANES), F32)]
             + [pltpu.VMEM((dst_rows * TILES, LANES), F32)] * copies1 + [pltpu.VMEM((src_rows * TILES, LANES), F32)] * copies1,
-            compiler_params=params(50),
-        )(d4, s4, w_loc, hub_ids, used, x_t, xh, hx, dy_out, dhh, w_first, bias)
-
-        dz2, dyh, h1h, dz2h = pl.pallas_call(
+            "edges_forward", params())
+
+        dz2, dyh, h1h, dz2h = call(
             functools.partial(middle_kernel, groups),
-            name="middle",
-            out_shape=(shape((nodes, LANES), BF16), shape((hubs, HID), F32), shape((home, HID), BF16), shape((home, LANES), BF16)),
-            in_specs=[VMEM] * 6,
-            out_specs=(VMEM,) * 4,
-            scratch_shapes=[pltpu.VMEM((groups, block, LANES), F32), pltpu.VMEM((groups, home, HID + LANES), F32),
-                            pltpu.VMEM((groups, home, HID), F32), pltpu.VMEM((home, HID), F32)] + sems(3),
-            compiler_params=params(12, 1),
-        )(hz.reshape(groups, block, LANES), hub.reshape(groups, home, HID + LANES), dz, send_lanes, w_second, bias)
-
-        dz1, hz1, hub1, dw2, biases = pl.pallas_call(
+            [(hub.reshape(groups, home, HID + LANES), "vmem"), (hz.reshape(groups, block, LANES), "vmem"), (dz, "vmem"),
+             (bias, "vmem"), (w_second, "vmem"), (send_lanes, "vmem")],
+            (shape((nodes, LANES), BF16), shape((hubs, HID), F32), shape((home, HID), BF16), shape((home, LANES), BF16)),
+            [pltpu.VMEM((groups, block, LANES), F32), pltpu.VMEM((groups, home, HID + LANES), F32),
+             pltpu.VMEM((groups, home, HID), F32), pltpu.VMEM((home, HID), F32)] + sems(3),
+            "middle", params(1))
+
+        dz1, hz1, hub1, dw2, biases = call(
             functools.partial(edges_backward_kernel, copies2, unroll2, feat),
-            name="edges_backward",
-            out_shape=(shape((nodes, HID), F32), shape((TILES, halo, LANES), F32), shape((hubs, HID), F32), shape((HID, LANES), F32), shape((8, LANES), F32)),
-            in_specs=[SMEM] * 5 + [VMEM] * 8,
-            out_specs=(VMEM,) * 5,
-            scratch_shapes=[pltpu.VMEM((dst_rows * TILES, LANES), F32)] + [pltpu.VMEM((src_rows * TILES, LANES), F32)] * copies2,
-            compiler_params=params(44),
-        )(d4, s4, w_loc, hub_ids, used, h1, dz2, dyh, w_second, h1h, dz2h, xh, db2)
+            [(w_second, "vmem"), (h1, "vmem"), (dz2, "vmem"), (dyh, "vmem"), (h1h, "vmem"), (dz2h, "vmem"),
+             (d4, "smem"), (s4, "smem"), (w_loc, "smem"), (used, "smem"), (hub_ids, "smem"), (xh, "vmem"), (db2, "vmem")],
+            (shape((nodes, HID), F32), shape((TILES, halo, LANES), F32), shape((hubs, HID), F32), shape((HID, LANES), F32), shape((8, LANES), F32)),
+            [pltpu.VMEM((dst_rows * TILES, LANES), F32)] + [pltpu.VMEM((src_rows * TILES, LANES), F32)] * copies2,
+            "edges_backward", params())
 
         chips = groups // 2
         part = HID // groups
-        dz1, dw1, dw2, biases = pl.pallas_call(
+        dz1, dz1h, dw1, dw2, biases = call(
             functools.partial(last_kernel, groups),
-            name="last_exchange",
-            out_shape=(shape((nodes, HID), BF16), shape((TILES, groups, 8, LANES), F32), shape((2, chips, part, LANES), F32), shape((8, LANES), F32)),
-            in_specs=[VMEM] * 8,
-            out_specs=(VMEM,) * 4,
-            scratch_shapes=[pltpu.VMEM((TILES, groups, block, LANES), F32), pltpu.VMEM((groups, home, HID), F32),
-                            pltpu.VMEM((groups, 8, LANES), F32), pltpu.VMEM((home, HID), F32), pltpu.VMEM((groups, home, HID), F32),
-                            pltpu.VMEM((chips, part, LANES), F32), pltpu.VMEM((chips, part, LANES), F32), pltpu.VMEM((chips, part, LANES), F32),
-                            pltpu.VMEM((part, LANES), F32),
-                            pltpu.VMEM((TILES, groups * 8, LANES), F32), pltpu.VMEM((TILES, groups, 8, LANES), F32), pltpu.VMEM((TILES, 8, LANES), F32)] + sems(18),
-            compiler_params=params(20, 2),
-        )(hz1.reshape(TILES, groups, block, LANES), hub1.reshape(groups, home, HID), dw2.reshape(2, chips, part, LANES), biases, dz1,
-          x_t, send_lanes, hub_lanes)
-
-        grad_xt, grad_w1, grad_w2, grad_b1, grad_b2 = pl.pallas_call(
+            [(hub1.reshape(groups, home, HID), "vmem"), (hz1.reshape(TILES, groups, block, LANES), "vmem"),
+             (dw2.reshape(2, chips, part, LANES), "vmem"), (biases, "vmem"), (send_lanes, "vmem"), (x_t, "vmem"), (hx, "vmem"), (dz1, "vmem")],
+            (shape((nodes, HID), BF16), shape((groups, home, HID), BF16), shape((TILES, groups, 8, LANES), F32),
+             shape((2, chips, part, LANES), F32), shape((8, LANES), F32)),
+            [pltpu.VMEM((nodes, halo), BF16), pltpu.VMEM((TILES, groups, block, LANES), F32), pltpu.VMEM((groups, home, HID), F32),
+             pltpu.VMEM((groups, 8, LANES), F32), pltpu.VMEM((home, HID), BF16),
+             pltpu.VMEM((chips, part, LANES), F32), pltpu.VMEM((chips, part, LANES), F32), pltpu.VMEM((chips, part, LANES), F32),
+             pltpu.VMEM((part, LANES), F32),
+             pltpu.VMEM((TILES, groups * 8, LANES), F32), pltpu.VMEM((TILES, groups, 8, LANES), F32), pltpu.VMEM((TILES, 8, LANES), F32)] + sems(18),
+            "last_exchange", params(2))
+
+        grad_xt, grad_w1, grad_w2, grad_b1, grad_b2 = call(
             outputs_kernel,
-            name="outputs",
-            out_shape=(shape((feat, nodes), F32), shape((feat, HID), F32), shape((HID, out), F32), shape((1, HID), F32), shape((1, out), F32)),
-            in_specs=[VMEM] * 5,
-            out_specs=(VMEM,) * 5,
-            compiler_params=params(12),
-        )(dz1, w_first, dw1, dw2.reshape(HID, LANES), biases)
+            [(w_first, "vmem"), (hub_lanes, "vmem"), (dz1h.reshape(hubs, HID), "vmem"), (dw1, "vmem"), (dw2.reshape(HID, LANES), "vmem"), (biases, "vmem"), (dz1, "vmem")],
+            (shape((feat, nodes), F32), shape((feat, HID), F32), shape((HID, out), F32), shape((1, HID), F32), shape((1, out), F32)),
+            [], "outputs", params())
         return grad_xt.T, grad_w1, grad_w2, grad_b1.reshape(HID), grad_b2.reshape(out)
 
     return jax.shard_map(

time: 123 us -> 115 us (0.935)
  local copies, waits for them, and re-layouts: 11.2 us -> 0 us
  Pallas kernels: 110 us -> 114 us
    unnamed x40 -> x0, local copies, waits for them, and re-layouts: 11.2 us -> none
    pallas_call x6, Pallas kernels: 110 us -> 114 us  [call(): pl.pallas_call(body, name=name, out_shape=out_shape, in_specs=[HBM] * n_i...]
where the time goes in v3:
time: 115 us
  Pallas kernels  114 us (99%)
    pallas_call x6, Pallas kernels, call(): pl.pallas_call(body, name=name, out_shape=out_shape, in_specs=[HBM] * n_i...  114 us

profile of v3, /device:TPU:0, one launch (start us, length us, event | category | flops | bytes accessed | tf_op | source)
XLA Modules:
  0.0 114.8 jit_solution(13978967690581088926)
XLA Ops:
  0.6 11.3 %gather_rows.1 = (bf16[512,128]{1,0:T(8,128)(2,1)}, f32[64,128]{1,0:T(8,128)}, f32[64,128]{1,0:T(8,128)}, s32[64,128]{1,0:T(8,128)}, s32[64,128]{1,0:T(8,128)}, /*index=5*/s32[8,128]{1,0:T(8,128)}, f32[8,128]{1,0:T(8,128)}) custom-call(s32[1,64]{1,0:T(1,128)} %bitcast.38, bf16[50,2048]{1,0:T(8,128)(2,1)} %bitcast.19, s32[512]{0:T(512)} %refs_2_.2, ...), custom_call_target="tpu_custom_call" | custom-call | tf_op jit(solution)/shard_map/gather_rows/pallas_call | solution.py:60
  11.9 27.1 %edges_forward.1 = (bf16[2048,512]{1,0:T(8,128)(2,1)}, f32[2048,128]{1,0:T(8,128)}, f32[512,128]{1,0:T(8,128)}, f32[64,640]{1,0:T(8,128)}) custom-call(bf16[50,512]{1,0:T(8,128)(2,1)} %refs_0_.5, bf16[50,2048]{1,0:T(8,128)(2,1)} %bitcast.20, f32[2048,121]{1,0:T(8,128)} %refs_2_.3, bf16[512,128]{1,0:T(8,128)(2,1)} %get-tuple-element.35.refs_3_.refs_11_, ...), custom_call_target="tpu_custom_call" | custom-call | tf_op jit(solution)/shard_map/edges_forward/pallas_call | solution.py:60
  39.0 11.4 %middle.1 = (bf16[2048,128]{1,0:T(8,128)(2,1)}, f32[64,512]{1,0:T(8,128)}, bf16[8,512]{1,0:T(8,128)(2,1)}, bf16[8,128]{1,0:T(8,128)(2,1)}) custom-call(f32[8,8,640]{2,1,0:T(8,128)} %bitcast.27, f32[8,64,128]{2,1,0:T(8,128)} %bitcast.25, f32[2048,128]{1,0:T(8,128)} %get-tuple-element.44.refs_2_, f32[1,512]{1,0:T(1,128)} %bitcast.41, ...), custom_call_target="tpu_custom_call" | custom-call | tf_op jit(solution)/shard_map/middle/pallas_call | solution.py:60
  50.4 24.4 %edges_backward.1 = (f32[2048,512]{1,0:T(8,128)}, f32[4,512,128]{2,1,0:T(8,128)}, f32[64,512]{1,0:T(8,128)}, f32[512,128]{1,0:T(8,128)}, f32[8,128]{1,0:T(8,128)}) custom-call(bf16[512,121]{1,0:T(8,128)(2,1)} %refs_0_.4, bf16[2048,512]{1,0:T(8,128)(2,1)} %get-tuple-element.41.refs_1_, bf16[2048,128]{1,0:T(8,128)(2,1)} %get-tuple-element.45.refs_2_, ...), custom_call_target="tpu_custom_call" | custom-call | tf_op jit(solution)/shard_map/edges_backward/pallas_call | solution.py:60
  74.8 35.6 %last_exchange.1 = (bf16[2048,512]{1,0:T(8,128)(2,1)}, bf16[8,8,512]{2,1,0:T(8,128)(2,1)}, f32[4,8,8,128]{3,2,1,0:T(8,128)}, f32[2,4,64,128]{3,2,1,0:T(8,128)}, f32[8,128]{1,0:T(8,128)}) custom-call(f32[8,8,512]{2,1,0:T(8,128)} %bitcast.32, f32[4,8,64,128]{3,2,1,0:T(8,128)} %bitcast.22, f32[2,4,64,128]{3,2,1,0:T(8,128)} %bitcast.24, ...), custom_call_target="tpu_custom_call" | custom-call | tf_op jit(solution)/shard_map/last_exchange/pallas_call | solution.py:60
  110.4 4.2 %outputs.1 = (f32[50,2048]{1,0:T(8,128)}, f32[50,512]{1,0:T(8,128)}, f32[512,121]{1,0:T(8,128)}, f32[1,512]{1,0:T(1,128)}, f32[1,121]{1,0:T(1,128)}) custom-call(bf16[50,512]{1,0:T(8,128)(2,1)} %refs_0_.5, s32[1,64]{1,0:T(1,128)} %bitcast.39, bf16[64,512]{1,0:T(8,128)(2,1)} %bitcast.33, f32[4,8,8,128]{3,2,1,0:T(8,128)} %get-tuple-element.56.refs_3_, ...), custom_call_target="tpu_custom_call" | custom-call | tf_op jit(solution)/shard_map/outputs/pallas_call | solution.py:60

commit v4 on v3

--- a/solution.py
+++ b/solution.py
@@ -11,6 +11,7 @@
 CONTRACT_ROWS = (((0,), (0,)), ((), ()))
 CONTRACT_COLS = (((1,), (1,)), ((), ()))
 LANES = 128
+WAYS = 4
 HID = 512
 TILES = HID // LANES
 CHUNK = 256
@@ -96,6 +97,10 @@
     return jnp.concatenate([value, jnp.zeros((rows, LANES - cols), value.dtype)], axis=1)
 
 
+def hub_block(device, groups):
+    return lax.rem(device, 2) * (groups // 2) + device // 2
+
+
 def greet(groups, me):
     barrier = pltpu.get_barrier_semaphore()
     for step in range(1, groups):
@@ -122,8 +127,8 @@
 
 
 def gather_kernel(groups, hubrow, xt, send_idx, hub_ids, dh, dst, src, w,
-                  xh_ref, hx_ref, dhh_ref, d4_ref, s4_ref, used_ref, db2_ref,
-                  x32, xg, hxg, dhg, xs, xr, dhr, ssem, rsem, flush):
+                  xh_ref, hx_ref, dhh_ref, used_ref, db2_ref, wide_ref, *rest, flush):
+    lists, (x32, xg, hxg, dhg, xs, xr, dhr, ssem, rsem) = rest[:3 * WAYS], rest[3 * WAYS:]
     me = lax.axis_index("graph")
     barrier = greet(groups, me)
     feat, nodes = xt.ref.shape
@@ -173,15 +178,36 @@
         peer = lax.rem(me + step, groups)
         copies.append(send(xs.at[peer], xr.at[me], ssem.at[0, step], rsem.at[0, step], peer))
         copies.append(send(dhg, dhr.at[me], ssem.at[1, step], rsem.at[1, step], peer))
-    d4_ref[...] = dst.get()[...] * TILES
-    s4_ref[...] = src.get()[...] * TILES
-    used = jnp.where(w.get()[...] > 0.0, 1.0, 0.0).sum(axis=0, keepdims=True).sum(axis=1, keepdims=True)
+    dst_ref, src_ref, w_ref = dst.get(), src.get(), w.get()
+    blocks = w_ref.shape[0]
+    for q in range(WAYS):
+        part = pl.ds(q, blocks // WAYS, stride=WAYS)
+        lists[q][...] = dst_ref[part, :] * TILES
+        lists[WAYS + q][...] = src_ref[part, :] * TILES
+        lists[2 * WAYS + q][...] = w_ref[part, :]
+    flush(*lists)
+    diagonal = iota((LANES, LANES), 0) == iota((LANES, LANES), 1)
+    ones = jnp.ones((LANES, LANES), BF16)
+
+    def widen(i, carry):
+        for q in range(WAYS):
+            row = lists[2 * WAYS + q][pl.ds(i, 1), :]
+            spread = jnp.zeros((LANES, LANES), F32)
+            for piece in reversed(split3(row)):
+                column = jnp.where(diagonal, jnp.broadcast_to(piece.astype(F32), (LANES, LANES)), 0.0).astype(BF16)
+                spread = spread + dot(column, ones)
+            wide_ref[pl.ds(pl.multiple_of((q * (blocks // WAYS) + i) * LANES, LANES), LANES), :] = spread
+        return carry
+
+    lax.fori_loop(0, blocks // WAYS, widen, 0)
+    flush(wide_ref)
+    used = jnp.where(w_ref[...] > 0.0, 1.0, 0.0).sum(axis=0, keepdims=True).sum(axis=1, keepdims=True)
     used_ref[...] = jnp.broadcast_to(used, used_ref.shape).astype(I32)
     total = jnp.zeros((8, dh_ref.shape[1]), F32)
     for row in range(0, nodes, CHUNK):
         total = total + dh_ref[pl.ds(row, CHUNK), :].reshape(CHUNK // 8, 8, dh_ref.shape[1]).sum(axis=0)
     db2_ref[...] = jnp.broadcast_to(pad_lanes(total.sum(axis=0, keepdims=True)), db2_ref.shape)
-    flush(d4_ref, s4_ref, used_ref, db2_ref)
+    flush(used_ref, db2_ref)
     xr[me] = xs[me]
     dhr[me] = dhg[...]
     for copy in copies:
@@ -202,6 +228,10 @@
     return own, pl.multiple_of(jnp.clip(row, 0, nodes - 1) * TILES, TILES)
 
 
+def trips(used_ref, unroll):
+    return (used_ref[0, 0] + (WAYS * LANES - 1)) // (WAYS * LANES) * (LANES // unroll)
+
+
 def strided(first, rows):
     return pl.ds(first, rows, stride=TILES)
 
@@ -213,8 +243,8 @@
     return value
 
 
-def edges_forward_kernel(copies, unroll, w1, xt, dh, xh, hx, dhh, d4, s4, w, used, hub_ids, b1,
-                         h1_ref, dz_ref, hz_ref, hub_out, zt, dt, *accs, flush):
+def edges_forward_kernel(copies, unroll, w1, xt, dh, xh, hx, dhh, used, hub_ids, b1, *rest, flush):
+    lists, (h1_ref, dz_ref, hz_ref, hub_out, zt, dt), accs = rest[:3 * WAYS], rest[3 * WAYS:3 * WAYS + 6], rest[3 * WAYS + 6:]
     ya, da = accs[:copies], accs[copies:]
     me = lax.axis_index("graph")
     feat, nodes = xt.ref.shape
@@ -239,24 +269,23 @@
         put_rows(nodes + row, dot(xh_ref[pl.ds(row, CHUNK), pl.ds(0, feat)], w1))
     put_rows(nodes + halo, dot(hx_ref[:, pl.ds(0, feat)].astype(BF16), w1))
     dt[strided(nodes * TILES, hubs), :] = dhh.get()[...]
-    d4_ref, s4_ref, used_ref, w_ref, hub_ref, b1_ref = d4.get(), s4.get(), used.get(), w.get(), hub_ids.get(), b1.get()
+    used_ref, hub_ref, b1_ref = used.get(), hub_ids.get(), b1.get()
+    lists = [item.get() for item in lists]
 
     def step(i, carry):
-        for u0 in range(0, unroll, copies):
-            new = []
-            for u in range(min(copies, unroll - u0)):
-                j = i * unroll + u0 + u
-                s4 = pl.multiple_of(s4_ref[j], TILES)
-                d4 = pl.multiple_of(d4_ref[j], TILES)
-                w = w_ref[j]
-                new.append((s4, d4, ya[u][pl.ds(d4, TILES), :] + w * zt[pl.ds(s4, TILES), :],
-                            da[u][pl.ds(s4, 1), :] + w * dt[pl.ds(d4, 1), :]))
-            for u, (s4, d4, y_new, z_new) in enumerate(new):
-                ya[u][pl.ds(d4, TILES), :] = y_new
-                da[u][pl.ds(s4, 1), :] = z_new
-        return carry
-
-    lax.fori_loop(0, (used_ref[0, 0] + (unroll - 1)) // unroll, step, 0)
+        for n in range(unroll * WAYS):
+            q, u = n % WAYS, n % copies
+            j = i * unroll + n // WAYS
+            d4 = pl.multiple_of(lists[q][j], TILES)
+            s4 = pl.multiple_of(lists[WAYS + q][j], TILES)
+            w = lists[2 * WAYS + q][j]
+            y_new = ya[u][pl.ds(d4, TILES), :] + w * zt[pl.ds(s4, TILES), :]
+            z_new = da[u][pl.ds(s4, 1), :] + w * dt[pl.ds(d4, 1), :]
+            ya[u][pl.ds(d4, TILES), :] = y_new
+            da[u][pl.ds(s4, 1), :] = z_new
+        return carry
+
+    lax.fori_loop(0, trips(used_ref, unroll), step, 0)
 
     def fold(k, carry):
         own, row = hub_position(hub_ref, k, base, nodes)
@@ -301,13 +330,14 @@
     block = hz.ref.shape[1]
     halo = groups * block
     hub_ref, hz_ref = hub.get(), hz.get()
-    hubr[me] = hub_ref[me]
+    own = hub_block(me, groups)
+    hubr[me] = hub_ref[own]
     hzr[me] = jnp.zeros(hzr.shape[1:], F32)
     pl.semaphore_wait(barrier, groups - 1)
     hub_copies, halo_copies, back = [], [], []
     for step in range(1, groups):
         peer = lax.rem(me + step, groups)
-        hub_copies.append(send(hub_ref.at[peer], hubr.at[me], ssem.at[0, step], rsem.at[0, step], peer))
+        hub_copies.append(send(hub_ref.at[hub_block(peer, groups)], hubr.at[me], ssem.at[0, step], rsem.at[0, step], peer))
     for step in range(1, groups):
         peer = lax.rem(me + step, groups)
         halo_copies.append(send(hz_ref.at[peer], hzr.at[me], ssem.at[1, step], rsem.at[1, step], peer))
@@ -324,8 +354,8 @@
     dys[...] = jnp.where(pre > 0, dot(dz2h[:, :out], w2_ref[...], CONTRACT_COLS), 0.0)
     for step in range(1, groups):
         peer = lax.rem(me + step, groups)
-        back.append(send(dys, dyr.at[me], ssem.at[2, step], rsem.at[2, step], peer))
-    dyr[me] = dys[...]
+        back.append(send(dys, dyr.at[own], ssem.at[2, step], rsem.at[2, step], peer))
+    dyr[own] = dys[...]
     for copy in halo_copies:
         copy.wait()
     pieces = split3(hzr[...].reshape(halo, LANES))
@@ -342,8 +372,9 @@
         dyh_ref[pl.ds(q * home, home), :] = dyr[q]
 
 
-def edges_backward_kernel(copies, unroll, feat, w2, h1, dz2, dyh, h1h, dz2h, d4, s4, w, used, hub_ids, xh, db2,
-                          dz1_ref, hz_ref, hub_out, dw2_ref, bias_ref, yt, *za, flush):
+def edges_backward_kernel(copies, unroll, feat, groups, w2, h1, dz2, dyh, h1h, dz2h, used, hub_ids, xh, db2, wide, *rest, flush):
+    lists, rest = rest[:2 * WAYS], rest[2 * WAYS:]
+    (dz1_ref, hz_ref, hub_out, dw2_ref, bias_ref, yt), za = rest[:6], rest[6:]
     me = lax.axis_index("graph")
     nodes = h1.ref.shape[0]
     out = w2.ref.shape[1]
@@ -353,7 +384,7 @@
     for acc in za:
         acc[...] = jnp.zeros_like(acc)
     w2, h1_ref, dz2_ref, dyh_ref, h1h_ref, dz2h_ref = w2.get()[...], h1.get(), dz2.get(), dyh.get(), h1h.get(), dz2h.get()
-    mine = dyh_ref[pl.ds(pl.multiple_of(me * home, 8), home), :]
+    mine = dyh_ref[pl.ds(pl.multiple_of(hub_block(me, groups) * home, 8), home), :]
     db1 = mine
     for row in range(0, nodes, CHUNK):
         rows = pl.ds(row, CHUNK)
@@ -369,7 +400,9 @@
         yt[strided(nodes * TILES + c, hubs), :] = dyh_ref[:, pl.ds(c * LANES, LANES)]
     dw2_ref[...] = dot(h1_ref[...], dz2_ref[...], CONTRACT_ROWS) + dot(h1h_ref[...], dz2h_ref[...], CONTRACT_ROWS)
     flush(dw2_ref, bias_ref)
-    d4_ref, s4_ref, used_ref, w_ref, hub_ref, xh_ref = d4.get(), s4.get(), used.get(), w.get(), hub_ids.get(), xh.get()
+    used_ref, hub_ref, xh_ref, wide_ref = used.get(), hub_ids.get(), xh.get(), wide.get()
+    lists = [item.get() for item in lists]
+    length = wide_ref.shape[0] // WAYS
 
     def place(k, carry):
         own, row = hub_position(hub_ref, k, base, nodes)
@@ -380,19 +413,16 @@
     lax.fori_loop(0, hubs, place, 0)
 
     def step(i, carry):
-        for u0 in range(0, unroll, copies):
-            new = []
-            for u in range(copies):
-                j = i * unroll + u0 + u
-                s4 = pl.multiple_of(s4_ref[j], TILES)
-                d4 = pl.multiple_of(d4_ref[j], TILES)
-                w = w_ref[j]
-                new.append((s4, za[u][pl.ds(s4, TILES), :] + w * yt[pl.ds(d4, TILES), :]))
-            for u, (s4, z_new) in enumerate(new):
-                za[u][pl.ds(s4, TILES), :] = z_new
-        return carry
-
-    lax.fori_loop(0, (used_ref[0, 0] + (unroll - 1)) // unroll, step, 0)
+        for n in range(unroll * WAYS):
+            q, u = n % WAYS, n % copies
+            j = pl.multiple_of(i * unroll, unroll) + n // WAYS
+            d4 = pl.multiple_of(lists[q][j], TILES)
+            s4 = pl.multiple_of(lists[WAYS + q][j], TILES)
+            w = wide_ref[pl.ds(q * length + j, 1), :]
+            za[u][pl.ds(s4, TILES), :] = za[u][pl.ds(s4, TILES), :] + w * yt[pl.ds(d4, TILES), :]
+        return carry
+
+    lax.fori_loop(0, trips(used_ref, unroll), step, 0)
 
     def fold(k, carry):
         own, row = hub_position(hub_ref, k, base, nodes)
@@ -418,68 +448,74 @@
         hz_ref[c] = jnp.where(tag > 0.0, 0.0, hz)
 
 
-def last_kernel(groups, hub, hz, dw2, bias, sendrow, xt, hx, dz1,
-                dz_out, dha, dw1a, dw2a, bias_out,
-                onehot, hzr, hubr, biasr, dhs, dw2p, dw2h, dw2r, dw2s, dw1s, dw1r, dw1t, ssem, rsem, flush):
+def last_kernel(groups, hub, hz, dw2, bias, sendrow, xt, hx, dz1, w1, hubrow,
+                gxt_ref, dw1a, dw2a, bias_out,
+                dz_out, onehot, hzr, hubp, hubh, hubr, biasp, biash, biasr, dhs, dha, dw2p, dw2h, dw2r, dw2s, dw1s, dw1r, dw1t, ssem, rsem, flush):
     me = lax.axis_index("graph")
     barrier = greet(groups, me)
     feat, nodes = xt.ref.shape
-    home = hub.ref.shape[1]
+    chips, home = hub.ref.shape[1:3]
+    hubs = groups * home
     block = hz.ref.shape[2]
     halo = groups * block
+    base = me * nodes
+    core, chip = lax.rem(me, 2), me // 2
+    partner = me + 1 - 2 * core
+    own = hub_block(me, groups)
+    peers = [lax.rem(me + step, groups) for step in range(1, groups)]
+    others = [lax.rem(me + 2 * step, groups) for step in range(1, chips)]
     hub_ref, hz_ref, dw2_ref, bias_ref = hub.get(), hz.get(), dw2.get(), bias.get()
-    core = lax.rem(me, 2)
-    partner = me + 1 - 2 * core
-    chip = me // 2
-    chips = groups // 2
-    part = dw2_ref.shape[2]
-    hubr[me] = hub_ref[me]
-    biasr[me] = bias_ref[...]
+    pl.semaphore_wait(barrier, groups - 1)
+
+    def to(devices, slot, src, dst):
+        return [send(src(peer), dst, ssem.at[slot, i], rsem.at[slot, i], peer) for i, peer in enumerate(devices)]
+
+    def wait(pending):
+        for copy in pending:
+            copy.wait()
+
+    pair_copies = (to([partner], 0, lambda p: hub_ref.at[1 - core], hubp) + to([partner], 1, lambda p: dw2_ref.at[1 - core], dw2p)
+                   + to([partner], 2, lambda p: bias_ref, biasp))
+    halo_copies = [to(peers, 9, lambda p: hz_ref.at[0, p], hzr.at[0, me])]
+    sendrow = sendrow.get()[...]
+    for row in range(0, nodes, CHUNK):
+        onehot[pl.ds(row, CHUNK), :] = (iota((CHUNK, halo), 0) + row == sendrow).astype(BF16)
     for c in range(TILES):
         hzr[c, me] = jnp.zeros((block, LANES), F32)
         dw1s[c] = jnp.zeros(dw1s.shape[1:], F32)
-    pl.semaphore_wait(barrier, groups - 1)
-    peers = [lax.rem(me + step, groups) for step in range(1, groups)]
-    others = [lax.rem(me + 2 * step, groups) for step in range(1, chips)]
-
-    def to(devices, slot, src, dst):
-        return [send(src(peer), dst, ssem.at[slot, i], rsem.at[slot, i], peer) for i, peer in enumerate(devices)]
-
-    def wait(pending):
-        for copy in pending:
-            copy.wait()
-
-    hub_copies = to(peers, 0, lambda p: hub_ref.at[p], hubr.at[me])
-    pair_copies = to([partner], 1, lambda p: dw2_ref.at[1 - core], dw2p)
-    halo_copies = [to(peers, 5 + c, lambda p: hz_ref.at[c, p], hzr.at[c, me]) for c in range(2)]
+    wait(pair_copies)
+    hubh[...] = hub_ref[core] + hubp[...]
+    dw2h[...] = dw2_ref[core] + dw2p[...]
+    biash[...] = bias_ref[...] + biasp[...]
+    hubr[chip] = hubh[chip]
+    dw2r[chip] = dw2h[chip]
+    biasr[chip] = biash[...]
+    hub_copies = to(others, 3, lambda p: hubh.at[p // 2], hubr.at[chip])
+    dw2_copies = to(others, 4, lambda p: dw2h.at[p // 2], dw2r.at[chip])
+    bias_copies = to(others, 5, lambda p: biash, biasr.at[chip])
+    halo_copies += [to(peers, 9 + c, lambda p: hz_ref.at[c, p], hzr.at[c, me]) for c in range(1, TILES)]
+
+    def total_over(ref, count):
+        total = ref[0]
+        for q in range(1, count):
+            total = total + ref[q]
+        return total
+
+    xt_ref, dz1_ref, hx_ref, w1, hubrow = xt.get(), dz1.get(), hx.get(), w1.get()[...], hubrow.get()[...]
     wait(hub_copies)
-    total = hubr[0]
-    for q in range(1, groups):
-        total = total + hubr[q]
-    dz1h = total.astype(BF16)
+    dz1h = total_over(hubr, chips).astype(BF16)
     dhs[...] = dz1h
-    back_copies = to(peers, 3, lambda p: dhs, dha.at[me])
-    dha[me] = dhs[...]
-    wait(pair_copies)
-    dw2h[...] = dw2_ref[core] + dw2p[...]
-    dw2r[chip] = dw2h[chip]
-    dw2_copies = to(others, 2, lambda p: dw2h.at[p // 2], dw2r.at[chip])
-    halo_copies += [to(peers, 5 + c, lambda p: hz_ref.at[c, p], hzr.at[c, me]) for c in range(2, TILES)]
-    bias_copies = to(peers, 4, lambda p: bias_ref, biasr.at[me])
-    hx_mine = hx.get()[pl.ds(pl.multiple_of(me * home, 8), home), :].astype(BF16)
+    back_copies = to(peers, 6, lambda p: dhs, dha.at[own])
+    dha[own] = dz1h
+    hx_mine = hx_ref[pl.ds(pl.multiple_of(own * home, 8), home), :].astype(BF16)
     dw1h = dot(hx_mine[:, :feat], dz1h, CONTRACT_ROWS)
-    sendrow, xt_ref, dz1_ref = sendrow.get()[...], xt.get(), dz1.get()
-    for row in range(0, nodes, CHUNK):
-        onehot[pl.ds(row, CHUNK), :] = (iota((CHUNK, halo), 0) + row == sendrow).astype(BF16)
     rs_copies, ag_copies = [None] * TILES, [None] * TILES
 
     def spread(c):
         wait(rs_copies[c])
-        total = dw1r[c, 0]
-        for q in range(1, groups):
-            total = total + dw1r[c, q]
+        total = total_over(dw1r.at[c], groups)
         dw1t[c] = total
-        ag_copies[c] = to(peers, 13 + c, lambda p: dw1t.at[c], dw1a.at[c, me])
+        ag_copies[c] = to(peers, 17 + c, lambda p: dw1t.at[c], dw1a.at[c, me])
         dw1a[c, me] = total
 
     for c in range(TILES):
@@ -496,45 +532,44 @@
 
         lax.fori_loop(0, nodes // CHUNK, rows_step, 0)
         dw1s[c, pl.ds(0, feat), :] = dot(xt_ref[...], dz_out[:, cols]) + dw1h[:, c * LANES:(c + 1) * LANES]
-        rs_copies[c] = to(peers, 9 + c, lambda p: dw1s.at[c, pl.ds(pl.multiple_of(p * 8, 8), 8)], dw1r.at[c, me])
+        rs_copies[c] = to(peers, 13 + c, lambda p: dw1s.at[c, pl.ds(pl.multiple_of(p * 8, 8), 8)], dw1r.at[c, me])
         dw1r[c, me] = dw1s[c, pl.ds(pl.multiple_of(me * 8, 8), 8), :]
         if c == 0:
             wait(dw2_copies)
-            total = dw2r[0]
-            for q in range(1, chips):
-                total = total + dw2r[q]
+            total = total_over(dw2r, chips)
             dw2s[...] = total
-            dw2_back = to(peers, 17, lambda p: dw2s, dw2a.at[core, chip])
+            dw2_back = to(others, 7, lambda p: dw2s, dw2a.at[core, chip])
             dw2a[core, chip] = total
         if c > 0:
             spread(c - 1)
-    flush(dz_out)
-    wait(bias_copies)
-    total = biasr[0]
-    for q in range(1, groups):
-        total = total + biasr[q]
-    bias_out[...] = total
-    spread(TILES - 1)
-    wait(dw2_back)
+        if c == 2:
+            wait(dw2_back)
+            dw2_pair = to([partner], 8, lambda p: dw2a.at[core], dw2a.at[core])
     wait(back_copies)
-    for c in range(TILES):
-        wait(ag_copies[c])
-
-
-def outputs_kernel(w1, hubrow, dzh, dw1, dw2, bias, dz, gxt_ref, gw1_ref, gw2_ref, gb1_ref, gb2_ref, flush):
-    nodes = dz.ref.shape[0]
-    hubs = dzh.ref.shape[0]
-    feat = w1.ref.shape[0]
-    out = gw2_ref.shape[1]
-    base = lax.axis_index("graph") * nodes
-    w1, hubrow, dzh_ref, dz_ref = w1.get()[...], hubrow.get()[...], dzh.get(), dz.get()
+    hub_rows = dha[...].reshape(hubs, HID)
     for row in range(0, nodes, 2 * CHUNK):
         rows = pl.ds(row, 2 * CHUNK)
         owned = (iota((2 * CHUNK, hubs), 0) + (base + row) == hubrow).astype(BF16)
-        dz = (dz_ref[rows, :].astype(F32) + dot(owned, dzh_ref[...])).astype(BF16)
+        dz = (dz_out[rows, :].astype(F32) + dot(owned, hub_rows)).astype(BF16)
         gxt_ref[:, rows] = dot(w1, dz, CONTRACT_COLS)
     flush(gxt_ref)
-    dw1_ref, dw2_ref, bias_ref = dw1.get(), dw2.get(), bias.get()
+    wait(bias_copies)
+    bias_out[...] = total_over(biasr, chips)
+    flush(bias_out)
+    spread(TILES - 1)
+    wait(dw2_pair)
+    flush(dw2a)
+    for c in range(TILES):
+        wait(ag_copies[c])
+
+
+def outputs_kernel(gxt, dw2, bias, dw1, gxt_ref, gw1_ref, gw2_ref, gb1_ref, gb2_ref, flush):
+    feat, out = gw1_ref.shape[0], gw2_ref.shape[1]
+    gxt_ref[...] = gxt.get()[...]
+    flush(gxt_ref)
+    gw2_ref[...] = dw2.get()[:, pl.ds(0, out)]
+    flush(gw2_ref)
+    bias_ref, dw1_ref = bias.get(), dw1.get()
     for c in range(TILES):
         cols = pl.ds(c * LANES, LANES)
         for q in range(dw1_ref.shape[1]):
@@ -542,7 +577,6 @@
             if rows > 0:
                 gw1_ref[pl.ds(q * 8, rows), cols] = dw1_ref[c, q, pl.ds(0, rows), :]
         gb1_ref[:, cols] = bias_ref[pl.ds(c, 1), :]
-    gw2_ref[...] = dw2_ref[:, pl.ds(0, out)]
     gb2_ref[...] = bias_ref[pl.ds(TILES, 1), pl.ds(0, out)]
 
 
@@ -557,8 +591,8 @@
     part_spec = P("data")
     part_rows = P("data", None)
     replicated = P()
-    copies1, unroll1 = 3, 64
-    copies2, unroll2 = 4, 64
+    copies1, unroll1 = 3, 16
+    copies2, unroll2 = 5, 16
 
     def params(collective_id=None):
         if collective_id is None:
@@ -579,25 +613,26 @@
         bias = b_first.reshape(1, HID)
         sems = lambda n: [pltpu.SemaphoreType.DMA((n, groups)), pltpu.SemaphoreType.DMA((n, groups))]
         table = lambda a: a.reshape(edges // LANES, LANES)
-        rows = (edges // LANES, LANES)
+        part_list = (edges // LANES // WAYS, LANES)
         packed = (block + hubs) // 2
 
-        xh, hx, dhh, d4, s4, used, db2 = call(
+        xh, hx, dhh, used, db2, wide, *lists = call(
             functools.partial(gather_kernel, groups),
             [(hub_lanes, "vmem"), (x_t, "vmem"), (send_loc, "smem"), (hub_ids, "smem"), (dy_out, "vmem"),
              (table(dst_loc), "vmem"), (table(src_loc), "vmem"), (table(w_loc), "vmem")],
             (shape((halo, LANES), BF16), shape((hubs, LANES), F32), shape((hubs, LANES), F32),
-             shape(rows, I32), shape(rows, I32), shape((8, LANES), I32), shape((8, LANES), F32)),
+             shape((8, LANES), I32), shape((8, LANES), F32), shape((edges, LANES), F32))
+            + (shape(part_list, I32),) * (2 * WAYS) + (shape(part_list, F32),) * WAYS,
             [pltpu.VMEM((nodes, LANES), F32), pltpu.VMEM((halo, LANES), F32), pltpu.VMEM((hubs, LANES), F32),
              pltpu.VMEM((hubs, LANES), F32), pltpu.VMEM((groups, packed, LANES), BF16),
              pltpu.VMEM((groups, packed, LANES), BF16), pltpu.VMEM((groups, hubs, LANES), F32)] + sems(2),
             "gather_rows", params(0))
-        d4, s4 = d4.reshape(edges), s4.reshape(edges)
+        lists = [(item.reshape(edges // WAYS), "smem") for item in lists]
 
         h1, dz, hz, hub = call(
             functools.partial(edges_forward_kernel, copies1, unroll1),
             [(w_first, "vmem"), (x_t, "vmem"), (dy_out, "vmem"), (xh, "vmem"), (hx, "vmem"), (dhh, "vmem"),
-             (d4, "smem"), (s4, "smem"), (w_loc, "smem"), (used, "smem"), (hub_ids, "smem"), (bias, "vmem")],
+             (used, "smem"), (hub_ids, "smem"), (bias, "vmem")] + lists,
             (shape((nodes, HID), BF16), shape((nodes, LANES), F32), shape((halo, LANES), F32), shape((hubs, HID + LANES), F32)),
             [pltpu.VMEM((src_rows * TILES, LANES), F32), pltpu.VMEM((dst_rows * TILES, LANES), F32)]
             + [pltpu.VMEM((dst_rows * TILES, LANES), F32)] * copies1 + [pltpu.VMEM((src_rows * TILES, LANES), F32)] * copies1,
@@ -613,31 +648,31 @@
             "middle", params(1))
 
         dz1, hz1, hub1, dw2, biases = call(
-            functools.partial(edges_backward_kernel, copies2, unroll2, feat),
+            functools.partial(edges_backward_kernel, copies2, unroll2, feat, groups),
             [(w_second, "vmem"), (h1, "vmem"), (dz2, "vmem"), (dyh, "vmem"), (h1h, "vmem"), (dz2h, "vmem"),
-             (d4, "smem"), (s4, "smem"), (w_loc, "smem"), (used, "smem"), (hub_ids, "smem"), (xh, "vmem"), (db2, "vmem")],
+             (used, "smem"), (hub_ids, "smem"), (xh, "vmem"), (db2, "vmem"), (wide, "vmem")] + lists[:2 * WAYS],
             (shape((nodes, HID), F32), shape((TILES, halo, LANES), F32), shape((hubs, HID), F32), shape((HID, LANES), F32), shape((8, LANES), F32)),
             [pltpu.VMEM((dst_rows * TILES, LANES), F32)] + [pltpu.VMEM((src_rows * TILES, LANES), F32)] * copies2,
             "edges_backward", params())
 
         chips = groups // 2
         part = HID // groups
-        dz1, dz1h, dw1, dw2, biases = call(
+        grad_xt, dw1, dw2, biases = call(
             functools.partial(last_kernel, groups),
-            [(hub1.reshape(groups, home, HID), "vmem"), (hz1.reshape(TILES, groups, block, LANES), "vmem"),
-             (dw2.reshape(2, chips, part, LANES), "vmem"), (biases, "vmem"), (send_lanes, "vmem"), (x_t, "vmem"), (hx, "vmem"), (dz1, "vmem")],
-            (shape((nodes, HID), BF16), shape((groups, home, HID), BF16), shape((TILES, groups, 8, LANES), F32),
-             shape((2, chips, part, LANES), F32), shape((8, LANES), F32)),
-            [pltpu.VMEM((nodes, halo), BF16), pltpu.VMEM((TILES, groups, block, LANES), F32), pltpu.VMEM((groups, home, HID), F32),
-             pltpu.VMEM((groups, 8, LANES), F32), pltpu.VMEM((home, HID), BF16),
-             pltpu.VMEM((chips, part, LANES), F32), pltpu.VMEM((chips, part, LANES), F32), pltpu.VMEM((chips, part, LANES), F32),
-             pltpu.VMEM((part, LANES), F32),
-             pltpu.VMEM((TILES, groups * 8, LANES), F32), pltpu.VMEM((TILES, groups, 8, LANES), F32), pltpu.VMEM((TILES, 8, LANES), F32)] + sems(18),
+            [(hub1.reshape(2, chips, home, HID), "vmem"), (hz1.reshape(TILES, groups, block, LANES), "vmem"),
+             (dw2.reshape(2, chips, part, LANES), "vmem"), (biases, "vmem"), (send_lanes, "vmem"), (x_t, "vmem"), (hx, "vmem"),
+             (dz1, "vmem"), (w_first, "vmem"), (hub_lanes, "vmem")],
+            (shape((feat, nodes), F32), shape((TILES, groups, 8, LANES), F32), shape((2, chips, part, LANES), F32), shape((8, LANES), F32)),
+            [pltpu.VMEM((nodes, HID), BF16), pltpu.VMEM((nodes, halo), BF16), pltpu.VMEM((TILES, groups, block, LANES), F32)]
+            + [pltpu.VMEM((chips, home, HID), F32)] * 3 + [pltpu.VMEM((8, LANES), F32)] * 2 + [pltpu.VMEM((chips, 8, LANES), F32)]
+            + [pltpu.VMEM((home, HID), BF16), pltpu.VMEM((groups, home, HID), BF16)]
+            + [pltpu.VMEM((chips, part, LANES), F32)] * 3 + [pltpu.VMEM((part, LANES), F32)]
+            + [pltpu.VMEM((TILES, groups * 8, LANES), F32), pltpu.VMEM((TILES, groups, 8, LANES), F32), pltpu.VMEM((TILES, 8, LANES), F32)] + sems(21),
             "last_exchange", params(2))
 
         grad_xt, grad_w1, grad_w2, grad_b1, grad_b2 = call(
             outputs_kernel,
-            [(w_first, "vmem"), (hub_lanes, "vmem"), (dz1h.reshape(hubs, HID), "vmem"), (dw1, "vmem"), (dw2.reshape(HID, LANES), "vmem"), (biases, "vmem"), (dz1, "vmem")],
+            [(grad_xt, "vmem"), (dw2.reshape(HID, LANES), "vmem"), (biases, "vmem"), (dw1, "vmem")],
             (shape((feat, nodes), F32), shape((feat, HID), F32), shape((HID, out), F32), shape((1, HID), F32), shape((1, out), F32)),
             [], "outputs", params())
         return grad_xt.T, grad_w1, grad_w2, grad_b1.reshape(HID), grad_b2.reshape(out)

time: 115 us -> 108 us (0.939)
  Pallas kernels: 114 us -> 107 us
    pallas_call x6, Pallas kernels: 114 us -> 107 us  [call(): pl.pallas_call(body, name=name, out_shape=out_shape, in_specs=[HBM] * n_i...]
where the time goes in v4:
time: 108 us
  Pallas kernels  107 us (99%)
    pallas_call x6, Pallas kernels, call(): pl.pallas_call(body, name=name, out_shape=out_shape, in_specs=[HBM] * n_i...  107 us

profile of v4, /device:TPU:0, one launch (start us, length us, event | category | flops | bytes accessed | tf_op | source)
XLA Modules:
  0.0 108.0 jit_solution(7729123686434344116)
XLA Ops:
  0.6 11.4 %gather_rows.1 = (bf16[512,128]{1,0:T(8,128)(2,1)}, f32[64,128]{1,0:T(8,128)}, f32[64,128]{1,0:T(8,128)}, s32[8,128]{1,0:T(8,128)}, f32[8,128]{1,0:T(8,128)}, /*...) custom-call(s32[1,64]{1,0:T(1,128)} %bitcast.58, ...), custom_call_target="tpu_custom_call" | custom-call | tf_op jit(solution)/shard_map/gather_rows/pallas_call | solution.py:61
  12.0 25.7 %edges_forward.1 = (bf16[2048,512]{1,0:T(8,128)(2,1)}, f32[2048,128]{1,0:T(8,128)}, f32[512,128]{1,0:T(8,128)}, f32[64,640]{1,0:T(8,128)}) custom-call(bf16[50,512]{1,0:T(8,128)(2,1)} %refs_8_.1, bf16[50,2048]{1,0:T(8,128)(2,1)} %bitcast.29, f32[2048,121]{1,0:T(8,128)} %refs_2_.3, bf16[512,128]{1,0:T(8,128)(2,1)} %get-tuple-element.45.refs_3_.refs_8_, ...), custom_call_target="tpu_custom_call" | custom-call | tf_op jit(solution)/shard_map/edges_forward/pallas_call | solution.py:61
  37.8 11.4 %middle.1 = (bf16[2048,128]{1,0:T(8,128)(2,1)}, f32[64,512]{1,0:T(8,128)}, bf16[8,512]{1,0:T(8,128)(2,1)}, bf16[8,128]{1,0:T(8,128)(2,1)}) custom-call(f32[8,8,640]{2,1,0:T(8,128)} %bitcast.35, f32[8,64,128]{2,1,0:T(8,128)} %bitcast.33, f32[2048,128]{1,0:T(8,128)} %get-tuple-element.64.refs_2_, f32[1,512]{1,0:T(1,128)} %bitcast.65, ...), custom_call_target="tpu_custom_call" | custom-call | tf_op jit(solution)/shard_map/middle/pallas_call | solution.py:61
  49.2 21.8 %edges_backward.1 = (f32[2048,512]{1,0:T(8,128)}, f32[4,512,128]{2,1,0:T(8,128)}, f32[64,512]{1,0:T(8,128)}, f32[512,128]{1,0:T(8,128)}, f32[8,128]{1,0:T(8,128)}) custom-call(bf16[512,121]{1,0:T(8,128)(2,1)} %refs_0_.3, bf16[2048,512]{1,0:T(8,128)(2,1)} %get-tuple-element.61.refs_1_, bf16[2048,128]{1,0:T(8,128)(2,1)} %get-tuple-element.65.refs_2_, ...), custom_call_target="tpu_custom_call" | custom-call | tf_op jit(solution)/shard_map/edges_backward/pallas_call | solution.py:61
  71.0 34.9 %last_exchange.1 = (f32[50,2048]{1,0:T(8,128)}, f32[4,8,8,128]{3,2,1,0:T(8,128)}, f32[2,4,64,128]{3,2,1,0:T(8,128)}, f32[8,128]{1,0:T(8,128)}) custom-call(f32[2,4,8,512]{3,2,1,0:T(8,128)} %bitcast.36, f32[4,8,64,128]{3,2,1,0:T(8,128)} %bitcast.31, f32[2,4,64,128]{3,2,1,0:T(8,128)} %bitcast.32, f32[8,128]{1,0:T(8,128)} %get-tuple-element.74.refs_3_, ...), custom_call_target="tpu_custom_call" | custom-call | tf_op jit(solution)/shard_map/last_exchange/pallas_call | solution.py:61
  105.9 2.0 %outputs.1 = (f32[50,2048]{1,0:T(8,128)}, f32[50,512]{1,0:T(8,128)}, f32[512,121]{1,0:T(8,128)}, f32[1,512]{1,0:T(1,128)}, f32[1,121]{1,0:T(1,128)}) custom-call(f32[50,2048]{1,0:T(8,128)} %get-tuple-element.76.refs_0_, f32[512,128]{1,0:T(8,128)} %bitcast.34, f32[8,128]{1,0:T(8,128)} %get-tuple-element.78.refs_2_, f32[4,8,8,128]{3,2,1,0:T(8,128)} %get-tuple-element.79.refs_3_), custom_call_target="tpu_custom_call" | custom-call | tf_op jit(solution)/shard_map/outputs/pallas_call | solution.py:61

commit v5 on v4

--- a/solution.py
+++ b/solution.py
@@ -33,16 +33,19 @@
 
 def call(kernel, args, out_shape, scratch_shapes, name, compiler_params):
     spaces = {"vmem": pltpu.VMEM, "smem": pltpu.SMEM}
-    in_buffers = [spaces[space](array.shape, array.dtype) for array, space in args]
+    moved = [n for n, (_, space) in enumerate(args) if space != "hbm"]
+    in_buffers = [spaces[args[n][1]](args[n][0].shape, args[n][0].dtype) for n in moved]
     out_buffers = [pltpu.VMEM(out.shape, out.dtype) for out in out_shape]
     n_in, n_out = len(args), len(out_shape)
 
     def body(*refs):
         inputs, outputs = refs[:n_in], refs[n_in:n_in + n_out]
-        bufs = refs[n_in + n_out:2 * n_in + 2 * n_out]
-        scratch, sems, out_sems = refs[2 * n_in + 2 * n_out:-2], refs[-2], refs[-1]
-        fetched = [Fetched(ref, bufs[n], sems.at[n]) for n, ref in enumerate(inputs)]
-        results = bufs[n_in:]
+        bufs = refs[n_in + n_out:n_in + 2 * n_out + len(moved)]
+        scratch, sems, out_sems = refs[n_in + 2 * n_out + len(moved):-2], refs[-2], refs[-1]
+        fetched = list(inputs)
+        for k, n in enumerate(moved):
+            fetched[n] = Fetched(inputs[n], bufs[k], sems.at[k])
+        results = bufs[len(moved):]
         stores = {}
 
         def flush(*buffers):
@@ -52,8 +55,8 @@
                 stores[n].start()
 
         kernel(*fetched, *results, *scratch, flush=flush)
-        for item in fetched:
-            item.get()
+        for n in moved:
+            fetched[n].get()
         flush(*[results[n] for n in range(n_out) if n not in stores])
         for n in range(n_out):
             stores[n].wait()
@@ -86,8 +89,9 @@
 
 
 def select_rows(onehot, value, dims=(((1,), (0,)), ((), ()))):
-    high, mid, low = split3(value)
-    return dot(onehot, low, dims) + dot(onehot, mid, dims) + dot(onehot, high, dims)
+    width = value.shape[1]
+    picked = dot(onehot, jnp.concatenate(split3(value), axis=1), dims)
+    return picked[:, 2 * width:] + picked[:, width:2 * width] + picked[:, :width]
 
 
 def pad_lanes(value):
@@ -126,9 +130,9 @@
     return jnp.concatenate([value, pltpu.roll(value, LANES // 2, 1)], axis=0)
 
 
-def gather_kernel(groups, hubrow, xt, send_idx, hub_ids, dh, dst, src, w,
+def gather_kernel(groups, hub_ids, dh, hubrow, xt, send_idx, dst, src, w,
                   xh_ref, hx_ref, dhh_ref, used_ref, db2_ref, wide_ref, *rest, flush):
-    lists, (x32, xg, hxg, dhg, xs, xr, dhr, ssem, rsem) = rest[:3 * WAYS], rest[3 * WAYS:]
+    lists, (x32, xg, hxg, dhg, dhp, dhs, xs, xr, dhr, ssem, rsem) = rest[:3 * WAYS], rest[3 * WAYS:]
     me = lax.axis_index("graph")
     barrier = greet(groups, me)
     feat, nodes = xt.ref.shape
@@ -136,6 +140,26 @@
     halo = send_idx.ref.shape[0]
     block = halo // groups
     base = me * nodes
+    chips = groups // 2
+    core, chip = lax.rem(me, 2), me // 2
+    dhg[...] = jnp.zeros_like(dhg)
+    hub_ref, dh_ref = hub_ids.get(), dh.get()
+
+    def hub_position_of(k):
+        row = hub_ref[k] - base
+        return jnp.logical_and(row >= 0, row < nodes), jnp.clip(row, 0, nodes - 1)
+
+    def pick_grad(i, carry):
+        for u in range(8):
+            k = i * 8 + u
+            own, row = hub_position_of(k)
+            value = dh_ref[pl.ds(row, 1), :]
+            dhg[pl.ds(k, 1), pl.ds(0, value.shape[1])] = jnp.where(own, value, 0.0)
+        return carry
+
+    lax.fori_loop(0, hubs // 8, pick_grad, 0)
+    pl.semaphore_wait(barrier, groups - 1)
+    pair = send(dhg, dhp, ssem.at[1, 0], rsem.at[1, 0], me + 1 - 2 * core)
     eye = (iota((feat, LANES), 0) == iota((feat, LANES), 1)).astype(BF16)
     tags = jnp.where(iota((hubs, LANES), 1) == feat, iota((hubs, LANES), 0) + 1, 0).astype(F32).astype(BF16)
     hubrow = hubrow.get()[...]
@@ -143,7 +167,6 @@
     for row in range(0, nodes, CHUNK):
         owned = (iota((CHUNK, hubs), 0) + (base + row) == hubrow).astype(BF16)
         x32[pl.ds(row, CHUNK), :] = dot(xt_ref[:, pl.ds(row, CHUNK)], eye, CONTRACT_ROWS) + dot(owned, tags)
-
     send_ref = send_idx.get()
 
     def pick(i, carry):
@@ -153,18 +176,12 @@
         return carry
 
     lax.fori_loop(0, halo // 16, pick, 0)
-    dhg[...] = jnp.zeros_like(dhg)
-    hub_ref, dh_ref = hub_ids.get(), dh.get()
 
     def pick_hub(i, carry):
         for u in range(8):
             k = i * 8 + u
-            row = hub_ref[k] - base
-            own = jnp.logical_and(row >= 0, row < nodes)
-            row = jnp.clip(row, 0, nodes - 1)
+            own, row = hub_position_of(k)
             hxg[pl.ds(k, 1), :] = jnp.where(own, x32[pl.ds(row, 1), :], 0.0)
-            value = dh_ref[pl.ds(row, 1), :]
-            dhg[pl.ds(k, 1), pl.ds(0, value.shape[1])] = jnp.where(own, value, 0.0)
         return carry
 
     lax.fori_loop(0, hubs // 8, pick_hub, 0)
@@ -172,12 +189,19 @@
     for q in range(groups):
         xs[q, pl.ds(0, block // 2), :] = pack_rows(xg[pl.ds(q * block, block), :])
         xs[q, pl.ds(block // 2, hubs // 2), :] = hub_rows
-    pl.semaphore_wait(barrier, groups - 1)
     copies = []
     for step in range(1, groups):
         peer = lax.rem(me + step, groups)
         copies.append(send(xs.at[peer], xr.at[me], ssem.at[0, step], rsem.at[0, step], peer))
-        copies.append(send(dhg, dhr.at[me], ssem.at[1, step], rsem.at[1, step], peer))
+    pair.wait()
+    dhs[...] = dhg[...] + dhp[...]
+    dhr[chip] = dhs[...]
+    half = pl.ds(pl.multiple_of(core * (hubs // 2), 8), hubs // 2)
+    for step in range(1, chips):
+        for other in range(2):
+            n = 2 * step + other
+            peer = 2 * lax.rem(chip + step, chips) + lax.rem(core + other, 2)
+            copies.append(send(dhs.at[half], dhr.at[chip, half], ssem.at[1, n], rsem.at[1, n], peer))
     dst_ref, src_ref, w_ref = dst.get(), src.get(), w.get()
     blocks = w_ref.shape[0]
     for q in range(WAYS):
@@ -209,7 +233,6 @@
     db2_ref[...] = jnp.broadcast_to(pad_lanes(total.sum(axis=0, keepdims=True)), db2_ref.shape)
     flush(used_ref, db2_ref)
     xr[me] = xs[me]
-    dhr[me] = dhg[...]
     for copy in copies:
         copy.wait()
     hx = jnp.zeros((hubs // 2, LANES), F32)
@@ -217,15 +240,16 @@
     for q in range(groups):
         xh_ref[pl.ds(q * block, block), :] = unpack_rows(xr[q, pl.ds(0, block // 2), :].astype(F32)).astype(BF16)
         hx = hx + xr[q, pl.ds(block // 2, hubs // 2), :].astype(F32)
+    for q in range(chips):
         dhh = dhh + dhr[q]
     hx_ref[...] = unpack_rows(hx)
     dhh_ref[...] = dhh
 
 
-def hub_position(hub_ref, k, base, nodes):
+def hub_position(hub_ref, k, base, nodes, spare):
     row = hub_ref[k] - base
     own = jnp.logical_and(row >= 0, row < nodes)
-    return own, pl.multiple_of(jnp.clip(row, 0, nodes - 1) * TILES, TILES)
+    return pl.multiple_of(jnp.where(own, row, spare + k) * TILES, TILES)
 
 
 def trips(used_ref, unroll):
@@ -253,7 +277,7 @@
     for acc in ya:
         acc[...] = jnp.zeros_like(acc)
     for acc in da:
-        acc[strided(0, nodes + halo + hubs), :] = jnp.zeros((nodes + halo + hubs, LANES), F32)
+        acc[strided(0, nodes + halo + 2 * hubs), :] = jnp.zeros((nodes + halo + 2 * hubs, LANES), F32)
     w1 = w1.get()[...]
     xt_ref, dh_ref, xh_ref, hx_ref = xt.get(), dh.get(), xh.get(), hx.get()
 
@@ -287,19 +311,23 @@
 
     lax.fori_loop(0, trips(used_ref, unroll), step, 0)
 
-    def fold(k, carry):
-        own, row = hub_position(hub_ref, k, base, nodes)
-        here = pl.multiple_of((nodes + k) * TILES, TILES)
-        ya[0][pl.ds(here, TILES), :] += jnp.where(own, total_of(ya, pl.ds(row, TILES)), 0.0)
-        here = (nodes + halo + k) * TILES
-        value = total_of(da, pl.ds(row, 1))
-        da[0][pl.ds(here, 1), :] += jnp.where(own, value, 0.0)
-        da[0][pl.ds(row, 1), :] = jnp.where(own, 0.0, value)
-        for acc in da[1:]:
-            acc[pl.ds(row, 1), :] = jnp.zeros((1, LANES), F32)
-        return carry
-
-    lax.fori_loop(0, hubs, fold, 0)
+    def fold(i, carry):
+        new = []
+        for u in range(8):
+            k = i * 8 + u
+            y_row = hub_position(hub_ref, k, base, nodes, nodes + hubs)
+            z_row = hub_position(hub_ref, k, base, nodes, nodes + halo + hubs)
+            y_hub = pl.ds(pl.multiple_of((nodes + k) * TILES, TILES), TILES)
+            z_hub = pl.ds(pl.multiple_of((nodes + halo + k) * TILES, TILES), 1)
+            new.append((y_hub, z_hub, z_row, ya[0][y_hub, :] + total_of(ya, pl.ds(y_row, TILES)), da[0][z_hub, :] + total_of(da, pl.ds(z_row, 1))))
+        for y_hub, z_hub, z_row, y_new, z_new in new:
+            ya[0][y_hub, :] = y_new
+            da[0][z_hub, :] = z_new
+            for acc in da:
+                acc[pl.ds(z_row, 1), :] = jnp.zeros((1, LANES), F32)
+        return carry
+
+    lax.fori_loop(0, hubs // 8, fold, 0)
     for row in range(0, nodes, CHUNK):
         for c in range(TILES):
             cols = pl.ds(c * LANES, LANES)
@@ -398,19 +426,22 @@
     for c in range(TILES):
         bias_ref[pl.ds(c, 1), :] = db1[:, c * LANES:(c + 1) * LANES]
         yt[strided(nodes * TILES + c, hubs), :] = dyh_ref[:, pl.ds(c * LANES, LANES)]
-    dw2_ref[...] = dot(h1_ref[...], dz2_ref[...], CONTRACT_ROWS) + dot(h1h_ref[...], dz2h_ref[...], CONTRACT_ROWS)
+    dw2_ref[...] = dot(dz2_ref[...], h1_ref[...], CONTRACT_ROWS) + dot(dz2h_ref[...], h1h_ref[...], CONTRACT_ROWS)
     flush(dw2_ref, bias_ref)
     used_ref, hub_ref, xh_ref, wide_ref = used.get(), hub_ids.get(), xh.get(), wide.get()
     lists = [item.get() for item in lists]
     length = wide_ref.shape[0] // WAYS
 
-    def place(k, carry):
-        own, row = hub_position(hub_ref, k, base, nodes)
-        here = pl.multiple_of((nodes + k) * TILES, TILES)
-        yt[pl.ds(row, TILES), :] = jnp.where(own, yt[pl.ds(here, TILES), :], yt[pl.ds(row, TILES), :])
-        return carry
-
-    lax.fori_loop(0, hubs, place, 0)
+    def place(i, carry):
+        new = []
+        for u in range(8):
+            k = i * 8 + u
+            new.append((hub_position(hub_ref, k, base, nodes, nodes + hubs), yt[pl.ds(pl.multiple_of((nodes + k) * TILES, TILES), TILES), :]))
+        for row, value in new:
+            yt[pl.ds(row, TILES), :] = value
+        return carry
+
+    lax.fori_loop(0, hubs // 8, place, 0)
 
     def step(i, carry):
         for n in range(unroll * WAYS):
@@ -424,17 +455,20 @@
 
     lax.fori_loop(0, trips(used_ref, unroll), step, 0)
 
-    def fold(k, carry):
-        own, row = hub_position(hub_ref, k, base, nodes)
-        here = pl.multiple_of((nodes + halo + k) * TILES, TILES)
-        value = total_of(za, pl.ds(row, TILES))
-        za[0][pl.ds(here, TILES), :] += jnp.where(own, value, 0.0)
-        za[0][pl.ds(row, TILES), :] = jnp.where(own, 0.0, value)
-        for acc in za[1:]:
-            acc[pl.ds(row, TILES), :] = jnp.zeros((TILES, LANES), F32)
-        return carry
-
-    lax.fori_loop(0, hubs, fold, 0)
+    def fold(i, carry):
+        new = []
+        for u in range(8):
+            k = i * 8 + u
+            row = hub_position(hub_ref, k, base, nodes, nodes + halo + hubs)
+            here = pl.ds(pl.multiple_of((nodes + halo + k) * TILES, TILES), TILES)
+            new.append((row, here, za[0][here, :] + total_of(za, pl.ds(row, TILES))))
+        for row, here, value in new:
+            za[0][here, :] = value
+            for acc in za:
+                acc[pl.ds(row, TILES), :] = jnp.zeros((TILES, LANES), F32)
+        return carry
+
+    lax.fori_loop(0, hubs // 8, fold, 0)
     for row in range(0, nodes, CHUNK):
         for c in range(TILES):
             dz1_ref[pl.ds(row, CHUNK), pl.ds(c * LANES, LANES)] = total_of(za, strided(row * TILES + c, CHUNK))
@@ -540,11 +574,10 @@
             dw2s[...] = total
             dw2_back = to(others, 7, lambda p: dw2s, dw2a.at[core, chip])
             dw2a[core, chip] = total
-        if c > 0:
-            spread(c - 1)
-        if c == 2:
-            wait(dw2_back)
-            dw2_pair = to([partner], 8, lambda p: dw2a.at[core], dw2a.at[core])
+    for c in range(TILES - 1):
+        spread(c)
+    wait(dw2_back)
+    dw2_pair = to([partner], 8, lambda p: dw2a.at[core], dw2a.at[core])
     wait(back_copies)
     hub_rows = dha[...].reshape(hubs, HID)
     for row in range(0, nodes, 2 * CHUNK):
@@ -567,7 +600,7 @@
     feat, out = gw1_ref.shape[0], gw2_ref.shape[1]
     gxt_ref[...] = gxt.get()[...]
     flush(gxt_ref)
-    gw2_ref[...] = dw2.get()[:, pl.ds(0, out)]
+    gw2_ref[...] = dw2.get()[...].T[:, :out]
     flush(gw2_ref)
     bias_ref, dw1_ref = bias.get(), dw1.get()
     for c in range(TILES):
@@ -606,7 +639,7 @@
         hubs = hub_ids.shape[0]
         out = dy_out.shape[1]
         block, home = halo // groups, hubs // groups
-        src_rows, dst_rows = nodes + halo + hubs, nodes + hubs
+        src_rows, dst_rows = nodes + halo + 2 * hubs, nodes + 2 * hubs
         x_t = x_loc.T
         hub_lanes = hub_ids.reshape(1, hubs)
         send_lanes = send_loc.reshape(1, halo)
@@ -618,14 +651,15 @@
 
         xh, hx, dhh, used, db2, wide, *lists = call(
             functools.partial(gather_kernel, groups),
-            [(hub_lanes, "vmem"), (x_t, "vmem"), (send_loc, "smem"), (hub_ids, "smem"), (dy_out, "vmem"),
+            [(hub_ids, "smem"), (dy_out, "vmem"), (hub_lanes, "vmem"), (x_t, "vmem"), (send_loc, "smem"),
              (table(dst_loc), "vmem"), (table(src_loc), "vmem"), (table(w_loc), "vmem")],
             (shape((halo, LANES), BF16), shape((hubs, LANES), F32), shape((hubs, LANES), F32),
              shape((8, LANES), I32), shape((8, LANES), F32), shape((edges, LANES), F32))
             + (shape(part_list, I32),) * (2 * WAYS) + (shape(part_list, F32),) * WAYS,
             [pltpu.VMEM((nodes, LANES), F32), pltpu.VMEM((halo, LANES), F32), pltpu.VMEM((hubs, LANES), F32),
-             pltpu.VMEM((hubs, LANES), F32), pltpu.VMEM((groups, packed, LANES), BF16),
-             pltpu.VMEM((groups, packed, LANES), BF16), pltpu.VMEM((groups, hubs, LANES), F32)] + sems(2),
+             pltpu.VMEM((hubs, LANES), F32), pltpu.VMEM((hubs, LANES), F32), pltpu.VMEM((hubs, LANES), F32),
+             pltpu.VMEM((groups, packed, LANES), BF16), pltpu.VMEM((groups, packed, LANES), BF16),
+             pltpu.VMEM((groups // 2, hubs, LANES), F32)] + sems(2),
             "gather_rows", params(0))
         lists = [(item.reshape(edges // WAYS), "smem") for item in lists]
 
@@ -651,28 +685,28 @@
             functools.partial(edges_backward_kernel, copies2, unroll2, feat, groups),
             [(w_second, "vmem"), (h1, "vmem"), (dz2, "vmem"), (dyh, "vmem"), (h1h, "vmem"), (dz2h, "vmem"),
              (used, "smem"), (hub_ids, "smem"), (xh, "vmem"), (db2, "vmem"), (wide, "vmem")] + lists[:2 * WAYS],
-            (shape((nodes, HID), F32), shape((TILES, halo, LANES), F32), shape((hubs, HID), F32), shape((HID, LANES), F32), shape((8, LANES), F32)),
+            (shape((nodes, HID), F32), shape((TILES, halo, LANES), F32), shape((hubs, HID), F32), shape((LANES, HID), F32), shape((8, LANES), F32)),
             [pltpu.VMEM((dst_rows * TILES, LANES), F32)] + [pltpu.VMEM((src_rows * TILES, LANES), F32)] * copies2,
             "edges_backward", params())
 
         chips = groups // 2
-        part = HID // groups
+        part = LANES // groups
         grad_xt, dw1, dw2, biases = call(
             functools.partial(last_kernel, groups),
             [(hub1.reshape(2, chips, home, HID), "vmem"), (hz1.reshape(TILES, groups, block, LANES), "vmem"),
-             (dw2.reshape(2, chips, part, LANES), "vmem"), (biases, "vmem"), (send_lanes, "vmem"), (x_t, "vmem"), (hx, "vmem"),
+             (dw2.reshape(2, chips, part, HID), "vmem"), (biases, "vmem"), (send_lanes, "vmem"), (x_t, "vmem"), (hx, "vmem"),
              (dz1, "vmem"), (w_first, "vmem"), (hub_lanes, "vmem")],
-            (shape((feat, nodes), F32), shape((TILES, groups, 8, LANES), F32), shape((2, chips, part, LANES), F32), shape((8, LANES), F32)),
+            (shape((feat, nodes), F32), shape((TILES, groups, 8, LANES), F32), shape((2, chips, part, HID), F32), shape((8, LANES), F32)),
             [pltpu.VMEM((nodes, HID), BF16), pltpu.VMEM((nodes, halo), BF16), pltpu.VMEM((TILES, groups, block, LANES), F32)]
             + [pltpu.VMEM((chips, home, HID), F32)] * 3 + [pltpu.VMEM((8, LANES), F32)] * 2 + [pltpu.VMEM((chips, 8, LANES), F32)]
             + [pltpu.VMEM((home, HID), BF16), pltpu.VMEM((groups, home, HID), BF16)]
-            + [pltpu.VMEM((chips, part, LANES), F32)] * 3 + [pltpu.VMEM((part, LANES), F32)]
+            + [pltpu.VMEM((chips, part, HID), F32)] * 3 + [pltpu.VMEM((part, HID), F32)]
             + [pltpu.VMEM((TILES, groups * 8, LANES), F32), pltpu.VMEM((TILES, groups, 8, LANES), F32), pltpu.VMEM((TILES, 8, LANES), F32)] + sems(21),
             "last_exchange", params(2))
 
         grad_xt, grad_w1, grad_w2, grad_b1, grad_b2 = call(
             outputs_kernel,
-            [(grad_xt, "vmem"), (dw2.reshape(HID, LANES), "vmem"), (biases, "vmem"), (dw1, "vmem")],
+            [(grad_xt, "vmem"), (dw2.reshape(LANES, HID), "vmem"), (biases, "vmem"), (dw1, "vmem")],
             (shape((feat, nodes), F32), shape((feat, HID), F32), shape((HID, out), F32), shape((1, HID), F32), shape((1, out), F32)),
             [], "outputs", params())
         return grad_xt.T, grad_w1, grad_w2, grad_b1.reshape(HID), grad_b2.reshape(out)

time: 108 us -> 102 us (0.944)
  Pallas kernels: 107 us -> 101 us
    pallas_call x6, Pallas kernels: 107 us -> 101 us  [call(): pl.pallas_call(body, name=name, out_shape=out_shape, in_specs=[HBM] * n_i...]
where the time goes in v5:
time: 102 us
  Pallas kernels  101 us (99%)
    pallas_call x6, Pallas kernels, call(): pl.pallas_call(body, name=name, out_shape=out_shape, in_specs=[HBM] * n_i...  101 us

profile of v5, /device:TPU:0, one launch (start us, length us, event | category | flops | bytes accessed | tf_op | source)
XLA Modules:
  0.0 101.5 jit_solution(8619902289742615269)
XLA Ops:
  0.6 12.4 %gather_rows.1 = (bf16[512,128]{1,0:T(8,128)(2,1)}, f32[64,128]{1,0:T(8,128)}, f32[64,128]{1,0:T(8,128)}, s32[8,128]{1,0:T(8,128)}, f32[8,128]{1,0:T(8,128)}, /*...) custom-call(s32[64]{0:T(128)} %refs_7_.3, ...), custom_call_target="tpu_custom_call" | custom-call | tf_op jit(solution)/shard_map/gather_rows/pallas_call | solution.py:64
  13.1 14.2 %edges_forward.1 = (bf16[2048,512]{1,0:T(8,128)(2,1)}, f32[2048,128]{1,0:T(8,128)}, f32[512,128]{1,0:T(8,128)}, f32[64,640]{1,0:T(8,128)}) custom-call(bf16[50,512]{1,0:T(8,128)(2,1)} %refs_8_.1, bf16[50,2048]{1,0:T(8,128)(2,1)} %bitcast.29, f32[2048,121]{1,0:T(8,128)} %refs_2_.1, bf16[512,128]{1,0:T(8,128)(2,1)} %get-tuple-element.45.refs_3_.refs_8_, ...), custom_call_target="tpu_custom_call" | custom-call | tf_op jit(solution)/shard_map/edges_forward/pallas_call | solution.py:64
  27.3 21.7 %middle.1 = (bf16[2048,128]{1,0:T(8,128)(2,1)}, f32[64,512]{1,0:T(8,128)}, bf16[8,512]{1,0:T(8,128)(2,1)}, bf16[8,128]{1,0:T(8,128)(2,1)}) custom-call(f32[8,8,640]{2,1,0:T(8,128)} %bitcast.35, f32[8,64,128]{2,1,0:T(8,128)} %bitcast.33, f32[2048,128]{1,0:T(8,128)} %get-tuple-element.64.refs_2_, f32[1,512]{1,0:T(1,128)} %bitcast.65, ...), custom_call_target="tpu_custom_call" | custom-call | tf_op jit(solution)/shard_map/middle/pallas_call | solution.py:64
  49.0 13.9 %edges_backward.1 = (f32[2048,512]{1,0:T(8,128)}, f32[4,512,128]{2,1,0:T(8,128)}, f32[64,512]{1,0:T(8,128)}, f32[128,512]{1,0:T(8,128)}, f32[8,128]{1,0:T(8,128)}) custom-call(bf16[512,121]{1,0:T(8,128)(2,1)} %refs_0_.5, bf16[2048,512]{1,0:T(8,128)(2,1)} %get-tuple-element.61.refs_1_, bf16[2048,128]{1,0:T(8,128)(2,1)} %get-tuple-element.65.refs_2_, ...), custom_call_target="tpu_custom_call" | custom-call | tf_op jit(solution)/shard_map/edges_backward/pallas_call | solution.py:64
  62.9 36.5 %last_exchange.1 = (f32[50,2048]{1,0:T(8,128)}, f32[4,8,8,128]{3,2,1,0:T(8,128)}, f32[2,4,16,512]{3,2,1,0:T(8,128)}, f32[8,128]{1,0:T(8,128)}) custom-call(f32[2,4,8,512]{3,2,1,0:T(8,128)} %bitcast.36, f32[4,8,64,128]{3,2,1,0:T(8,128)} %bitcast.31, f32[2,4,16,512]{3,2,1,0:T(8,128)} %bitcast.32, f32[8,128]{1,0:T(8,128)} %get-tuple-element.74.refs_3_, ...), custom_call_target="tpu_custom_call" | custom-call | tf_op jit(solution)/shard_map/last_exchange/pallas_call | solution.py:64
  99.3 2.0 %outputs.1 = (f32[50,2048]{1,0:T(8,128)}, f32[50,512]{1,0:T(8,128)}, f32[512,121]{1,0:T(8,128)}, f32[1,512]{1,0:T(1,128)}, f32[1,121]{1,0:T(1,128)}) custom-call(f32[50,2048]{1,0:T(8,128)} %get-tuple-element.76.refs_0_, f32[128,512]{1,0:T(8,128)} %bitcast.34, f32[8,128]{1,0:T(8,128)} %get-tuple-element.78.refs_2_, f32[4,8,8,128]{3,2,1,0:T(8,128)} %get-tuple-element.79.refs_3_), custom_call_target="tpu_custom_call" | custom-call | tf_op jit(solution)/shard_map/outputs/pallas_call | solution.py:64

commit v6 on v5

--- a/solution.py
+++ b/solution.py
@@ -15,6 +15,7 @@
 HID = 512
 TILES = HID // LANES
 CHUNK = 256
+TALL = 1024
 VMEM_LIMIT = 67043328
 HBM = pl.BlockSpec(memory_space=pltpu.HBM)
 
@@ -490,7 +491,7 @@
     feat, nodes = xt.ref.shape
     chips, home = hub.ref.shape[1:3]
     hubs = groups * home
-    block = hz.ref.shape[2]
+    block = hz.shape[2]
     halo = groups * block
     base = me * nodes
     core, chip = lax.rem(me, 2), me // 2
@@ -498,7 +499,6 @@
     own = hub_block(me, groups)
     peers = [lax.rem(me + step, groups) for step in range(1, groups)]
     others = [lax.rem(me + 2 * step, groups) for step in range(1, chips)]
-    hub_ref, hz_ref, dw2_ref, bias_ref = hub.get(), hz.get(), dw2.get(), bias.get()
     pl.semaphore_wait(barrier, groups - 1)
 
     def to(devices, slot, src, dst):
@@ -508,9 +508,10 @@
         for copy in pending:
             copy.wait()
 
+    halo_copies = [to(peers, 9, lambda p: hz.at[0, p], hzr.at[0, me])]
+    hub_ref, dw2_ref, bias_ref = hub.get(), dw2.get(), bias.get()
     pair_copies = (to([partner], 0, lambda p: hub_ref.at[1 - core], hubp) + to([partner], 1, lambda p: dw2_ref.at[1 - core], dw2p)
                    + to([partner], 2, lambda p: bias_ref, biasp))
-    halo_copies = [to(peers, 9, lambda p: hz_ref.at[0, p], hzr.at[0, me])]
     sendrow = sendrow.get()[...]
     for row in range(0, nodes, CHUNK):
         onehot[pl.ds(row, CHUNK), :] = (iota((CHUNK, halo), 0) + row == sendrow).astype(BF16)
@@ -527,7 +528,7 @@
     hub_copies = to(others, 3, lambda p: hubh.at[p // 2], hubr.at[chip])
     dw2_copies = to(others, 4, lambda p: dw2h.at[p // 2], dw2r.at[chip])
     bias_copies = to(others, 5, lambda p: biash, biasr.at[chip])
-    halo_copies += [to(peers, 9 + c, lambda p: hz_ref.at[c, p], hzr.at[c, me]) for c in range(1, TILES)]
+    halo_copies += [to(peers, 9 + c, lambda p: hz.at[c, p], hzr.at[c, me]) for c in range(1, TILES)]
 
     def total_over(ref, count):
         total = ref[0]
@@ -536,13 +537,6 @@
         return total
 
     xt_ref, dz1_ref, hx_ref, w1, hubrow = xt.get(), dz1.get(), hx.get(), w1.get()[...], hubrow.get()[...]
-    wait(hub_copies)
-    dz1h = total_over(hubr, chips).astype(BF16)
-    dhs[...] = dz1h
-    back_copies = to(peers, 6, lambda p: dhs, dha.at[own])
-    dha[own] = dz1h
-    hx_mine = hx_ref[pl.ds(pl.multiple_of(own * home, 8), home), :].astype(BF16)
-    dw1h = dot(hx_mine[:, :feat], dz1h, CONTRACT_ROWS)
     rs_copies, ag_copies = [None] * TILES, [None] * TILES
 
     def spread(c):
@@ -558,13 +552,21 @@
         pieces = jnp.concatenate(split3(hzr[c].reshape(halo, LANES)), axis=1)
 
         def rows_step(i, carry):
-            rows = pl.ds(pl.multiple_of(i * CHUNK, CHUNK), CHUNK)
+            rows = pl.ds(pl.multiple_of(i * TALL, TALL), TALL)
             value = dot(onehot[rows, :], pieces)
             value = value[:, 2 * LANES:] + value[:, LANES:2 * LANES] + value[:, :LANES]
             dz_out[rows, cols] = (dz1_ref[rows, cols] + value).astype(BF16)
             return carry
 
-        lax.fori_loop(0, nodes // CHUNK, rows_step, 0)
+        lax.fori_loop(0, nodes // TALL, rows_step, 0)
+        if c == 0:
+            wait(hub_copies)
+            dz1h = total_over(hubr, chips).astype(BF16)
+            dhs[...] = dz1h
+            back_copies = to(peers, 6, lambda p: dhs, dha.at[own])
+            dha[own] = dz1h
+            hx_mine = hx_ref[pl.ds(pl.multiple_of(own * home, 8), home), :].astype(BF16)
+            dw1h = dot(hx_mine[:, :feat], dz1h, CONTRACT_ROWS)
         dw1s[c, pl.ds(0, feat), :] = dot(xt_ref[...], dz_out[:, cols]) + dw1h[:, c * LANES:(c + 1) * LANES]
         rs_copies[c] = to(peers, 13 + c, lambda p: dw1s.at[c, pl.ds(pl.multiple_of(p * 8, 8), 8)], dw1r.at[c, me])
         dw1r[c, me] = dw1s[c, pl.ds(pl.multiple_of(me * 8, 8), 8), :]
@@ -624,8 +626,8 @@
     part_spec = P("data")
     part_rows = P("data", None)
     replicated = P()
-    copies1, unroll1 = 3, 16
-    copies2, unroll2 = 5, 16
+    copies1, unroll1 = 3, 32
+    copies2, unroll2 = 5, 32
 
     def params(collective_id=None):
         if collective_id is None:
@@ -693,7 +695,7 @@
         part = LANES // groups
         grad_xt, dw1, dw2, biases = call(
             functools.partial(last_kernel, groups),
-            [(hub1.reshape(2, chips, home, HID), "vmem"), (hz1.reshape(TILES, groups, block, LANES), "vmem"),
+            [(hub1.reshape(2, chips, home, HID), "vmem"), (hz1.reshape(TILES, groups, block, LANES), "hbm"),
              (dw2.reshape(2, chips, part, HID), "vmem"), (biases, "vmem"), (send_lanes, "vmem"), (x_t, "vmem"), (hx, "vmem"),
              (dz1, "vmem"), (w_first, "vmem"), (hub_lanes, "vmem")],
             (shape((feat, nodes), F32), shape((TILES, groups, 8, LANES), F32), shape((2, chips, part, HID), F32), shape((8, LANES), F32)),

time: 102 us -> 100 us (0.980)
  Pallas kernels: 101 us -> 99.4 us
    pallas_call x6, Pallas kernels: 101 us -> 99.4 us  [call(): pl.pallas_call(body, name=name, out_shape=out_shape, in_specs=[HBM] * n_i...]
where the time goes in v6:
time: 100 us
  Pallas kernels  99.4 us (99%)
    pallas_call x6, Pallas kernels, call(): pl.pallas_call(body, name=name, out_shape=out_shape, in_specs=[HBM] * n_i...  99.4 us

profile of v6, /device:TPU:0, one launch (start us, length us, event | category | flops | bytes accessed | tf_op | source)
XLA Modules:
  0.0 100.2 jit_solution(13173781915774157424)
XLA Ops:
  0.6 12.4 %gather_rows.1 = (bf16[512,128]{1,0:T(8,128)(2,1)}, f32[64,128]{1,0:T(8,128)}, f32[64,128]{1,0:T(8,128)}, s32[8,128]{1,0:T(8,128)}, f32[8,128]{1,0:T(8,128)}, /*...) custom-call(s32[64]{0:T(128)} %refs_7_.3, ...), custom_call_target="tpu_custom_call" | custom-call | tf_op jit(solution)/shard_map/gather_rows/pallas_call | solution.py:65
  13.1 11.5 %edges_forward.1 = (bf16[2048,512]{1,0:T(8,128)(2,1)}, f32[2048,128]{1,0:T(8,128)}, f32[512,128]{1,0:T(8,128)}, f32[64,640]{1,0:T(8,128)}) custom-call(bf16[50,512]{1,0:T(8,128)(2,1)} %refs_8_.1, bf16[50,2048]{1,0:T(8,128)(2,1)} %bitcast.29, f32[2048,121]{1,0:T(8,128)} %refs_2_.1, bf16[512,128]{1,0:T(8,128)(2,1)} %get-tuple-element.45.refs_3_.refs_8_, ...), custom_call_target="tpu_custom_call" | custom-call | tf_op jit(solution)/shard_map/edges_forward/pallas_call | solution.py:65
  24.6 23.9 %middle.1 = (bf16[2048,128]{1,0:T(8,128)(2,1)}, f32[64,512]{1,0:T(8,128)}, bf16[8,512]{1,0:T(8,128)(2,1)}, bf16[8,128]{1,0:T(8,128)(2,1)}) custom-call(f32[8,8,640]{2,1,0:T(8,128)} %bitcast.35, f32[8,64,128]{2,1,0:T(8,128)} %bitcast.33, f32[2048,128]{1,0:T(8,128)} %get-tuple-element.64.refs_2_, f32[1,512]{1,0:T(1,128)} %bitcast.65, ...), custom_call_target="tpu_custom_call" | custom-call | tf_op jit(solution)/shard_map/middle/pallas_call | solution.py:65
  48.6 12.3 %edges_backward.1 = (f32[2048,512]{1,0:T(8,128)}, f32[4,512,128]{2,1,0:T(8,128)}, f32[64,512]{1,0:T(8,128)}, f32[128,512]{1,0:T(8,128)}, f32[8,128]{1,0:T(8,128)}) custom-call(bf16[512,121]{1,0:T(8,128)(2,1)} %refs_0_.5, bf16[2048,512]{1,0:T(8,128)(2,1)} %get-tuple-element.61.refs_1_, bf16[2048,128]{1,0:T(8,128)(2,1)} %get-tuple-element.65.refs_2_, ...), custom_call_target="tpu_custom_call" | custom-call | tf_op jit(solution)/shard_map/edges_backward/pallas_call | solution.py:65
  60.9 37.1 %last_exchange.1 = (f32[50,2048]{1,0:T(8,128)}, f32[4,8,8,128]{3,2,1,0:T(8,128)}, f32[2,4,16,512]{3,2,1,0:T(8,128)}, f32[8,128]{1,0:T(8,128)}) custom-call(f32[2,4,8,512]{3,2,1,0:T(8,128)} %bitcast.36, f32[4,8,64,128]{3,2,1,0:T(8,128)} %bitcast.31, f32[2,4,16,512]{3,2,1,0:T(8,128)} %bitcast.32, f32[8,128]{1,0:T(8,128)} %get-tuple-element.74.refs_3_, ...), custom_call_target="tpu_custom_call" | custom-call | tf_op jit(solution)/shard_map/last_exchange/pallas_call | solution.py:65
  98.0 2.0 %outputs.1 = (f32[50,2048]{1,0:T(8,128)}, f32[50,512]{1,0:T(8,128)}, f32[512,121]{1,0:T(8,128)}, f32[1,512]{1,0:T(1,128)}, f32[1,121]{1,0:T(1,128)}) custom-call(f32[50,2048]{1,0:T(8,128)} %get-tuple-element.76.refs_0_, f32[128,512]{1,0:T(8,128)} %bitcast.34, f32[8,128]{1,0:T(8,128)} %get-tuple-element.78.refs_2_, f32[4,8,8,128]{3,2,1,0:T(8,128)} %get-tuple-element.79.refs_3_), custom_call_target="tpu_custom_call" | custom-call | tf_op jit(solution)/shard_map/outputs/pallas_call | solution.py:65

commit v7 on v6

--- a/solution.py
+++ b/solution.py
@@ -132,7 +132,7 @@
 
 
 def gather_kernel(groups, hub_ids, dh, hubrow, xt, send_idx, dst, src, w,
-                  xh_ref, hx_ref, dhh_ref, used_ref, db2_ref, wide_ref, *rest, flush):
+                  xh_ref, hx_ref, dhh_ref, used_ref, db2_ref, *rest, flush):
     lists, (x32, xg, hxg, dhg, dhp, dhs, xs, xr, dhr, ssem, rsem) = rest[:3 * WAYS], rest[3 * WAYS:]
     me = lax.axis_index("graph")
     barrier = greet(groups, me)
@@ -211,22 +211,8 @@
         lists[WAYS + q][...] = src_ref[part, :] * TILES
         lists[2 * WAYS + q][...] = w_ref[part, :]
     flush(*lists)
-    diagonal = iota((LANES, LANES), 0) == iota((LANES, LANES), 1)
-    ones = jnp.ones((LANES, LANES), BF16)
-
-    def widen(i, carry):
-        for q in range(WAYS):
-            row = lists[2 * WAYS + q][pl.ds(i, 1), :]
-            spread = jnp.zeros((LANES, LANES), F32)
-            for piece in reversed(split3(row)):
-                column = jnp.where(diagonal, jnp.broadcast_to(piece.astype(F32), (LANES, LANES)), 0.0).astype(BF16)
-                spread = spread + dot(column, ones)
-            wide_ref[pl.ds(pl.multiple_of((q * (blocks // WAYS) + i) * LANES, LANES), LANES), :] = spread
-        return carry
-
-    lax.fori_loop(0, blocks // WAYS, widen, 0)
-    flush(wide_ref)
-    used = jnp.where(w_ref[...] > 0.0, 1.0, 0.0).sum(axis=0, keepdims=True).sum(axis=1, keepdims=True)
+    place = (iota(w_ref.shape, 0) * LANES + iota(w_ref.shape, 1) + 1).astype(F32)
+    used = jnp.where(w_ref[...] > 0.0, place, 0.0).max(axis=0, keepdims=True).max(axis=1, keepdims=True)
     used_ref[...] = jnp.broadcast_to(used, used_ref.shape).astype(I32)
     total = jnp.zeros((8, dh_ref.shape[1]), F32)
     for row in range(0, nodes, CHUNK):
@@ -348,8 +334,8 @@
     hub_out[:, pl.ds(HID, LANES)] = hub_z
 
 
-def middle_kernel(groups, hub, hz, dz, b1, w2, sendrow,
-                  dz2_ref, dyh_ref, h1h_ref, dz2h_ref,
+def middle_kernel(groups, hub, hz, dz, b1, w2, sendrow, w,
+                  dz2_ref, dyh_ref, h1h_ref, dz2h_ref, wide_ref,
                   hzr, hubr, dyr, dys, ssem, rsem, flush):
     me = lax.axis_index("graph")
     barrier = greet(groups, me)
@@ -370,6 +356,23 @@
     for step in range(1, groups):
         peer = lax.rem(me + step, groups)
         halo_copies.append(send(hz_ref.at[peer], hzr.at[me], ssem.at[1, step], rsem.at[1, step], peer))
+    w_ref = w.get()
+    blocks = w_ref.shape[0]
+    diagonal = iota((LANES, LANES), 0) == iota((LANES, LANES), 1)
+    ones = jnp.ones((LANES, LANES), BF16)
+
+    def widen(i, carry):
+        for q in range(WAYS):
+            row = w_ref[pl.ds(i * WAYS + q, 1), :]
+            spread = jnp.zeros((LANES, LANES), F32)
+            for piece in reversed(split3(row)):
+                column = jnp.where(diagonal, jnp.broadcast_to(piece.astype(F32), (LANES, LANES)), 0.0).astype(BF16)
+                spread = spread + dot(column, ones)
+            wide_ref[pl.ds(pl.multiple_of((q * (blocks // WAYS) + i) * LANES, LANES), LANES), :] = spread
+        return carry
+
+    lax.fori_loop(0, blocks // WAYS, widen, 0)
+    flush(wide_ref)
     for copy in hub_copies:
         copy.wait()
     total = hubr[0]
@@ -651,12 +654,12 @@
         part_list = (edges // LANES // WAYS, LANES)
         packed = (block + hubs) // 2
 
-        xh, hx, dhh, used, db2, wide, *lists = call(
+        xh, hx, dhh, used, db2, *lists = call(
             functools.partial(gather_kernel, groups),
             [(hub_ids, "smem"), (dy_out, "vmem"), (hub_lanes, "vmem"), (x_t, "vmem"), (send_loc, "smem"),
              (table(dst_loc), "vmem"), (table(src_loc), "vmem"), (table(w_loc), "vmem")],
             (shape((halo, LANES), BF16), shape((hubs, LANES), F32), shape((hubs, LANES), F32),
-             shape((8, LANES), I32), shape((8, LANES), F32), shape((edges, LANES), F32))
+             shape((8, LANES), I32), shape((8, LANES), F32))
             + (shape(part_list, I32),) * (2 * WAYS) + (shape(part_list, F32),) * WAYS,
             [pltpu.VMEM((nodes, LANES), F32), pltpu.VMEM((halo, LANES), F32), pltpu.VMEM((hubs, LANES), F32),
              pltpu.VMEM((hubs, LANES), F32), pltpu.VMEM((hubs, LANES), F32), pltpu.VMEM((hubs, LANES), F32),
@@ -674,11 +677,11 @@
             + [pltpu.VMEM((dst_rows * TILES, LANES), F32)] * copies1 + [pltpu.VMEM((src_rows * TILES, LANES), F32)] * copies1,
             "edges_forward", params())
 
-        dz2, dyh, h1h, dz2h = call(
+        dz2, dyh, h1h, dz2h, wide = call(
             functools.partial(middle_kernel, groups),
             [(hub.reshape(groups, home, HID + LANES), "vmem"), (hz.reshape(groups, block, LANES), "vmem"), (dz, "vmem"),
-             (bias, "vmem"), (w_second, "vmem"), (send_lanes, "vmem")],
-            (shape((nodes, LANES), BF16), shape((hubs, HID), F32), shape((home, HID), BF16), shape((home, LANES), BF16)),
+             (bias, "vmem"), (w_second, "vmem"), (send_lanes, "vmem"), (table(w_loc), "vmem")],
+            (shape((nodes, LANES), BF16), shape((hubs, HID), F32), shape((home, HID), BF16), shape((home, LANES), BF16), shape((edges, LANES), F32)),
             [pltpu.VMEM((groups, block, LANES), F32), pltpu.VMEM((groups, home, HID + LANES), F32),
              pltpu.VMEM((groups, home, HID), F32), pltpu.VMEM((home, HID), F32)] + sems(3),
             "middle", params(1))

time: 100 us -> 99.7 us (level)
  no operation moved by 1% of the time
where the time goes in v7:
time: 99.7 us; the launch traced here: 99.8 us
  Pallas kernels  98.9 us (99%)
    pallas_call x6, Pallas kernels, call(): pl.pallas_call(body, name=name, out_shape=out_shape, in_specs=[HBM] * n_i...  98.9 us

profile of v7, /device:TPU:0, one launch (start us, length us, event | category | flops | bytes accessed | tf_op | source)
XLA Modules:
  0.0 99.8 jit_solution(8543056193979845319)
XLA Ops:
  0.6 11.5 %gather_rows.1 = (bf16[512,128]{1,0:T(8,128)(2,1)}, f32[64,128]{1,0:T(8,128)}, f32[64,128]{1,0:T(8,128)}, s32[8,128]{1,0:T(8,128)}, f32[8,128]{1,0:T(8,128)}, /*...) custom-call(s32[64]{0:T(128)} %refs_7_.3, ...), custom_call_target="tpu_custom_call" | custom-call | tf_op jit(solution)/shard_map/gather_rows/pallas_call | solution.py:65
  12.1 14.1 %edges_forward.1 = (bf16[2048,512]{1,0:T(8,128)(2,1)}, f32[2048,128]{1,0:T(8,128)}, f32[512,128]{1,0:T(8,128)}, f32[64,640]{1,0:T(8,128)}) custom-call(bf16[50,512]{1,0:T(8,128)(2,1)} %refs_8_.1, bf16[50,2048]{1,0:T(8,128)(2,1)} %bitcast.29, f32[2048,121]{1,0:T(8,128)} %refs_2_.1, bf16[512,128]{1,0:T(8,128)(2,1)} %get-tuple-element.45.refs_3_.refs_8_, ...), custom_call_target="tpu_custom_call" | custom-call | tf_op jit(solution)/shard_map/edges_forward/pallas_call | solution.py:65
  26.2 22.1 %middle.1 = (bf16[2048,128]{1,0:T(8,128)(2,1)}, f32[64,512]{1,0:T(8,128)}, bf16[8,512]{1,0:T(8,128)(2,1)}, bf16[8,128]{1,0:T(8,128)(2,1)}, f32[8192,128]{1,0:T(8,128)}) custom-call(f32[8,8,640]{2,1,0:T(8,128)} %bitcast.35, f32[8,64,128]{2,1,0:T(8,128)} %bitcast.33, f32[2048,128]{1,0:T(8,128)} %get-tuple-element.64.refs_2_, f32[1,512]{1,0:T(1,128)} %bitcast.66, ...), custom_call_target="tpu_custom_call" | custom-call | tf_op jit(solution)/shard_map/middle/pallas_call | solution.py:65
  48.2 13.8 %edges_backward.1 = (f32[2048,512]{1,0:T(8,128)}, f32[4,512,128]{2,1,0:T(8,128)}, f32[64,512]{1,0:T(8,128)}, f32[128,512]{1,0:T(8,128)}, f32[8,128]{1,0:T(8,128)}) custom-call(bf16[512,121]{1,0:T(8,128)(2,1)} %refs_0_.5, bf16[2048,512]{1,0:T(8,128)(2,1)} %get-tuple-element.61.refs_1_, bf16[2048,128]{1,0:T(8,128)(2,1)} %get-tuple-element.65.refs_2_, ...), custom_call_target="tpu_custom_call" | custom-call | tf_op jit(solution)/shard_map/edges_backward/pallas_call | solution.py:65
  62.0 35.5 %last_exchange.1 = (f32[50,2048]{1,0:T(8,128)}, f32[4,8,8,128]{3,2,1,0:T(8,128)}, f32[2,4,16,512]{3,2,1,0:T(8,128)}, f32[8,128]{1,0:T(8,128)}) custom-call(f32[2,4,8,512]{3,2,1,0:T(8,128)} %bitcast.36, f32[4,8,64,128]{3,2,1,0:T(8,128)} %bitcast.31, f32[2,4,16,512]{3,2,1,0:T(8,128)} %bitcast.32, f32[8,128]{1,0:T(8,128)} %get-tuple-element.74.refs_3_, ...), custom_call_target="tpu_custom_call" | custom-call | tf_op jit(solution)/shard_map/last_exchange/pallas_call | solution.py:65
  97.6 2.0 %outputs.1 = (f32[50,2048]{1,0:T(8,128)}, f32[50,512]{1,0:T(8,128)}, f32[512,121]{1,0:T(8,128)}, f32[1,512]{1,0:T(1,128)}, f32[1,121]{1,0:T(1,128)}) custom-call(f32[50,2048]{1,0:T(8,128)} %get-tuple-element.76.refs_0_, f32[128,512]{1,0:T(8,128)} %bitcast.34, f32[8,128]{1,0:T(8,128)} %get-tuple-element.78.refs_2_, f32[4,8,8,128]{3,2,1,0:T(8,128)} %get-tuple-element.79.refs_3_), custom_call_target="tpu_custom_call" | custom-call | tf_op jit(solution)/shard_map/outputs/pallas_call | solution.py:65

commit v8 on v7

--- a/solution.py
+++ b/solution.py
@@ -15,7 +15,7 @@
 HID = 512
 TILES = HID // LANES
 CHUNK = 256
-TALL = 1024
+TALL = 2048
 VMEM_LIMIT = 67043328
 HBM = pl.BlockSpec(memory_space=pltpu.HBM)
 
@@ -390,14 +390,13 @@
     dyr[own] = dys[...]
     for copy in halo_copies:
         copy.wait()
-    pieces = split3(hzr[...].reshape(halo, LANES))
+    pieces = jnp.concatenate(split3(hzr[...].reshape(halo, LANES)), axis=1)
     dz_ref = dz.get()
     for row in range(0, nodes, CHUNK):
         onehot = (iota((CHUNK, halo), 0) + row == sendrow).astype(BF16)
-        value = dz_ref[pl.ds(row, CHUNK), :]
-        for piece in reversed(pieces):
-            value = value + dot(onehot, piece)
-        dz2_ref[pl.ds(row, CHUNK), :] = value.astype(BF16)
+        value = dot(onehot, pieces)
+        value = value[:, 2 * LANES:] + value[:, LANES:2 * LANES] + value[:, :LANES]
+        dz2_ref[pl.ds(row, CHUNK), :] = (dz_ref[pl.ds(row, CHUNK), :] + value).astype(BF16)
     for copy in back:
         copy.wait()
     for q in range(groups):

time: 99.7 us -> 99.1 us (level)
  no operation moved by 1% of the time
where the time goes in v8:
time: 99.1 us; the launch traced here: 98.9 us
  Pallas kernels  98.1 us (99%)
    pallas_call x6, Pallas kernels, call(): pl.pallas_call(body, name=name, out_shape=out_shape, in_specs=[HBM] * n_i...  98.1 us

profile of v8, /device:TPU:0, one launch (start us, length us, event | category | flops | bytes accessed | tf_op | source)
XLA Modules:
  0.0 98.9 jit_solution(13790612725151058843)
XLA Ops:
  0.6 11.5 %gather_rows.1 = (bf16[512,128]{1,0:T(8,128)(2,1)}, f32[64,128]{1,0:T(8,128)}, f32[64,128]{1,0:T(8,128)}, s32[8,128]{1,0:T(8,128)}, f32[8,128]{1,0:T(8,128)}, /*...) custom-call(s32[64]{0:T(128)} %refs_7_.3, ...), custom_call_target="tpu_custom_call" | custom-call | tf_op jit(solution)/shard_map/gather_rows/pallas_call | solution.py:65
  12.1 11.5 %edges_forward.1 = (bf16[2048,512]{1,0:T(8,128)(2,1)}, f32[2048,128]{1,0:T(8,128)}, f32[512,128]{1,0:T(8,128)}, f32[64,640]{1,0:T(8,128)}) custom-call(bf16[50,512]{1,0:T(8,128)(2,1)} %refs_8_.1, bf16[50,2048]{1,0:T(8,128)(2,1)} %bitcast.29, f32[2048,121]{1,0:T(8,128)} %refs_2_.1, bf16[512,128]{1,0:T(8,128)(2,1)} %get-tuple-element.45.refs_3_.refs_8_, ...), custom_call_target="tpu_custom_call" | custom-call | tf_op jit(solution)/shard_map/edges_forward/pallas_call | solution.py:65
  23.6 24.2 %middle.1 = (bf16[2048,128]{1,0:T(8,128)(2,1)}, f32[64,512]{1,0:T(8,128)}, bf16[8,512]{1,0:T(8,128)(2,1)}, bf16[8,128]{1,0:T(8,128)(2,1)}, f32[8192,128]{1,0:T(8,128)}) custom-call(f32[8,8,640]{2,1,0:T(8,128)} %bitcast.35, f32[8,64,128]{2,1,0:T(8,128)} %bitcast.33, f32[2048,128]{1,0:T(8,128)} %get-tuple-element.64.refs_2_, f32[1,512]{1,0:T(1,128)} %bitcast.66, ...), custom_call_target="tpu_custom_call" | custom-call | tf_op jit(solution)/shard_map/middle/pallas_call | solution.py:65
  47.8 12.3 %edges_backward.1 = (f32[2048,512]{1,0:T(8,128)}, f32[4,512,128]{2,1,0:T(8,128)}, f32[64,512]{1,0:T(8,128)}, f32[128,512]{1,0:T(8,128)}, f32[8,128]{1,0:T(8,128)}) custom-call(bf16[512,121]{1,0:T(8,128)(2,1)} %refs_0_.5, bf16[2048,512]{1,0:T(8,128)(2,1)} %get-tuple-element.61.refs_1_, bf16[2048,128]{1,0:T(8,128)(2,1)} %get-tuple-element.65.refs_2_, ...), custom_call_target="tpu_custom_call" | custom-call | tf_op jit(solution)/shard_map/edges_backward/pallas_call | solution.py:65
  60.1 36.6 %last_exchange.1 = (f32[50,2048]{1,0:T(8,128)}, f32[4,8,8,128]{3,2,1,0:T(8,128)}, f32[2,4,16,512]{3,2,1,0:T(8,128)}, f32[8,128]{1,0:T(8,128)}) custom-call(f32[2,4,8,512]{3,2,1,0:T(8,128)} %bitcast.36, f32[4,8,64,128]{3,2,1,0:T(8,128)} %bitcast.31, f32[2,4,16,512]{3,2,1,0:T(8,128)} %bitcast.32, f32[8,128]{1,0:T(8,128)} %get-tuple-element.74.refs_3_, ...), custom_call_target="tpu_custom_call" | custom-call | tf_op jit(solution)/shard_map/last_exchange/pallas_call | solution.py:65
  96.7 2.0 %outputs.1 = (f32[50,2048]{1,0:T(8,128)}, f32[50,512]{1,0:T(8,128)}, f32[512,121]{1,0:T(8,128)}, f32[1,512]{1,0:T(1,128)}, f32[1,121]{1,0:T(1,128)}) custom-call(f32[50,2048]{1,0:T(8,128)} %get-tuple-element.76.refs_0_, f32[128,512]{1,0:T(8,128)} %bitcast.34, f32[8,128]{1,0:T(8,128)} %get-tuple-element.78.refs_2_, f32[4,8,8,128]{3,2,1,0:T(8,128)} %get-tuple-element.79.refs_3_), custom_call_target="tpu_custom_call" | custom-call | tf_op jit(solution)/shard_map/outputs/pallas_call | solution.py:65

commit v9 on v8

--- a/solution.py
+++ b/solution.py
@@ -16,6 +16,7 @@
 TILES = HID // LANES
 CHUNK = 256
 TALL = 2048
+MIDDLE = 1024
 VMEM_LIMIT = 67043328
 HBM = pl.BlockSpec(memory_space=pltpu.HBM)
 
@@ -392,11 +393,11 @@
         copy.wait()
     pieces = jnp.concatenate(split3(hzr[...].reshape(halo, LANES)), axis=1)
     dz_ref = dz.get()
-    for row in range(0, nodes, CHUNK):
-        onehot = (iota((CHUNK, halo), 0) + row == sendrow).astype(BF16)
+    for row in range(0, nodes, MIDDLE):
+        onehot = (iota((MIDDLE, halo), 0) + row == sendrow).astype(BF16)
         value = dot(onehot, pieces)
         value = value[:, 2 * LANES:] + value[:, LANES:2 * LANES] + value[:, :LANES]
-        dz2_ref[pl.ds(row, CHUNK), :] = (dz_ref[pl.ds(row, CHUNK), :] + value).astype(BF16)
+        dz2_ref[pl.ds(row, MIDDLE), :] = (dz_ref[pl.ds(row, MIDDLE), :] + value).astype(BF16)
     for copy in back:
         copy.wait()
     for q in range(groups):

time: 99.1 us -> 99.4 us (level)
  no operation moved by 1% of the time
where the time goes in v9:
time: 99.4 us; the launch traced here: 99.2 us
  Pallas kernels  98.4 us (99%)
    pallas_call x6, Pallas kernels, call(): pl.pallas_call(body, name=name, out_shape=out_shape, in_specs=[HBM] * n_i...  98.4 us

profile of v9, /device:TPU:0, one launch (start us, length us, event | category | flops | bytes accessed | tf_op | source)
XLA Modules:
  0.0 99.2 jit_solution(7413339808904185066)
XLA Ops:
  0.6 11.5 %gather_rows.1 = (bf16[512,128]{1,0:T(8,128)(2,1)}, f32[64,128]{1,0:T(8,128)}, f32[64,128]{1,0:T(8,128)}, s32[8,128]{1,0:T(8,128)}, f32[8,128]{1,0:T(8,128)}, /*...) custom-call(s32[64]{0:T(128)} %refs_7_.3, ...), custom_call_target="tpu_custom_call" | custom-call | tf_op jit(solution)/shard_map/gather_rows/pallas_call | solution.py:66
  12.1 15.9 %edges_forward.1 = (bf16[2048,512]{1,0:T(8,128)(2,1)}, f32[2048,128]{1,0:T(8,128)}, f32[512,128]{1,0:T(8,128)}, f32[64,640]{1,0:T(8,128)}) custom-call(bf16[50,512]{1,0:T(8,128)(2,1)} %refs_8_.1, bf16[50,2048]{1,0:T(8,128)(2,1)} %bitcast.29, f32[2048,121]{1,0:T(8,128)} %refs_2_.1, bf16[512,128]{1,0:T(8,128)(2,1)} %get-tuple-element.45.refs_3_.refs_8_, ...), custom_call_target="tpu_custom_call" | custom-call | tf_op jit(solution)/shard_map/edges_forward/pallas_call | solution.py:66
  28.0 19.9 %middle.1 = (bf16[2048,128]{1,0:T(8,128)(2,1)}, f32[64,512]{1,0:T(8,128)}, bf16[8,512]{1,0:T(8,128)(2,1)}, bf16[8,128]{1,0:T(8,128)(2,1)}, f32[8192,128]{1,0:T(8,128)}) custom-call(f32[8,8,640]{2,1,0:T(8,128)} %bitcast.35, f32[8,64,128]{2,1,0:T(8,128)} %bitcast.33, f32[2048,128]{1,0:T(8,128)} %get-tuple-element.64.refs_2_, f32[1,512]{1,0:T(1,128)} %bitcast.66, ...), custom_call_target="tpu_custom_call" | custom-call | tf_op jit(solution)/shard_map/middle/pallas_call | solution.py:66
  48.0 14.8 %edges_backward.1 = (f32[2048,512]{1,0:T(8,128)}, f32[4,512,128]{2,1,0:T(8,128)}, f32[64,512]{1,0:T(8,128)}, f32[128,512]{1,0:T(8,128)}, f32[8,128]{1,0:T(8,128)}) custom-call(bf16[512,121]{1,0:T(8,128)(2,1)} %refs_0_.5, bf16[2048,512]{1,0:T(8,128)(2,1)} %get-tuple-element.61.refs_1_, bf16[2048,128]{1,0:T(8,128)(2,1)} %get-tuple-element.65.refs_2_, ...), custom_call_target="tpu_custom_call" | custom-call | tf_op jit(solution)/shard_map/edges_backward/pallas_call | solution.py:66
  62.8 34.2 %last_exchange.1 = (f32[50,2048]{1,0:T(8,128)}, f32[4,8,8,128]{3,2,1,0:T(8,128)}, f32[2,4,16,512]{3,2,1,0:T(8,128)}, f32[8,128]{1,0:T(8,128)}) custom-call(f32[2,4,8,512]{3,2,1,0:T(8,128)} %bitcast.36, f32[4,8,64,128]{3,2,1,0:T(8,128)} %bitcast.31, f32[2,4,16,512]{3,2,1,0:T(8,128)} %bitcast.32, f32[8,128]{1,0:T(8,128)} %get-tuple-element.74.refs_3_, ...), custom_call_target="tpu_custom_call" | custom-call | tf_op jit(solution)/shard_map/last_exchange/pallas_call | solution.py:66
  97.0 2.0 %outputs.1 = (f32[50,2048]{1,0:T(8,128)}, f32[50,512]{1,0:T(8,128)}, f32[512,121]{1,0:T(8,128)}, f32[1,512]{1,0:T(1,128)}, f32[1,121]{1,0:T(1,128)}) custom-call(f32[50,2048]{1,0:T(8,128)} %get-tuple-element.76.refs_0_, f32[128,512]{1,0:T(8,128)} %bitcast.34, f32[8,128]{1,0:T(8,128)} %get-tuple-element.78.refs_2_, f32[4,8,8,128]{3,2,1,0:T(8,128)} %get-tuple-element.79.refs_3_), custom_call_target="tpu_custom_call" | custom-call | tf_op jit(solution)/shard_map/outputs/pallas_call | solution.py:66
